TPU v7x, 32 devices: a whole 2x2x4 slice. The times are simulated.
32 devices in a mesh: block: 4 (over y, core), patch: 8 (over z, x).
Axes of the slice: x: 2, y: 2, z: 4, core: 2. Of those that a mesh axis runs over, the one named last changes fastest.
Arguments:
- samples_in: bfloat16 [8, 16, 512, 128], P('block', None, 'patch'), may hold values from -6 to 6
- block_order: int32 [8, 8], P('patch'), may hold values from 0 to 7, each once within a row
- seam_link: int32 [8], P('patch'), may hold values from 0 to 1, as said below
- w_in: bfloat16 [8, 32, 256], P('block'), may hold values from -1.5 to 1.5
- w_mid: bfloat16 [8, 2, 256, 256], P('block'), may hold values from -0.5 to 0.5
- w_feat: bfloat16 [8, 256, 64], P('block'), may hold values from -0.375 to 0.375
- w_density: bfloat16 [8, 256], P('block'), may hold values from -0.375 to 0.375
- w_conv: bfloat16 [4, 3, 3, 64, 64], replicated, may hold values from -0.375 to 0.375
- w_color: bfloat16 [3, 64], replicated, may hold values from -0.75 to 0.75
Outputs:
- pixels: float32 [3, 64, 2048], P(None, 'block', 'patch')
Inputs may be any that keep to these rules, and one draw needn't show every extreme that they name: Each row of block_order names every one of the 8 blocks once, in the order in which that patch's rays pass them, nearest first. seam_link[p] is 1 where patch p + 1 continues patch p to the right in one image; the entry before last is always 1; the last entry is not read.
All inputs are finite; a program needn't handle non-finite values.
Results may differ from a plain program's by a relative error of at most 0.015.
Values may be sent and summed in bfloat16 or wider, within the bound.
No kernel may reach another device: no remote copies, remote signals or barrier semaphores. Data moves between devices by JAX's collectives and lax.ppermute only.
A program may use at most 64 MiB of HBM per device.

v0:
```python
import jax
import jax.numpy as jnp
from jax import lax
from jax.sharding import PartitionSpec as P

ENC = 32
SAMP = 4


step_length = 0.03
highest = lax.Precision.HIGHEST


def shifted(block, axis, distance):
    devices = range(lax.axis_size(axis))
    route = [(i - distance, i) for i in devices if i - distance in devices]
    return lax.ppermute(block, axis, route)


def padded_2(block, sides, width):
    for axis, dim in sides:
        count = lax.axis_size(axis)
        forward = [(i, i + 1) for i in range(count - 1)]
        backward = [(target, source) for source, target in forward]
        low = lax.ppermute(
            lax.slice_in_dim(block, block.shape[dim] - width, None, axis=dim), axis, forward
        )
        high = lax.ppermute(lax.slice_in_dim(block, 0, width, axis=dim), axis, backward)
        block = jnp.concatenate([low, block, high], axis=dim)
    return block


def block_field(samples, w_first, w_hidden, w_head, w_dens):
    count = samples.shape[0]
    flat = samples.reshape(count * SAMP, ENC)
    hidden = jax.nn.relu(jnp.dot(flat, w_first, preferred_element_type=jnp.float32)).astype(
        jnp.bfloat16
    )
    hidden = jax.nn.relu(jnp.dot(hidden, w_hidden[0], preferred_element_type=jnp.float32)).astype(
        jnp.bfloat16
    )
    hidden = jax.nn.relu(jnp.dot(hidden, w_hidden[1], preferred_element_type=jnp.float32)).astype(
        jnp.bfloat16
    )
    feature = lax.dot_general(
        w_head, hidden, (((0,), (1,)), ((), ())), preferred_element_type=jnp.float32
    )
    density = jax.nn.softplus(jnp.dot(hidden, w_dens, preferred_element_type=jnp.float32))
    optical = step_length * density.reshape(count, SAMP)
    earlier = jnp.cumsum(optical, axis=1) - optical
    weights = jnp.exp(-earlier) * -jnp.expm1(-optical)
    colour = jnp.sum(feature.reshape(feature.shape[0], count, SAMP) * weights[None], axis=2)
    return (jnp.sum(optical, axis=1), colour)


def ranks_of(order_row):
    blocks = order_row.shape[0]
    places = jnp.arange(blocks, dtype=jnp.int32)
    hits = (order_row[None, :] == places[:, None]).astype(jnp.int32)
    return jnp.sum(places[None, :] * hits, axis=1)


def enlarge(image):
    return jnp.repeat(jnp.repeat(image, 2, axis=1), 2, axis=2)


def conv_valid(padded, kernel):
    rows = padded.shape[1] - 2
    width = padded.shape[2] - 2
    result = jnp.zeros((kernel.shape[2], rows, width), jnp.float32)
    for down in range(3):
        for across in range(3):
            window = padded[:, down : down + rows, across : across + width]
            result = result + lax.dot_general(
                kernel[down, across],
                window,
                (((1,), (0,)), ((), ())),
                preferred_element_type=jnp.float32,
            )
    return result


def open_columns(padded, rim, left_open, right_open):
    width = padded.shape[2]
    column = jnp.arange(width, dtype=jnp.int32)
    scale = jnp.where(
        column < rim,
        left_open,
        jnp.where(column >= width - rim, right_open, jnp.ones_like(left_open)),
    )
    return padded * scale[None, None, :]


def open_rows(padded, rim, top_open, bottom_open):
    height = padded.shape[1]
    row_ids = jnp.arange(height, dtype=jnp.int32)
    scale = jnp.where(
        row_ids < rim,
        top_open,
        jnp.where(row_ids >= height - rim, bottom_open, jnp.ones_like(top_open)),
    )
    return padded * scale[None, :, None]


def body(samples_in, block_order, seam_link, w_in, w_mid, w_feat, w_density, w_conv, w_color):
    blk_dev = samples_in.shape[0]
    groups = lax.axis_size("block")
    rows_all = samples_in.shape[1]
    cols_here = samples_in.shape[2]
    ray_count = rows_all * cols_here
    rays = samples_in.reshape(blk_dev, ray_count, samples_in.shape[3])
    depth_list = []
    colour_list = []
    for member in range(blk_dev):
        depth_sum, colour = block_field(
            rays[member], w_in[member], w_mid[member], w_feat[member], w_density[member]
        )
        depth_list.append(depth_sum)
        colour_list.append(colour)
    depth_own = jnp.stack(depth_list)
    colour_own = jnp.stack(colour_list)
    rank = ranks_of(block_order[0])
    position = lax.axis_index("block")
    depth_all = lax.all_gather(depth_own, "block", axis=0, tiled=True)
    rank_own = lax.dynamic_slice_in_dim(rank, position * blk_dev, blk_dev)
    earlier = (rank[:, None] < rank_own[None, :]).astype(jnp.float32)
    prefix = jnp.dot(earlier.T, depth_all, precision=highest)
    partial_sum = jnp.sum(jnp.exp(-prefix)[:, None, :] * colour_own, axis=0)
    mixed = lax.psum_scatter(partial_sum, "block", scatter_dimension=1, tiled=True)
    rows_dev = ray_count // groups // cols_here
    composite = mixed.astype(jnp.bfloat16).reshape(mixed.shape[0], rows_dev, cols_here)
    patch_count = lax.axis_size("patch")
    patch_place = lax.axis_index("patch")
    left_open = shifted(seam_link, "patch", 1).astype(jnp.bfloat16)[0]
    right_open = (seam_link[0] * (patch_place < patch_count - 1).astype(jnp.int32)).astype(
        jnp.bfloat16
    )
    top_open = (position > 0).astype(jnp.bfloat16)
    bottom_open = (position < groups - 1).astype(jnp.bfloat16)

    def rim_pair(image, first_kernel, second_kernel):
        padded = padded_2(image, (("block", 1), ("patch", 2)), 1)
        padded = open_columns(padded, 1, left_open, right_open)
        middle = jax.nn.relu(conv_valid(enlarge(padded), first_kernel)).astype(jnp.bfloat16)
        middle = open_rows(open_columns(middle, 1, left_open, right_open), 1, top_open, bottom_open)
        return conv_valid(middle, second_kernel)

    decoded = jax.nn.relu(rim_pair(composite, w_conv[0], w_conv[1])).astype(jnp.bfloat16)
    final = rim_pair(decoded, w_conv[2], w_conv[3])
    return lax.dot_general(
        w_color.astype(jnp.float32), final, (((1,), (0,)), ((), ())), precision=highest
    )


def solution(mesh):
    return jax.shard_map(
        body,
        mesh=mesh,
        in_specs=(
            P("block", None, "patch", None),
            P("patch", None),
            P("patch"),
            P("block", None, None),
            P("block", None, None, None),
            P("block", None, None),
            P("block", None),
            P(),
            P(),
        ),
        out_specs=P(None, "block", "patch"),
        check_vma=False,
    )
```

profile of v0, /device:TPU:17, one launch (start us, length us, event | category | flops | bytes accessed | tf_op | source)
XLA Modules:
  0.0 135.6 jit_solution(282968862544781590)
XLA Ops:
  6.5 1.1 fusion.105
  8.1 2.2 %fusion.2 = bf16[4096,256]{1,0:T(8,128)(2,1)S(1)} fusion(bf16[4096,32]{1,0:T(8,128)(2,1)S(1)} %reshape_squeeze.6, bf16[2,2,256,256]{3,2,1,0:T(8,128)(2,1)} %param.13, bf16[2,32,256]{2,1,0:T(8,128)(2,1)S(1)} %copy-done.7), kind=kOutput, calls=%fused_computation.8 | convolution fusion | flops 608174080 | bytes 3293184 | tf_op jit(solution)/shard_map/dot_general | solution.py:39
  10.3 1.6 %fusion.3 = bf16[4096,256]{1,0:T(8,128)(2,1)S(1)} fusion(bf16[4096,256]{1,0:T(8,128)(2,1)S(1)} %fusion.2, bf16[2,2,256,256]{3,2,1,0:T(8,128)(2,1)} %param.13), kind=kOutput, calls=%fused_computation.9 | convolution fusion | flops 538968064 | bytes 4325376 | tf_op jit(solution)/shard_map/dot_general | solution.py:42
  12.8 1.7 %convolution_bitcast_fusion.1 = f32[64,4096]{1,0:T(8,128)} fusion(bf16[4096,256]{1,0:T(8,128)(2,1)S(1)} %fusion.3, bf16[2,256,64]{1,2,0:T(8,128)(2,1)S(1)} %copy-done.5), kind=kOutput, calls=%fused_computation.13 | convolution fusion | flops 134217728 | bytes 3178496 | tf_op jit(solution)/shard_map/dot_general | solution.py:45
  14.9 2.2 %fusion.4 = bf16[4096,256]{1,0:T(8,128)(2,1)S(1)} fusion(bf16[4096,32]{1,0:T(8,128)(2,1)S(1)} %reshape_squeeze.7, bf16[2,2,256,256]{3,2,1,0:T(8,128)(2,1)} %param.13, bf16[2,32,256]{2,1,0:T(8,128)(2,1)S(1)} %copy-done.7), kind=kOutput, calls=%fused_computation.10 | convolution fusion | flops 608174080 | bytes 3293184 | tf_op jit(solution)/shard_map/dot_general | solution.py:39
  17.2 1.6 %fusion.5 = bf16[4096,256]{1,0:T(8,128)(2,1)S(1)} fusion(bf16[4096,256]{1,0:T(8,128)(2,1)S(1)} %fusion.4, bf16[2,2,256,256]{3,2,1,0:T(8,128)(2,1)} %param.13), kind=kOutput, calls=%fused_computation.11 | convolution fusion | flops 538968064 | bytes 4325376 | tf_op jit(solution)/shard_map/dot_general | solution.py:42
  19.4 1.8 %convolution_bitcast_fusion = f32[64,4096]{1,0:T(8,128)} fusion(bf16[4096,256]{1,0:T(8,128)(2,1)S(1)} %fusion.5, bf16[2,256,64]{1,2,0:T(8,128)(2,1)S(1)} %copy-done.5), kind=kOutput, calls=%fused_computation.12 | convolution fusion | flops 134217728 | bytes 3178496 | tf_op jit(solution)/shard_map/dot_general | solution.py:45
  21.9 1.8 %copy.105 = f32[64,4096]{0,1:T(8,128)S(1)} copy(f32[64,4096]{1,0:T(8,128)} %convolution_bitcast_fusion.1) | data formatting | bytes 2097152 | tf_op jit(solution)/shard_map/dot_general | solution.py:45
  24.3 1.2 reduce_window_sum.17
  25.4 1.1 reduce_window_sum.18
  26.6 2.6 %fusion.103 = (f32[1024]{0:T(1024)S(1)}, f32[1024,4]{1,0:T(8,128)}, f32[1024,4]{1,0:T(8,128)}, f32[1024]{0:T(1024)S(1)}) fusion(f32[1024,4]{1,0:T(8,128)S(1)} %mul.130, f32[1024,4]{1,0:T(8,128)} %reduce_window_sum.17, f32[1024,4]{1,0:T(8,128)S(1)} %mul.132, f32[1024,4]{1,0:T(8,128)} %reduce_window_sum.18), kind=kLoop, calls=%fused_computation.198 | loop fusion | flops 47104 | bytes 106496 | tf_op jit(solution)/shard_map/reduce_sum | solution.py:53
  29.1 6.0 %all-gather = f32[4,2,1024]{2,1,0:T(2,128)S(1)} all-gather(f32[1,2,1024]{2,1,0:T(2,128)S(1)} %maximum_bitcast_fusion), channel_id=1, replica_groups=mesh['block'=4,'patch'=8] {'block'}, dimensions={0}, use_global_device_ids=true | all-gather | bytes 40960 | tf_op jit(solution)/shard_map/all_gather | solution.py:124
  35.2 3.2 %copy.106 = f32[64,4096]{0,1:T(8,128)} copy(f32[64,4096]{1,0:T(8,128)} %convolution_bitcast_fusion) | data formatting | bytes 2097152 | tf_op jit(solution)/shard_map/dot_general | solution.py:45
  38.4 5.6 %multiply_reduce_fusion.1 = f32[64,1024]{0,1:T(8,128)S(1)} fusion(f32[64,1024,4]{0,2,1:T(4,128)S(1)} %bitcast.275, f32[1024,4]{1,0:T(8,128)S(1)} %copy-done.3), kind=kLoop, calls=%fused_computation.15 | loop fusion | flops 458752 | bytes 1327104 | tf_op jit(solution)/shard_map/reduce_sum | solution.py:52
  44.3 5.6 %multiply_reduce_fusion = f32[64,1024]{0,1:T(8,128)S(1)} fusion(f32[64,1024,4]{0,2,1:T(4,128)S(1)} %bitcast.276, f32[1024,4]{1,0:T(8,128)S(1)} %copy-done.2), kind=kLoop, calls=%fused_computation.14 | loop fusion | flops 458752 | bytes 1327104 | tf_op jit(solution)/shard_map/reduce_sum | solution.py:52
  51.2 3.1 %collective-permute-start.4 = (s32[1]{0:T(128)}, s32[1]{0:T(128)}, u32[]{:S(2)}, u32[]{:S(2)}) collective-permute-start(s32[1]{0:T(128)} %param.11), channel_id=1, source_target_pairs={{0,1},{1,2},{2,3},{3,4},{4,5},{5,6},{6,7},{8,9},{9,10},{10,11},{11... | collective-permute-start | bytes 20 | tf_op jit(solution)/shard_map/ppermute | solution.py:17
  55.1 1.4 %collective-permute-done.4 = s32[1]{0:T(128)} collective-permute-done((s32[1]{0:T(128)}, s32[1]{0:T(128)}, u32[]{:S(2)}, u32[]{:S(2)}) %collective-permute-start.4) | collective-permute-done | bytes 36 | tf_op jit(solution)/shard_map/ppermute | solution.py:17
  57.1 14.6 %reduce-scatter.2.cloned.1.call-done = f32[64,256]{1,0:T(8,128)} async-done(((f32[64,1024]{1,0:T(8,128)}), f32[64,256]{1,0:T(8,128)}) %reduce-scatter.2.cloned.1.call-update) | async-done | bytes 65552 | tf_op jit(solution)/shard_map/reduce_scatter | solution.py:129
  72.8 3.0 %collective-permute-start = (bf16[64,1,64]{2,0,1:T(8,128)(2,1)S(1)}, bf16[64,1,64]{2,0,1:T(8,128)(2,1)S(1)}, u32[]{:S(2)}, u32[]{:S(2)}) collective-permute-start(bf16[64,1,64]{2,0,1:T(8,128)(2,1)S(1)} %copy.151), channel_id=1, source_target_pairs={{0,8},{8,16},{16,24},{1,9},{9,17},{17,25},{2,10},{10,18},{18,26},{... | collective-permute-start | bytes 24584 | tf_op jit(solution)/shard_map/ppermute | solution.py:25
  75.8 1.9 %collective-permute-start.1 = (bf16[64,1,64]{2,0,1:T(8,128)(2,1)S(1)}, bf16[64,1,64]{2,0,1:T(8,128)(2,1)S(1)}, u32[]{:S(2)}, u32[]{:S(2)}) collective-permute-start(bf16[64,1,64]{2,0,1:T(8,128)(2,1)S(1)} %copy.152), channel_id=1, source_target_pairs={{8,0},{16,8},{24,16},{9,1},{17,9},{25,17},{10,2},{18,10},{26,18},{... | collective-permute-start | bytes 24584 | tf_op jit(solution)/shard_map/ppermute | solution.py:28
  77.8 3.1 %collective-permute-done.1 = bf16[64,1,64]{2,0,1:T(8,128)(2,1)S(1)} collective-permute-done((bf16[64,1,64]{2,0,1:T(8,128)(2,1)S(1)}, bf16[64,1,64]{2,0,1:T(8,128)(2,1)S(1)}, u32[]{:S(2)}, u32[]{:S(2)}) %collective-permute-start.1) | collective-permute-done | bytes 8224 | tf_op jit(solution)/shard_map/ppermute | solution.py:28
  81.0 3.1 %collective-permute-start.2 = (bf16[64,6,1]{2,0,1:T(8,128)(2,1)S(1)}, bf16[64,6,1]{2,0,1:T(8,128)(2,1)S(1)}, u32[]{:S(2)}, u32[]{:S(2)}) collective-permute-start(bf16[64,6,1]{2,0,1:T(8,128)(2,1)S(1)} %get-tuple-element.19), channel_id=1, source_target_pairs={{0,1},{1,2},{2,3},{3,4},{4,5},{5,6},{6,7},{8,9},{9,10},{10,11},{11... | collective-permute-start | bytes 2312 | tf_op jit(solution)/shard_map/ppermute | solution.py:25
  84.1 3.1 %collective-permute-start.3 = (bf16[64,6,1]{2,0,1:T(8,128)(2,1)S(1)}, bf16[64,6,1]{2,0,1:T(8,128)(2,1)S(1)}, u32[]{:S(2)}, u32[]{:S(2)}) collective-permute-start(bf16[64,6,1]{2,0,1:T(8,128)(2,1)S(1)} %get-tuple-element.20), channel_id=1, source_target_pairs={{1,0},{2,1},{3,2},{4,3},{5,4},{6,5},{7,6},{9,8},{10,9},{11,10},{12... | collective-permute-start | bytes 2312 | tf_op jit(solution)/shard_map/ppermute | solution.py:28
  87.2 2.2 %collective-permute-done.3 = bf16[64,6,1]{2,0,1:T(8,128)(2,1)S(1)} collective-permute-done((bf16[64,6,1]{2,0,1:T(8,128)(2,1)S(1)}, bf16[64,6,1]{2,0,1:T(8,128)(2,1)S(1)}, u32[]{:S(2)}, u32[]{:S(2)}) %collective-permute-start.3) | collective-permute-done | bytes 800 | tf_op jit(solution)/shard_map/ppermute | solution.py:28
  95.4 3.4 %collective-permute-start.5 = (bf16[64,1,128]{2,0,1:T(8,128)(2,1)S(1)}, bf16[64,1,128]{2,0,1:T(8,128)(2,1)S(1)}, u32[]{:S(2)}, u32[]{:S(2)}) collective-permute-start(bf16[64,1,128]{2,0,1:T(8,128)(2,1)S(1)} %get-tuple-element.17), channel_id=1, source_target_pairs={{0,8},{8,16},{16,24},{1,9},{9,17},{17,25},{2,10},{10,18},{18,26},{... | collective-permute-start | bytes 49160 | tf_op jit(solution)/shard_map/ppermute | solution.py:25
  98.8 1.9 %collective-permute-start.6 = (bf16[64,1,128]{2,0,1:T(8,128)(2,1)S(1)}, bf16[64,1,128]{2,0,1:T(8,128)(2,1)S(1)}, u32[]{:S(2)}, u32[]{:S(2)}) collective-permute-start(bf16[64,1,128]{2,0,1:T(8,128)(2,1)S(1)} %get-tuple-element.18), channel_id=1, source_target_pairs={{8,0},{16,8},{24,16},{9,1},{17,9},{25,17},{10,2},{18,10},{26,18},{... | collective-permute-start | bytes 49160 | tf_op jit(solution)/shard_map/ppermute | solution.py:28
  100.8 3.1 %collective-permute-done.6 = bf16[64,1,128]{2,0,1:T(8,128)(2,1)S(1)} collective-permute-done((bf16[64,1,128]{2,0,1:T(8,128)(2,1)S(1)}, bf16[64,1,128]{2,0,1:T(8,128)(2,1)S(1)}, u32[]{:S(2)}, u32[]{:S(2)}) %collective-permute-start.6) | collective-permute-done | bytes 16416 | tf_op jit(solution)/shard_map/ppermute | solution.py:28
  104.0 4.0 %collective-permute-start.7 = (bf16[64,10,1]{2,0,1:T(8,128)(2,1)S(1)}, bf16[64,10,1]{2,0,1:T(8,128)(2,1)S(1)}, u32[]{:S(2)}, u32[]{:S(2)}) collective-permute-start(bf16[64,10,1]{2,0,1:T(8,128)(2,1)S(1)} %get-tuple-element.15), channel_id=1, source_target_pairs={{0,1},{1,2},{2,3},{3,4},{4,5},{5,6},{6,7},{8,9},{9,10},{10,11},{11... | collective-permute-start | bytes 3848 | tf_op jit(solution)/shard_map/ppermute | solution.py:25
  108.0 2.4 %collective-permute-start.8 = (bf16[64,10,1]{2,0,1:T(8,128)(2,1)S(1)}, bf16[64,10,1]{2,0,1:T(8,128)(2,1)S(1)}, u32[]{:S(2)}, u32[]{:S(2)}) collective-permute-start(bf16[64,10,1]{2,0,1:T(8,128)(2,1)S(1)} %get-tuple-element.16), channel_id=1, source_target_pairs={{1,0},{2,1},{3,2},{4,3},{5,4},{6,5},{7,6},{9,8},{10,9},{11,10},{12... | collective-permute-start | bytes 3848 | tf_op jit(solution)/shard_map/ppermute | solution.py:28
  111.2 3.5 %collective-permute-done.8 = bf16[64,10,1]{2,0,1:T(8,128)(2,1)S(1)} collective-permute-done((bf16[64,10,1]{2,0,1:T(8,128)(2,1)S(1)}, bf16[64,10,1]{2,0,1:T(8,128)(2,1)S(1)}, u32[]{:S(2)}, u32[]{:S(2)}) %collective-permute-start.8) | collective-permute-done | bytes 1312 | tf_op jit(solution)/shard_map/ppermute | solution.py:28
  117.3 0.9 fusion.14
  123.3 1.2 multiply_bitcast_fusion
  (103 shorter events, 25.0 us)
Async XLA Ops:
  6.5 121.1 %copy-start = (bf16[3,64]{1,0:T(4,128)(2,1)S(1)}, bf16[3,64]{1,0:T(4,128)(2,1)}, u32[]{:S(2)}) copy-start(bf16[3,64]{1,0:T(4,128)(2,1)} %param.17) | copy-start | bytes 1156
  6.5 1.5 %copy-start.7 = (bf16[2,32,256]{2,1,0:T(8,128)(2,1)S(1)}, bf16[2,32,256]{2,1,0:T(8,128)(2,1)}, u32[]{:S(2)}) copy-start(bf16[2,32,256]{2,1,0:T(8,128)(2,1)} %param.12) | copy-start | bytes 98308
  6.5 65.2 %reduce-scatter.2.cloned.1.call-start = ((), (), s32[]{:S(2)}) async-start(), calls=%async_computation.1 | async-start | bytes 327680 | tf_op jit(solution)/shard_map/reduce_scatter | solution.py:129
  10.3 1.6 %copy-start.6 = (bf16[2,256]{1,0:T(2,128)(2,1)S(1)}, bf16[2,256]{1,0:T(2,128)(2,1)}, u32[]{:S(2)}) copy-start(bf16[2,256]{1,0:T(2,128)(2,1)} %param.15) | copy-start | bytes 3076
  11.9 0.8 copy-start.5
  19.4 1.8 %copy-start.8 = (s32[1,8]{1,0:T(1,128)S(1)}, s32[1,8]{1,0:T(1,128)}, u32[]{:S(2)}) copy-start(s32[1,8]{1,0:T(1,128)} %param.10) | copy-start | bytes 100
  29.1 9.3 %copy-start.3 = (f32[1024,4]{1,0:T(8,128)S(1)}, f32[1024,4]{1,0:T(8,128)}, u32[]{:S(2)}) copy-start(f32[1024,4]{1,0:T(8,128)} %get-tuple-element.10) | copy-start | bytes 49156
  38.3 6.0 %copy-start.2 = (f32[1024,4]{1,0:T(8,128)S(1)}, f32[1024,4]{1,0:T(8,128)}, u32[]{:S(2)}) copy-start(f32[1024,4]{1,0:T(8,128)} %get-tuple-element.23) | copy-start | bytes 49156
  38.3 6.0 %copy-start.1 = (f32[64,4096]{0,1:T(8,128)S(1)}, f32[64,4096]{0,1:T(8,128)}, u32[]{:S(2)}) copy-start(f32[64,4096]{0,1:T(8,128)} %copy.106) | copy-start | bytes 3145732
  49.9 5.1 %copy-start.4 = (bf16[4,3,3,64,64]{4,3,2,1,0:T(8,128)(2,1)S(1)}, bf16[4,3,3,64,64]{4,3,2,1,0:T(8,128)(2,1)}, u32[]{:S(2)}) copy-start(bf16[4,3,3,64,64]{4,3,2,1,0:T(8,128)(2,1)} %param.16) | copy-start | bytes 884740
  51.2 5.3 %collective-permute-start.4 = (s32[1]{0:T(128)}, s32[1]{0:T(128)}, u32[]{:S(2)}, u32[]{:S(2)}) collective-permute-start(s32[1]{0:T(128)} %param.11), channel_id=1, source_target_pairs={{0,1},{1,2},{2,3},{3,4},{4,5},{5,6},{6,7},{8,9},{9,10},{10,11},{11... | collective-permute-start | bytes 20 | tf_op jit(solution)/shard_map/ppermute | solution.py:17
  72.8 4.9 %collective-permute-start = (bf16[64,1,64]{2,0,1:T(8,128)(2,1)S(1)}, bf16[64,1,64]{2,0,1:T(8,128)(2,1)S(1)}, u32[]{:S(2)}, u32[]{:S(2)}) collective-permute-start(bf16[64,1,64]{2,0,1:T(8,128)(2,1)S(1)} %copy.151), channel_id=1, source_target_pairs={{0,8},{8,16},{16,24},{1,9},{9,17},{17,25},{2,10},{10,18},{18,26},{... | collective-permute-start | bytes 24584 | tf_op jit(solution)/shard_map/ppermute | solution.py:25
  75.8 5.1 %collective-permute-start.1 = (bf16[64,1,64]{2,0,1:T(8,128)(2,1)S(1)}, bf16[64,1,64]{2,0,1:T(8,128)(2,1)S(1)}, u32[]{:S(2)}, u32[]{:S(2)}) collective-permute-start(bf16[64,1,64]{2,0,1:T(8,128)(2,1)S(1)} %copy.152), channel_id=1, source_target_pairs={{8,0},{16,8},{24,16},{9,1},{17,9},{25,17},{10,2},{18,10},{26,18},{... | collective-permute-start | bytes 24584 | tf_op jit(solution)/shard_map/ppermute | solution.py:28
  81.0 6.3 %collective-permute-start.2 = (bf16[64,6,1]{2,0,1:T(8,128)(2,1)S(1)}, bf16[64,6,1]{2,0,1:T(8,128)(2,1)S(1)}, u32[]{:S(2)}, u32[]{:S(2)}) collective-permute-start(bf16[64,6,1]{2,0,1:T(8,128)(2,1)S(1)} %get-tuple-element.19), channel_id=1, source_target_pairs={{0,1},{1,2},{2,3},{3,4},{4,5},{5,6},{6,7},{8,9},{9,10},{10,11},{11... | collective-permute-start | bytes 2312 | tf_op jit(solution)/shard_map/ppermute | solution.py:25
  84.1 5.4 %collective-permute-start.3 = (bf16[64,6,1]{2,0,1:T(8,128)(2,1)S(1)}, bf16[64,6,1]{2,0,1:T(8,128)(2,1)S(1)}, u32[]{:S(2)}, u32[]{:S(2)}) collective-permute-start(bf16[64,6,1]{2,0,1:T(8,128)(2,1)S(1)} %get-tuple-element.20), channel_id=1, source_target_pairs={{1,0},{2,1},{3,2},{4,3},{5,4},{6,5},{7,6},{9,8},{10,9},{11,10},{12... | collective-permute-start | bytes 2312 | tf_op jit(solution)/shard_map/ppermute | solution.py:28
  95.4 5.3 %collective-permute-start.5 = (bf16[64,1,128]{2,0,1:T(8,128)(2,1)S(1)}, bf16[64,1,128]{2,0,1:T(8,128)(2,1)S(1)}, u32[]{:S(2)}, u32[]{:S(2)}) collective-permute-start(bf16[64,1,128]{2,0,1:T(8,128)(2,1)S(1)} %get-tuple-element.17), channel_id=1, source_target_pairs={{0,8},{8,16},{16,24},{1,9},{9,17},{17,25},{2,10},{10,18},{18,26},{... | collective-permute-start | bytes 49160 | tf_op jit(solution)/shard_map/ppermute | solution.py:25
  98.8 5.1 %collective-permute-start.6 = (bf16[64,1,128]{2,0,1:T(8,128)(2,1)S(1)}, bf16[64,1,128]{2,0,1:T(8,128)(2,1)S(1)}, u32[]{:S(2)}, u32[]{:S(2)}) collective-permute-start(bf16[64,1,128]{2,0,1:T(8,128)(2,1)S(1)} %get-tuple-element.18), channel_id=1, source_target_pairs={{8,0},{16,8},{24,16},{9,1},{17,9},{25,17},{10,2},{18,10},{26,18},{... | collective-permute-start | bytes 49160 | tf_op jit(solution)/shard_map/ppermute | solution.py:28
  104.0 7.2 %collective-permute-start.7 = (bf16[64,10,1]{2,0,1:T(8,128)(2,1)S(1)}, bf16[64,10,1]{2,0,1:T(8,128)(2,1)S(1)}, u32[]{:S(2)}, u32[]{:S(2)}) collective-permute-start(bf16[64,10,1]{2,0,1:T(8,128)(2,1)S(1)} %get-tuple-element.15), channel_id=1, source_target_pairs={{0,1},{1,2},{2,3},{3,4},{4,5},{5,6},{6,7},{8,9},{9,10},{10,11},{11... | collective-permute-start | bytes 3848 | tf_op jit(solution)/shard_map/ppermute | solution.py:25
  108.0 6.7 %collective-permute-start.8 = (bf16[64,10,1]{2,0,1:T(8,128)(2,1)S(1)}, bf16[64,10,1]{2,0,1:T(8,128)(2,1)S(1)}, u32[]{:S(2)}, u32[]{:S(2)}) collective-permute-start(bf16[64,10,1]{2,0,1:T(8,128)(2,1)S(1)} %get-tuple-element.16), channel_id=1, source_target_pairs={{1,0},{2,1},{3,2},{4,3},{5,4},{6,5},{7,6},{9,8},{10,9},{11,10},{12... | collective-permute-start | bytes 3848 | tf_op jit(solution)/shard_map/ppermute | solution.py:28
Sparse Core Ops, SparseCore 0:
  51.3 20.3 reduce-scatter.1
where the time goes:
time: 137 us; the launch traced here: 136 us
  matrix products  29.6 us (22%)
  waiting for transfers between devices  28.8 us (21%)
  starting transfers between devices  25.9 us (19%)
  other arithmetic  17.8 us (13%)
  between operations  15.4 us (11%)
  local copies, waits for them, and re-layouts  12.1 us (9%)
  blocking collectives  6 us (4%)
    dot_general x36, matrix products, conv_valid(): lax.dot_general(kernel[down, across], window, (((1,), (0,)), ((), ())), p...  16.4 us
    reduce_scatter x1, waiting for transfers between devices, body(): lax.psum_scatter(partial_sum, 'block', scatter_dimension=1, tiled=True)  14.6 us
    ppermute x4, starting transfers between devices, padded_2(): lax.ppermute(lax.slice_in_dim(block, block.shape[dim] - width, None, axis...  13.4 us
    ppermute x4, waiting for transfers between devices, padded_2(): lax.ppermute(lax.slice_in_dim(block, 0, width, axis=dim), axis, backward)  11.9 us
    reduce_sum x2, other arithmetic, block_field(): jnp.sum(feature.reshape(feature.shape[0], count, SAMP) * weights[None], a...  11.2 us
    ppermute x4, starting transfers between devices, padded_2(): lax.ppermute(lax.slice_in_dim(block, 0, width, axis=dim), axis, backward)  9.34 us
    all_gather x1, blocking collectives, body(): depth_all = lax.all_gather(depth_own, 'block', axis=0, tiled=True)  6 us
    dot_general x2, local copies, waits for them, and re-layouts, block_field(): lax.dot_general(w_head, hidden, (((0,), (1,)), ((), ())), preferred_eleme...  5 us
  transfers between devices with their start and end apart: 10, of which 8 were waited for; matrix products, arithmetic and copies ran while one was open for 0% of the time, Pallas kernels for 0%

commit v1 on v0

v1 whole, which is shorter than its diff:
```python
import functools

import numpy as np

import jax
import jax.numpy as jnp
from jax import lax
from jax.experimental import pallas as pl
from jax.experimental.pallas import tpu as pltpu
from jax.sharding import PartitionSpec as P

STEP = 0.03
LANES = 128
EDGE = 2
LEAD = 8
F32 = jnp.float32
BF16 = jnp.bfloat16


def dot(a, b):
    return jnp.dot(a, b, preferred_element_type=F32)


def dot_t(a, b):
    return lax.dot_general(a, b, (((1,), (1,)), ((), ())), preferred_element_type=F32)


def relu16(x):
    return jnp.maximum(x, 0.0).astype(BF16)


def softplus(v):
    e = jnp.exp(-jnp.abs(v))
    tail = jnp.where(e < 1e-3, e * (1.0 - e * (0.5 - e * (1.0 / 3.0))), jnp.log(1.0 + e))
    return jnp.maximum(v, 0.0) + tail


def fade(optical):
    through = jnp.exp(-optical)
    small = optical * (1.0 - optical * (0.5 - optical * (1.0 / 6.0 - optical * (1.0 / 24.0))))
    return through, jnp.where(optical < 0.0625, small, 1.0 - through)


def field_rays(xs, win, wmid, whead, samples, enc):
    rays = xs[0].shape[0]
    lane = lax.broadcasted_iota(jnp.int32, xs[0].shape, 1)
    total = None
    for b, x in enumerate(xs):
        zero = jnp.zeros_like(x)
        parts = [
            jnp.where((lane >= s * enc) & (lane < (s + 1) * enc), x, zero) for s in range(samples)
        ]
        hidden = relu16(dot(jnp.concatenate(parts, axis=0), win[b]))
        hidden = relu16(dot(hidden, wmid[b, 0]))
        hidden = relu16(dot(hidden, wmid[b, 1]))
        head = dot(hidden, whead[b])
        total = head if total is None else total + head
    left = jnp.ones((rays, LANES), F32)
    colour = jnp.zeros((rays, LANES), F32)
    depth = jnp.zeros((rays, LANES), F32)
    for s in range(samples):
        own = total[s * rays : (s + 1) * rays]
        optical = STEP * softplus(own[:, LANES:])
        through, stop = fade(optical)
        colour = colour + (left * stop) * own[:, :LANES]
        left = left * through
        depth = depth + optical
    return colour, depth


def split16(x):
    high = x.astype(BF16).astype(F32)
    return high, x - high


def depth_rows(depth):
    turned = depth.T
    pair = jnp.concatenate([turned[0:1], turned[LANES // 2 : LANES // 2 + 1]], axis=0)
    high, low = split16(pair)
    return jnp.concatenate([high, low], axis=0)


def field_kernel(cfg, place_ref, own_ref, halo_ref, win_ref, wmid_ref, whead_ref, *rest):
    groups, samples, enc = cfg["groups"], cfg["samples"], cfg["enc"]
    outs = rest[:groups]
    col_own, col_halo, dep_own, dep_halo, tiled = rest[groups:]
    cols, rows_all, rows_dev = cfg["cols"], cfg["rows_all"], cfg["rows_dev"]
    blocks = own_ref.shape[0]
    pad = EDGE * cols
    count = rows_all * cols
    col_own[0:pad, :] = jnp.zeros((pad, LANES), BF16)
    col_own[pad + count :, :] = jnp.zeros((pad, LANES), BF16)
    dep_own[...] = jnp.zeros(dep_own.shape, F32)
    dep_halo[...] = jnp.zeros(dep_halo.shape, F32)
    for b in range(blocks):
        for s in range(samples):
            tiled[b, s * enc : (s + 1) * enc, :] = win_ref[b]
    step = cfg["chunk"]
    for first in range(0, count, step):
        xs = [own_ref[b, first : first + step, :] for b in range(blocks)]
        colour, depth = field_rays(xs, tiled, wmid_ref, whead_ref, samples, enc)
        col_own[pad + first : pad + first + step, :] = colour.astype(BF16)
        for k in range(step // LANES):
            at = 4 * ((pad + first) // LANES + k)
            dep_own[at : at + 4, :] = depth_rows(depth[k * LANES : (k + 1) * LANES])
    xs = [halo_ref[b] for b in range(blocks)]
    colour, depth = field_rays(xs, tiled, wmid_ref, whead_ref, samples, enc)
    col_halo[...] = colour.astype(BF16)
    hrays = depth.shape[0]
    for k in range(cfg["hchunks"]):
        part = depth[k * LANES : min((k + 1) * LANES, hrays)]
        if part.shape[0] < LANES:
            part = jnp.concatenate([part, jnp.zeros((LANES - part.shape[0], LANES), F32)], axis=0)
        dep_halo[4 * k : 4 * k + 4, :] = depth_rows(part)
    n_own, n_halo, n_dep = cfg["n_own"], cfg["n_halo"], cfg["n_dep"]
    place = place_ref[0]
    for s in range(groups):
        dest = cfg["dest"](place, s)
        out = outs[s]
        start = pl.multiple_of(dest * (rows_dev * cols), LANES)
        out[0:n_own, :] = col_own[pl.ds(start, n_own), :]
        start = pl.multiple_of(dest * (rows_dev * 2 * EDGE), 16)
        out[n_own : n_own + n_halo, :] = col_halo[pl.ds(start, n_halo), :]
        start = pl.multiple_of(dest * (4 * rows_dev * cols // LANES), 8)
        at = n_own + n_halo
        out[at : at + n_dep, :] = dep_own[pl.ds(start, n_dep), :].astype(BF16)
        out[at + n_dep :, :] = dep_halo[...].astype(BF16)


def decoder_kernel(cfg, info_ref, w0_ref, w1_ref, w2_ref, w3_ref, *rest):
    groups, nb = cfg["groups"], cfg["nb"]
    bufs = rest[:groups]
    out_ref = rest[groups]
    comp, x0, sa, xa, xc, rep = rest[groups + 1 : groups + 7]
    rank_ref = rest[groups + 7]
    cols, rows_dev, pitch = cfg["cols"], cfg["rows_dev"], cfg["pitch"]
    n_own, n_halo, n_dep = cfg["n_own"], cfg["n_halo"], cfg["n_dep"]
    rows_in = rows_dev + 2 * EDGE
    rows_mid = rows_dev + 2
    mid = rows_mid * pitch
    half = LANES // 2
    per_dev = nb // groups
    place = info_ref[0]
    left_open, right_open = info_ref[1].astype(F32), info_ref[2].astype(F32)
    top_open, bottom_open = info_ref[3].astype(F32), info_ref[4].astype(F32)

    earlier = []
    for side in range(3):
        for k in range(nb):
            rank_ref[info_ref[8 + side * nb + k]] = k
        wide = 2 * per_dev * groups
        row = jnp.zeros((nb, wide), jnp.int32)
        column = jnp.zeros((nb, wide), jnp.int32)
        lane = lax.broadcasted_iota(jnp.int32, (nb, wide), 1)
        sub = lax.broadcasted_iota(jnp.int32, (nb, wide), 0)
        for s in range(groups):
            source = cfg["source"](place, s)
            for i in range(per_dev):
                rank = rank_ref[source * per_dev + i]
                at = s * 2 * per_dev + i
                row = jnp.where((lane == at) | (lane == at + per_dev), rank, row)
                column = jnp.where(sub == s * per_dev + i, rank, column)
        earlier.append(jnp.where(row < column, 1.0, 0.0).astype(BF16))

    at = n_own + n_halo
    own_rows = [bufs[s][at : at + n_dep, :].astype(F32) for s in range(groups)]
    halo_rows = [bufs[s][at + n_dep :, :].astype(F32) for s in range(groups)]
    chunks = n_own // LANES
    factors = []
    for k in range(chunks):
        stack = jnp.concatenate([own_rows[s][4 * k : 4 * k + 4] for s in range(groups)], axis=0)
        factors.append(jnp.exp(-dot(earlier[0], stack.astype(BF16))))
    lane = lax.broadcasted_iota(jnp.int32, (nb, LANES), 1)
    on_left = (lane & (2 * EDGE - 1)) < EDGE
    for k in range(cfg["hchunks"]):
        stack = jnp.concatenate(
            [halo_rows[s][4 * k : 4 * k + 4] for s in range(groups)], axis=0
        ).astype(BF16)
        from_left = jnp.exp(-dot(earlier[1], stack)) * left_open
        from_right = jnp.exp(-dot(earlier[2], stack)) * right_open
        factors.append(jnp.where(on_left, from_left, from_right))
    used = len(factors) * nb
    factors.append(jnp.zeros((LANES - used, LANES), F32))
    turned = jnp.concatenate(factors, axis=0).T
    high, low = split16(turned)
    high, low = high.astype(BF16), low.astype(BF16)

    def spread(k):
        r = lax.broadcasted_iota(jnp.int32, (LANES, groups * LANES), 0)
        c = lax.broadcasted_iota(jnp.int32, (LANES, groups * LANES), 1)
        pick = jnp.where(r - k * nb == c // half, 1.0, 0.0).astype(BF16)
        return dot(high, pick) + dot(low, pick)

    def mix(weights, lo, n):
        acc = None
        for s in range(groups):
            term = weights[:, s * LANES : (s + 1) * LANES] * bufs[s][lo : lo + n, :].astype(F32)
            acc = term if acc is None else acc + term
        return acc + pltpu.roll(acc, half, 1)

    comp[...] = jnp.zeros(comp.shape, F32)
    base = pitch
    per_chunk = LANES // cols
    for k in range(chunks):
        mixed = mix(spread(k), k * LANES, LANES)
        for t in range(per_chunk):
            q = base + (k * per_chunk + t) * pitch + LEAD
            comp[q : q + cols, :] = mixed[t * cols : (t + 1) * cols]
    for k in range(cfg["hchunks"]):
        rep[k * LANES : (k + 1) * LANES, :] = spread(chunks + k)
    start = pl.multiple_of(place * (rows_dev * 2 * EDGE), 16)
    mixed = mix(rep[pl.ds(start, n_halo), :], n_own, n_halo)
    for r in range(rows_in):
        q = base + r * pitch + LEAD
        comp[q - EDGE : q, :] = mixed[r * 2 * EDGE : r * 2 * EDGE + EDGE]
        comp[q + cols : q + cols + EDGE, :] = mixed[r * 2 * EDGE + EDGE : (r + 1) * 2 * EDGE]

    n_in = rows_in * pitch
    lane = lax.broadcasted_iota(jnp.int32, (n_in, LANES), 1)
    here = jnp.where(lane < half, comp[base - 1 : base - 1 + n_in, :], comp[base : base + n_in, :])
    x0[:, 0:LANES] = here.astype(BF16)
    x0[:, LANES : 2 * LANES] = comp[base + 1 : base + 1 + n_in, :].astype(BF16)

    q = lax.broadcasted_iota(jnp.int32, (mid, 2 * LANES), 0)
    pos = q
    for r in range(1, rows_mid):
        pos = pos - jnp.where(q >= r * pitch, pitch, 0)
    mask = jnp.where(pos < LEAD, left_open, jnp.where(pos >= LEAD + cols, right_open, 1.0))
    mask = mask * jnp.where(q < pitch, top_open, jnp.where(q >= mid - pitch, bottom_open, 1.0))

    def windows(ref, pieces):
        return jnp.concatenate(
            [ref[r * pitch : r * pitch + n, a:b] for r, n, a, b in pieces], axis=1
        )

    wide = 2 * LANES
    lhs = windows(x0, [(d, mid, 0, wide) for d in range(3)])
    value = jnp.maximum(dot_t(lhs, w0_ref[...]), 0.0) * mask

    sa[0:8, :] = jnp.zeros((8, wide), F32)
    sa[8 + mid :, :] = jnp.zeros((8, wide), F32)
    three = 3 * LANES
    xa[0:pitch, :] = jnp.zeros((pitch, 2 * three), BF16)
    xa[pitch + mid :, :] = jnp.zeros((pitch, 2 * three), BF16)

    def lay_out(value):
        sa[8 : 8 + mid, :] = value
        for pr in range(2):
            for d in range(3):
                c = pr * three + d * LANES
                xa[pitch : pitch + mid, c : c + LANES] = sa[
                    7 + d : 7 + d + mid, pr * LANES : (pr + 1) * LANES
                ].astype(BF16)

    lay_out(value)
    lhs = windows(
        xa, [(0, mid, three, 2 * three), (1, mid, 0, 2 * three), (2, mid, 0, three)]
    )
    value = jnp.maximum(dot_t(lhs, w1_ref[...]), 0.0) * mask
    lay_out(value)
    for pr in range(2):
        for pc in range(2):
            where = [(0, 1), (1, 0), (1, 1)] if pr == 0 else [(1, 0), (1, 1), (2, 0)]
            lhs = windows(
                xa,
                [(d, mid, p * three + pc * LANES, p * three + pc * LANES + wide) for d, p in where],
            )
            value = jnp.maximum(dot_t(lhs, w2_ref[pc]), 0.0) * mask
            sa[8 : 8 + mid, :] = value
            for rr in range(2):
                at = (2 * pr + rr) * 4 * LANES
                tile = value[:, rr * LANES : (rr + 1) * LANES]
                xc[:, at + (1 + pc) * LANES : at + (2 + pc) * LANES] = tile.astype(BF16)
                slot, move = (3, 9) if pc == 0 else (0, 7)
                xc[:, at + slot * LANES : at + (slot + 1) * LANES] = sa[
                    move : move + mid, rr * LANES : (rr + 1) * LANES
                ].astype(BF16)
    n_out = rows_dev * pitch
    four = 4 * LANES
    lhs = windows(
        xc, [(0, n_out, 3 * four, 4 * four), (1, n_out, 0, 4 * four), (2, n_out, 0, four)]
    )
    final = dot_t(lhs, w3_ref[...])
    final = final + pltpu.roll(final, half, 1)
    rays = jnp.concatenate(
        [final[r * pitch + LEAD : r * pitch + LEAD + cols] for r in range(rows_dev)], axis=0
    )
    turned = rays.T
    stack = jnp.concatenate(
        [
            jnp.concatenate(
                [turned[16 * v : 16 * v + 16, r * cols : (r + 1) * cols] for v in range(4)], axis=1
            )
            for r in range(rows_dev)
        ],
        axis=0,
    )
    r = lax.broadcasted_iota(jnp.int32, (4 * cols, 4 * cols), 0)
    c = lax.broadcasted_iota(jnp.int32, (4 * cols, 4 * cols), 1)
    place_of = (c & 3) * cols + (c >> 2)
    pick = jnp.where(r == place_of, 1.0, 0.0).astype(BF16)
    high, low = split16(stack)
    image = dot(high.astype(BF16), pick) + dot(low.astype(BF16), pick)
    colours = out_ref.shape[0]
    for r in range(rows_dev):
        for u in range(4):
            for p in range(colours):
                at = r * 16 + u * colours + p
                out_ref[p, 4 * r + u : 4 * r + u + 1, :] = image[at : at + 1, :]


def phase_taps():
    t = np.zeros((2, 3, 3), np.float32)
    for p in range(2):
        for a in range(3):
            t[p, (p + a - 1) // 2 + 1, a] = 1
    return t


def decoder_weights(w_conv, w_color):
    feat = w_conv.shape[-1]
    w = w_conv.reshape(w_conv.shape[0], 9, feat, feat)
    t = phase_taps()

    def build(table, kernel):
        n, k = table.shape[:2]
        made = jnp.einsum(
            "nkt,toc->nokc", jnp.asarray(table, BF16), kernel, preferred_element_type=F32
        )
        return made.astype(BF16).reshape(n * feat, k * feat)

    t0 = np.zeros((2, 2, 3, 4, 3, 3), np.float32)
    t0[:, :, :, :3] = np.einsum("pda,qfe->pqdfae", t, t)
    w0 = build(t0.reshape(4, 12, 9), w[0])
    t1 = np.zeros((2, 2, 4, 6, 3, 3), np.float32)
    for p in range(2):
        for q in range(2):
            for a in range(3):
                for e in range(3):
                    t1[p, q, p + a, q + e + 1, a, e] = 1
    w1 = build(t1.reshape(4, 24, 9), w[1])
    both = []
    for pc in range(2):
        t2 = np.zeros((2, 2, 3, 4, 3, 3), np.float32)
        t2[:, :, :, 1 - pc : 4 - pc] = np.einsum("pda,qfe->pqdfae", t, t)
        both.append(build(t2.reshape(4, 12, 9), w[2]))
    w2 = jnp.stack(both)
    colours = w_color.shape[0]
    mixed = jnp.einsum(
        "po,aeoc->paec",
        w_color.astype(F32),
        w_conv[3].astype(F32),
        precision=lax.Precision.HIGHEST,
    )
    rows = []
    for v in range(4):
        for u in range(4):
            own = jnp.pad(mixed, ((0, 0), (u, 3 - u), (v + 1, 4 - v), (0, 0)))
            rows.append(own)
        rows.append(jnp.zeros((16 - 4 * colours,) + rows[-1].shape[1:], F32))
    w3 = jnp.concatenate(rows, axis=0)
    w3 = w3.reshape(w3.shape[0], -1)
    high = w3.astype(BF16)
    low = (w3 - high.astype(F32)).astype(BF16)
    return w0, w1, w2, jnp.concatenate([high, low], axis=0)


def body(samples_in, block_order, seam_link, w_in, w_mid, w_feat, w_density, w_conv, w_color):
    blk_dev, rows_all, cols, width = samples_in.shape
    groups, place = lax.axis_size("block"), lax.axis_index("block")
    patches, patch = lax.axis_size("patch"), lax.axis_index("patch")
    nb = block_order.shape[1]
    enc = w_in.shape[1]
    feat = w_feat.shape[2]
    rows_dev = rows_all // groups
    count = rows_all * cols
    power = groups & (groups - 1) == 0
    hrays = (rows_all + 2 * EDGE) * 2 * EDGE
    hchunks = -(-hrays // LANES)
    n_own = (rows_dev + 2 * EDGE) * cols
    n_halo = (rows_dev + 2 * EDGE) * 2 * EDGE
    n_dep = 4 * n_own // LANES
    n_tail = 16
    cfg = dict(
        groups=groups,
        nb=nb,
        samples=width // enc,
        enc=enc,
        cols=cols,
        rows_all=rows_all,
        rows_dev=rows_dev,
        pitch=cols + 16,
        chunk=2 * LANES,
        n_own=n_own,
        n_halo=n_halo,
        n_dep=n_dep,
        hchunks=hchunks,
        dest=(lambda p, s: p ^ s) if power else (lambda p, s: lax.rem(p + s, groups)),
        source=(lambda p, s: p ^ s) if power else (lambda p, s: lax.rem(p + groups - s, groups)),
    )

    odd = (patch & 1) == 1
    edge_l = samples_in[:, :, :EDGE].reshape(-1, width)
    edge_r = samples_in[:, :, cols - EDGE :].reshape(-1, width)
    meta = jnp.concatenate([block_order[0], seam_link]).astype(BF16)
    meta = jnp.pad(meta[None, :], ((0, 15), (0, width - nb - 1)))
    near = jnp.concatenate([jnp.where(odd, edge_l, edge_r), meta], axis=0)
    far = jnp.concatenate([jnp.where(odd, edge_r, edge_l), meta], axis=0)
    swap_near = [(i, i ^ 1) for i in range(patches) if i ^ 1 < patches]
    swap_far = []
    for i in range(1, patches - 1, 2):
        swap_far += [(i, i + 1), (i + 1, i)]
    far = lax.ppermute(far, "patch", swap_far)
    near = lax.ppermute(near, "patch", swap_near)
    from_left = jnp.where(odd, near, far)
    from_right = jnp.where(odd, far, near)
    edges = blk_dev * rows_all * EDGE
    halo = jnp.concatenate(
        [
            from_left[:edges].reshape(blk_dev, rows_all, EDGE, width),
            from_right[:edges].reshape(blk_dev, rows_all, EDGE, width),
        ],
        axis=2,
    )
    halo = jnp.pad(halo, ((0, 0), (EDGE, EDGE), (0, 0), (0, 0))).reshape(blk_dev, hrays, width)
    order_l = from_left[edges, : nb + 1].astype(jnp.int32)
    order_r = from_right[edges, : nb + 1].astype(jnp.int32)
    flags = jnp.stack(
        [
            place,
            order_l[nb] * (patch > 0),
            seam_link[0] * (patch < patches - 1),
            place > 0,
            place < groups - 1,
            place * 0,
            place * 0,
            place * 0,
        ]
    ).astype(jnp.int32)
    info = jnp.concatenate([flags, block_order[0], order_l[:nb], order_r[:nb]])

    heads = []
    for b in range(blk_dev):
        dens = jnp.broadcast_to(w_density[b][:, None], (w_density.shape[1], feat))
        blank = jnp.zeros_like(dens)
        parts = [blank] * (2 * blk_dev)
        parts[b] = w_feat[b]
        parts[blk_dev + b] = dens
        heads.append(jnp.concatenate(parts, axis=1))
    whead = jnp.stack(heads)

    size = n_own + n_halo + n_dep + n_tail
    smem = pl.BlockSpec(memory_space=pltpu.SMEM)
    vmem = pl.BlockSpec(memory_space=pltpu.VMEM)
    bufs = pl.pallas_call(
        functools.partial(field_kernel, cfg),
        out_shape=[jax.ShapeDtypeStruct((size, LANES), BF16)] * groups,
        in_specs=[smem] + [vmem] * 5,
        out_specs=[vmem] * groups,
        scratch_shapes=[
            pltpu.VMEM((count + 2 * EDGE * cols, LANES), BF16),
            pltpu.VMEM((hrays, LANES), BF16),
            pltpu.VMEM((4 * (count + 2 * EDGE * cols) // LANES, LANES), F32),
            pltpu.VMEM((n_tail, LANES), F32),
            pltpu.VMEM((blk_dev, width, w_in.shape[2]), BF16),
        ],
        name="field",
    )(jnp.reshape(place, (1,)), samples_in.reshape(blk_dev, count, width), halo, w_in, w_mid, whead)

    got = [bufs[0]]
    for s in range(1, groups):
        if power:
            route = [(i, i ^ s) for i in range(groups)]
        else:
            route = [(i, (i + s) % groups) for i in range(groups)]
        got.append(lax.ppermute(bufs[s], "block", route))

    w0, w1, w2, w3 = decoder_weights(w_conv, w_color)
    pitch = cfg["pitch"]
    rows_in, rows_mid = rows_dev + 2 * EDGE, rows_dev + 2
    return pl.pallas_call(
        functools.partial(decoder_kernel, cfg),
        out_shape=jax.ShapeDtypeStruct((w_color.shape[0], 4 * rows_dev, 4 * cols), F32),
        in_specs=[smem] + [vmem] * (4 + groups),
        out_specs=vmem,
        scratch_shapes=[
            pltpu.VMEM(((rows_in + 2) * pitch, LANES), F32),
            pltpu.VMEM((rows_in * pitch, 2 * LANES), BF16),
            pltpu.VMEM((rows_mid * pitch + 16, 2 * LANES), F32),
            pltpu.VMEM(((rows_mid + 2) * pitch, 6 * LANES), BF16),
            pltpu.VMEM((rows_mid * pitch, 16 * LANES), BF16),
            pltpu.VMEM((hchunks * LANES, groups * LANES), F32),
            pltpu.SMEM((nb,), jnp.int32),
        ],
        name="decoder",
    )(info, w0, w1, w2, w3, *got)


def solution(mesh):
    return jax.shard_map(
        body,
        mesh=mesh,
        in_specs=(
            P("block", None, "patch", None),
            P("patch", None),
            P("patch"),
            P("block", None, None),
            P("block", None, None, None),
            P("block", None, None),
            P("block", None),
            P(),
            P(),
        ),
        out_specs=P(None, "block", "patch"),
        check_vma=False,
    )
```

time: 137 us -> 52.2 us (0.38)
  the two profiles are of different devices: /device:TPU:17 before, /device:TPU:7 now
where the time goes in v1:
time: 52.2 us; the launch traced here: 51.8 us
  Pallas kernels  16.6 us (32%)
  local copies, waits for them, and re-layouts  11.5 us (22%)
  starting transfers between devices  7.25 us (14%)
  waiting for transfers between devices  6.04 us (12%)
  other arithmetic  5.89 us (11%)
  matrix products  2.9 us (6%)
  between operations  1.68 us (3%)
    pallas_call x1, Pallas kernels, body(): pl.pallas_call(functools.partial(field_kernel, cfg), out_shape=[jax.Shape...  9.42 us
    pallas_call x1, Pallas kernels, body(): pl.pallas_call(functools.partial(decoder_kernel, cfg), out_shape=jax.Shap...  7.13 us
    ppermute x3, waiting for transfers between devices, body(): got.append(lax.ppermute(bufs[s], 'block', route))  6.03 us
    ppermute x1, starting transfers between devices, body(): far = lax.ppermute(far, 'patch', swap_far)  4.12 us
    reshape x2, local copies, waits for them, and re-layouts, build(): return made.astype(BF16).reshape(n * feat, k * feat)  3.14 us
    ppermute x3, starting transfers between devices, body(): got.append(lax.ppermute(bufs[s], 'block', route))  2.88 us
    another operation x2, local copies, waits for them, and re-layouts, decoder_weights(): w2 = jnp.stack(both)  2.09 us
    unnamed x50, local copies, waits for them, and re-layouts  2.04 us
  transfers between devices with their start and end apart: 5, of which 2 were waited for; matrix products, arithmetic and copies ran while one was open for 30% of the time, Pallas kernels for 0%

profile of v1, /device:TPU:7, one launch (start us, length us, event | category | flops | bytes accessed | tf_op | source)
XLA Modules:
  0.0 51.8 jit_solution(940221793410502192)
XLA Ops:
  0.7 0.7 %convert.11 = bf16[1,8]{1,0:T(2,128)(2,1)S(1)} convert(s32[1,8]{1,0:T(1,128)} %param.14) | non-fusion elementwise | flops 8 | bytes 48 | tf_op jit(solution)/shard_map/convert.4
  1.3 0.9 %broadcast_select_fusion = (bf16[2,16,2,128]{3,2,1,0:T(2,128)(2,1)S(1)}, bf16[2,16,2,128]{3,2,1,0:T(2,128)(2,1)S(1)}) fusion(pred[]{:T(512)S(6)} %eq.3, bf16[2,16,64,128]{3,2,1,0:T(8,128)(2,1)} %param.13), kind=kLoop, calls=%fused_computation.49 | loop fusion | flops 16384 | bytes 65537 | tf_op jit(solution)/shard_map/jit(_where)/select_n | solution.py:408
  2.3 0.6 %pad_maximum_fusion.3 = (bf16[80,128]{1,0:T(8,128)(2,1)}, bf16[80,128]{1,0:T(8,128)(2,1)}) fusion(bf16[16,128]{1,0:T(8,128)(2,1)S(1)} %fusion.21, bf16[64,128]{1,0:T(8,128)(2,1)S(1)} %bitcast.85, bf16[64,128]{1,0:T(8,128)(2,1)S(1)} %bitcast.86), kind=kLoop, calls=%fused_computation.51 | loop fusion | flops 71680 | bytes 77824 | tf_op jit(solution)/shard_map/concatenate | solution.py:408
  2.9 0.3 collective-permute-start
  3.2 4.1 %collective-permute-start.1 = (bf16[80,128]{1,0:T(8,128)(2,1)}, bf16[80,128]{1,0:T(8,128)(2,1)S(1)}, u32[]{:S(2)}, u32[]{:S(2)}) collective-permute-start(bf16[80,128]{1,0:T(8,128)(2,1)} %get-tuple-element.28), channel_id=1, source_target_pairs={{1,2},{2,1},{3,4},{4,3},{5,6},{6,5},{9,10},{10,9},{11,12},{12,11},... | collective-permute-start | bytes 61448 | tf_op jit(solution)/shard_map/ppermute | solution.py:413
  7.3 1.8 %fusion.24 = (bf16[1,3,3,64,64]{4,3,2,1,0:T(8,128)(2,1)S(1)}, bf16[1,3,3,64,64]{4,3,2,1,0:T(8,128)(2,1)}, bf16[1,3,3,64,64]{4,3,2,1,0:T(8,128)(2,1)S(1)}) fusion(bf16[4,3,3,64,64]{4,3,2,1,0:T(8,128)(2,1)} %param.20), kind=kLoop, calls=%fused_computation.70 | loop fusion | bytes 442368 | tf_op jit(solution)/shard_map/slice | solution.py:346
  9.1 1.0 %fusion.12 = f32[3,3,3,64]{3,0,2,1:T(4,128)S(1)} fusion(bf16[4,3,3,64,64]{4,3,2,1,0:T(8,128)(2,1)} %param.20, bf16[3,64]{1,0:T(4,128)(2,1)S(1)} %copy-done), kind=kOutput, calls=%fused_computation.20 | convolution fusion | flops 221184 | bytes 154752 | tf_op jit(solution)/shard_map/po,aeoc->paec/dot_general | solution.py:349
  10.6 0.4 reshape.74
  11.1 0.3 copy-done.7
  11.5 0.7 %copy.71 = bf16[1,256,64]{2,1,0:T(8,128)(2,1)} copy(bf16[1,256,64]{1,2,0:T(8,128)(2,1)S(1)} %get-tuple-element.25) | data formatting | bytes 65536
  12.2 0.6 %slice_reduce_fusion.1 = (bf16[256]{0:T(256)(128)(2,1)}, bf16[256]{0:T(256)(128)(2,1)S(1)}) fusion(bf16[2,256]{1,0:T(2,128)(2,1)S(1)} %copy-done.11), kind=kLoop, calls=%fused_computation.65 | loop fusion | bytes 2048 | tf_op jit(solution)/shard_map/slice | solution.py:444
  12.8 0.4 fusion.2
  13.2 1.4 %reshape.91 = bf16[1,256,768]{2,1,0:T(8,128)(2,1)} reshape(bf16[4,64,12,64]{3,2,1,0:T(8,128)(2,1)S(1)} %fusion.2) | data formatting | bytes 786432 | tf_op jit(solution)/shard_map/stack;reshape | solution.py:347
  14.7 0.4 fusion.3
  15.1 0.7 %reshape.92 = bf16[1,256,768]{2,1,0:T(8,128)(2,1)S(1)} reshape(bf16[4,64,12,64]{3,2,1,0:T(8,128)(2,1)S(1)} %fusion.3) | data formatting | bytes 786432 | tf_op jit(solution)/shard_map/stack;reshape | solution.py:347
  15.8 0.4 fusion.1
  16.2 0.9 %pad_maximum_fusion.1.w3_ref = bf16[128,3072]{1,0:T(8,128)(2,1)} fusion(bf16[64,3072]{1,0:T(8,128)(2,1)S(1)} %get-tuple-element.15, bf16[64,3072]{1,0:T(8,128)(2,1)S(1)} %get-tuple-element.16), kind=kLoop, calls=%fused_computation.9 | loop fusion | flops 1572864 | bytes 1572864 | tf_op jit(solution)/shard_map/concatenate | solution.py:365
  17.2 1.0 %pad_maximum_fusion.w2_ref = bf16[2,256,768]{2,1,0:T(8,128)(2,1)} fusion(bf16[1,256,768]{2,1,0:T(8,128)(2,1)S(1)} %reshape.92, bf16[1,256,768]{2,1,0:T(8,128)(2,1)S(1)} %copy-done.1), kind=kLoop, calls=%fused_computation.8 | loop fusion | flops 393216 | bytes 1572864 | tf_op jit(solution)/shard_map/stack | solution.py:347
  18.2 0.6 %fusion = bf16[4,64,24,64]{3,2,1,0:T(8,128)(2,1)S(1)} fusion(bf16[4,24,9,1]{1,2,3,0:T(8,128)(2,1)S(1)} %copy-done.9, bf16[9,64,64]{2,1,0:T(8,128)(2,1)S(1)} %bitcast.79), kind=kOutput, calls=%fused_computation.1 | convolution fusion | flops 7471104 | bytes 861888 | tf_op jit(solution)/shard_map/nkt,toc->nokc/dot_general | solution.py:327
  19.2 0.7 %pad_maximum_fusion.2.whead_ref = bf16[2,256,256]{2,1,0:T(8,128)(2,1)} fusion(bf16[1,256,256]{2,1,0:T(8,128)(2,1)S(1)} %get-tuple-element.23, bf16[1,256,256]{2,1,0:T(8,128)(2,1)S(1)} %get-tuple-element.22), kind=kLoop, calls=%fused_computation.11 | loop fusion | flops 131072 | bytes 524288 | tf_op jit(solution)/shard_map/stack | solution.py:450
  20.0 1.7 %reshape.73.w1_ref = bf16[256,1536]{1,0:T(8,128)(2,1)} reshape(bf16[4,64,24,64]{3,2,1,0:T(8,128)(2,1)S(1)} %fusion) | data formatting | bytes 1572864 | tf_op jit(solution)/shard_map/reshape | solution.py:330
  21.7 1.4 %reshape.90.w0_ref = bf16[256,768]{1,0:T(8,128)(2,1)} reshape(bf16[4,64,12,64]{3,2,1,0:T(8,128)(2,1)S(1)} %fusion.1) | data formatting | bytes 786432 | tf_op jit(solution)/shard_map/reshape | solution.py:330
  23.2 0.6 %slice.67 = s32[1,1]{1,0:T(1,128)} slice(s32[1,9]{1,0:T(1,128)S(1)} %slice_convert_fusion), slice={[0:1], [8:9]} | slice | bytes 8 | tf_op jit(solution)/shard_map/slice | solution.py:431
  23.8 0.7 %select_maximum_fusion = bf16[2,20,4,128]{3,2,1,0:T(4,128)(2,1)} fusion(bf16[2,16,2,128]{3,2,1,0:T(2,128)(2,1)S(1)} %bitcast.88, bf16[2,16,2,128]{3,2,1,0:T(2,128)(2,1)S(1)} %bitcast.87), kind=kLoop, calls=%fused_computation.48 | loop fusion | flops 184320 | bytes 73728 | tf_op jit(solution)/shard_map/concatenate | solution.py:418
  24.5 9.4 %field.1 = (bf16[576,128]{1,0:T(8,128)(2,1)}, bf16[576,128]{1,0:T(8,128)(2,1)}, bf16[576,128]{1,0:T(8,128)(2,1)}, bf16[576,128]{1,0:T(8,128)(2,1)}) custom-call(s32[1]{0:T(128)} %bitcast.place_ref, bf16[2,1024,128]{2,1,0:T(8,128)(2,1)} %bitcast.81, bf16[2,80,128]{2,1,0:T(8,128)(2,1)} %bitcast.84, bf16[2,32,256]{2,1,0:T(8,128)(2,1)} %win_ref.1, ...), custom_call_target="tpu_custom_call" | custom-call | tf_op jit(solution)/shard_map/field/pallas_call | solution.py:455
  33.9 1.2 %collective-permute-start.2 = (bf16[576,128]{1,0:T(8,128)(2,1)}, bf16[576,128]{1,0:T(8,128)(2,1)S(1)}, u32[]{:S(2)}, u32[]{:S(2)}) collective-permute-start(bf16[576,128]{1,0:T(8,128)(2,1)} %get-tuple-element.10), channel_id=1, source_target_pairs={{0,8},{8,0},{16,24},{24,16},{1,9},{9,1},{17,25},{25,17},{2,10},{10... | collective-permute-start | bytes 442376 | tf_op jit(solution)/shard_map/ppermute | solution.py:476
  35.3 1.4 %collective-permute-start.4 = (bf16[576,128]{1,0:T(8,128)(2,1)}, bf16[576,128]{1,0:T(8,128)(2,1)S(1)}, u32[]{:S(2)}, u32[]{:S(2)}) collective-permute-start(bf16[576,128]{1,0:T(8,128)(2,1)} %get-tuple-element.12), channel_id=1, source_target_pairs={{0,24},{8,16},{16,8},{24,0},{1,25},{9,17},{17,9},{25,1},{2,26},{10... | collective-permute-start | bytes 442376 | tf_op jit(solution)/shard_map/ppermute | solution.py:476
  37.4 0.6 %concatenate.41.info_ref = s32[32]{0:T(128)} concatenate(s32[1]{0:T(128)} %bitcast.place_ref, s32[1]{0:T(128)} %bitcast.5, s32[1]{0:T(128)} %bitcast.7, s32[1]{0:T(128)} %bitcast.8, s32[1]{0:T(128)} %bitcast.9, s32[1]{0:T(128)} %constant.31.clone.1, s32[2]{0:T(128)S(1)} %broadcast.50, s32[8]{0:T(128)S(1)} %bitcast.89, s32[8]{0:T(128)S(1)} %slice_bitcast_fusion.1, s32[8]{0:T(128)S(1)} %fusion.23), dimensions={0} | concatenate | bytes 256 | tf_op jit(solution)/shard_map/concatenate | solution.py:440
  38.0 2.7 %collective-permute-done.3.rest_2_ = bf16[576,128]{1,0:T(8,128)(2,1)S(1)} collective-permute-done((bf16[576,128]{1,0:T(8,128)(2,1)}, bf16[576,128]{1,0:T(8,128)(2,1)S(1)}, u32[]{:S(2)}, u32[]{:S(2)}) %collective-permute-start.3) | collective-permute-done | bytes 147488 | tf_op jit(solution)/shard_map/ppermute | solution.py:476
  40.7 3.3 %collective-permute-done.4.rest_3_ = bf16[576,128]{1,0:T(8,128)(2,1)S(1)} collective-permute-done((bf16[576,128]{1,0:T(8,128)(2,1)}, bf16[576,128]{1,0:T(8,128)(2,1)S(1)}, u32[]{:S(2)}, u32[]{:S(2)}) %collective-permute-start.4) | collective-permute-done | bytes 147488 | tf_op jit(solution)/shard_map/ppermute | solution.py:476
  44.1 0.6 %copy-done.6 = bf16[576,128]{1,0:T(8,128)(2,1)} copy-done((bf16[576,128]{1,0:T(8,128)(2,1)}, bf16[576,128]{1,0:T(8,128)(2,1)S(1)}, u32[]{:S(2)}) %copy-start.6) | copy-done | bytes 147480
  44.7 7.1 %decoder.1 = f32[3,16,256]{2,1,0:T(8,128)} custom-call(s32[32]{0:T(128)} %concatenate.41.info_ref, bf16[256,768]{1,0:T(8,128)(2,1)} %reshape.90.w0_ref, bf16[256,1536]{1,0:T(8,128)(2,1)} %reshape.73.w1_ref, bf16[2,256,768]{2,1,0:T(8,128)(2,1)} %pad_maximum_fusion.w2_ref, bf16[128,3072]{1,0:T(8,128)(2,1)} %pad_maximum_fusion.1.w3_ref, ...), custom_call_target="tpu_custom_call" | custom-call | tf_op jit(solution)/shard_map/decoder/pallas_call | solution.py:481
  (66 shorter events, 1.2 us)
Async XLA Ops:
  0.0 9.1 %copy-start = (bf16[3,64]{1,0:T(4,128)(2,1)S(1)}, bf16[3,64]{1,0:T(4,128)(2,1)}, u32[]{:S(2)}) copy-start(bf16[3,64]{1,0:T(4,128)(2,1)} %param.21) | copy-start | bytes 1156
  2.9 20.2 %collective-permute-start = (bf16[80,128]{1,0:T(8,128)(2,1)}, bf16[80,128]{1,0:T(8,128)(2,1)S(1)}, u32[]{:S(2)}, u32[]{:S(2)}) collective-permute-start(bf16[80,128]{1,0:T(8,128)(2,1)} %get-tuple-element.29), channel_id=1, source_target_pairs={{0,1},{1,0},{2,3},{3,2},{4,5},{5,4},{6,7},{7,6},{8,9},{9,8},{10,11... | collective-permute-start | bytes 61448 | tf_op jit(solution)/shard_map/ppermute | solution.py:414
  3.2 19.9 %collective-permute-start.1 = (bf16[80,128]{1,0:T(8,128)(2,1)}, bf16[80,128]{1,0:T(8,128)(2,1)S(1)}, u32[]{:S(2)}, u32[]{:S(2)}) collective-permute-start(bf16[80,128]{1,0:T(8,128)(2,1)} %get-tuple-element.28), channel_id=1, source_target_pairs={{1,2},{2,1},{3,4},{4,3},{5,6},{6,5},{9,10},{10,9},{11,12},{12,11},... | collective-permute-start | bytes 61448 | tf_op jit(solution)/shard_map/ppermute | solution.py:413
  10.5 0.8 %copy-start.7 = (bf16[2,256,64]{1,2,0:T(8,128)(2,1)S(1)}, bf16[2,256,64]{1,2,0:T(8,128)(2,1)}, u32[]{:S(2)}) copy-start(bf16[2,256,64]{1,2,0:T(8,128)(2,1)} %param.18) | copy-start | bytes 196612
  10.5 1.7 %copy-start.11 = (bf16[2,256]{1,0:T(2,128)(2,1)S(1)}, bf16[2,256]{1,0:T(2,128)(2,1)}, u32[]{:S(2)}) copy-start(bf16[2,256]{1,0:T(2,128)(2,1)} %param.19) | copy-start | bytes 3076
  10.5 2.3 %copy-start.10 = (bf16[4,12,9,1]{2,1,3,0:T(8,128)(2,1)S(1)}, bf16[4,12,9,1]{2,1,3,0:T(8,128)(2,1)}, u32[]{:S(2)}) copy-start(bf16[4,12,9,1]{2,1,3,0:T(8,128)(2,1)} %constant.81) | copy-start | bytes 2596
  11.4 3.3 %copy-start.8 = (bf16[4,12,9,1]{2,1,3,0:T(8,128)(2,1)S(1)}, bf16[4,12,9,1]{2,1,3,0:T(8,128)(2,1)}, u32[]{:S(2)}) copy-start(bf16[4,12,9,1]{2,1,3,0:T(8,128)(2,1)} %constant.79) | copy-start | bytes 2596
  15.8 1.4 %copy-start.1 = (bf16[1,256,768]{2,1,0:T(8,128)(2,1)S(1)}, bf16[1,256,768]{2,1,0:T(8,128)(2,1)}, u32[]{:S(2)}) copy-start(bf16[1,256,768]{2,1,0:T(8,128)(2,1)} %reshape.91) | copy-start | bytes 1179652
  16.2 2.0 %copy-start.2 = (bf16[1,3,3,64,64]{4,3,2,1,0:T(8,128)(2,1)S(1)}, bf16[1,3,3,64,64]{4,3,2,1,0:T(8,128)(2,1)}, u32[]{:S(2)}) copy-start(bf16[1,3,3,64,64]{4,3,2,1,0:T(8,128)(2,1)} %get-tuple-element.18) | copy-start | bytes 221188
  16.2 2.0 %copy-start.9 = (bf16[4,24,9,1]{1,2,3,0:T(8,128)(2,1)S(1)}, bf16[4,24,9,1]{1,2,3,0:T(8,128)(2,1)}, u32[]{:S(2)}) copy-start(bf16[4,24,9,1]{1,2,3,0:T(8,128)(2,1)} %constant.80) | copy-start | bytes 5188
  17.2 1.6 %copy-start.12 = (bf16[256]{0:T(256)(128)(2,1)S(1)}, bf16[256]{0:T(256)(128)(2,1)}, u32[]{:S(2)}) copy-start(bf16[256]{0:T(256)(128)(2,1)} %get-tuple-element.13) | copy-start | bytes 1540
  17.2 1.8 %copy-start.3 = (bf16[1,256,64]{2,1,0:T(8,128)(2,1)S(1)}, bf16[1,256,64]{2,1,0:T(8,128)(2,1)}, u32[]{:S(2)}) copy-start(bf16[1,256,64]{2,1,0:T(8,128)(2,1)} %copy.71) | copy-start | bytes 98308
  21.7 15.7 %copy-start.13 = (s32[1,8]{1,0:T(1,128)S(1)}, s32[1,8]{1,0:T(1,128)}, u32[]{:S(2)}) copy-start(s32[1,8]{1,0:T(1,128)} %param.14) | copy-start | bytes 100
  33.9 4.2 %collective-permute-start.2 = (bf16[576,128]{1,0:T(8,128)(2,1)}, bf16[576,128]{1,0:T(8,128)(2,1)S(1)}, u32[]{:S(2)}, u32[]{:S(2)}) collective-permute-start(bf16[576,128]{1,0:T(8,128)(2,1)} %get-tuple-element.10), channel_id=1, source_target_pairs={{0,8},{8,0},{16,24},{24,16},{1,9},{9,1},{17,25},{25,17},{2,10},{10... | collective-permute-start | bytes 442376 | tf_op jit(solution)/shard_map/ppermute | solution.py:476
  35.1 5.6 %collective-permute-start.3 = (bf16[576,128]{1,0:T(8,128)(2,1)}, bf16[576,128]{1,0:T(8,128)(2,1)S(1)}, u32[]{:S(2)}, u32[]{:S(2)}) collective-permute-start(bf16[576,128]{1,0:T(8,128)(2,1)} %get-tuple-element.11), channel_id=1, source_target_pairs={{0,16},{8,24},{16,0},{24,8},{1,17},{9,25},{17,1},{25,9},{2,18},{10... | collective-permute-start | bytes 442376 | tf_op jit(solution)/shard_map/ppermute | solution.py:476
  35.3 8.7 %collective-permute-start.4 = (bf16[576,128]{1,0:T(8,128)(2,1)}, bf16[576,128]{1,0:T(8,128)(2,1)S(1)}, u32[]{:S(2)}, u32[]{:S(2)}) collective-permute-start(bf16[576,128]{1,0:T(8,128)(2,1)} %get-tuple-element.12), channel_id=1, source_target_pairs={{0,24},{8,16},{16,8},{24,0},{1,25},{9,17},{17,9},{25,1},{2,26},{10... | collective-permute-start | bytes 442376 | tf_op jit(solution)/shard_map/ppermute | solution.py:476
  38.0 6.0 %copy-start.4 = (bf16[576,128]{1,0:T(8,128)(2,1)}, bf16[576,128]{1,0:T(8,128)(2,1)S(1)}, u32[]{:S(2)}) copy-start(bf16[576,128]{1,0:T(8,128)(2,1)S(1)} %collective-permute-done.2.rest_1_) | copy-start | bytes 442372
  40.7 3.3 %copy-start.5 = (bf16[576,128]{1,0:T(8,128)(2,1)}, bf16[576,128]{1,0:T(8,128)(2,1)S(1)}, u32[]{:S(2)}) copy-start(bf16[576,128]{1,0:T(8,128)(2,1)S(1)} %collective-permute-done.3.rest_2_) | copy-start | bytes 442372
  44.1 0.6 %copy-start.6 = (bf16[576,128]{1,0:T(8,128)(2,1)}, bf16[576,128]{1,0:T(8,128)(2,1)S(1)}, u32[]{:S(2)}) copy-start(bf16[576,128]{1,0:T(8,128)(2,1)S(1)} %collective-permute-done.4.rest_3_) | copy-start | bytes 442372

commit v2 on v1

--- a/solution.py
+++ b/solution.py
@@ -1,6 +1,4 @@
 import functools
-
-import numpy as np
 
 import jax
 import jax.numpy as jnp
@@ -80,10 +78,10 @@
     return jnp.concatenate([high, low], axis=0)
 
 
-def field_kernel(cfg, place_ref, own_ref, halo_ref, win_ref, wmid_ref, whead_ref, *rest):
+def field_kernel(cfg, at_ref, own_ref, near_ref, far_ref, win_ref, wmid_ref, wf_ref, wd_ref, *rest):
     groups, samples, enc = cfg["groups"], cfg["samples"], cfg["enc"]
     outs = rest[:groups]
-    col_own, col_halo, dep_own, dep_halo, tiled = rest[groups:]
+    col_own, col_halo, dep_own, dep_halo, tiled, whead_ref, halo_ref = rest[groups:]
     cols, rows_all, rows_dev = cfg["cols"], cfg["rows_all"], cfg["rows_dev"]
     blocks = own_ref.shape[0]
     pad = EDGE * cols
@@ -95,6 +93,28 @@
     for b in range(blocks):
         for s in range(samples):
             tiled[b, s * enc : (s + 1) * enc, :] = win_ref[b]
+    feat, width = wf_ref.shape[2], wf_ref.shape[1]
+    dens = wd_ref[...].astype(F32)
+    for b in range(blocks):
+        r = lax.broadcasted_iota(jnp.int32, (feat, 2 * LANES), 0)
+        c = lax.broadcasted_iota(jnp.int32, (feat, 2 * LANES), 1)
+        lift = jnp.where(c - b * feat == r, 1.0, 0.0).astype(BF16)
+        r = lax.broadcasted_iota(jnp.int32, (width, width), 0)
+        c = lax.broadcasted_iota(jnp.int32, (width, width), 1)
+        diag = jnp.where(r == c, dens[b : b + 1], 0.0).astype(BF16)
+        c = lax.broadcasted_iota(jnp.int32, (width, 2 * LANES), 1)
+        repeat = jnp.where((c - LANES) // feat == b, 1.0, 0.0).astype(BF16)
+        whead_ref[b] = (dot(wf_ref[b], lift) + dot(diag, repeat)).astype(BF16)
+    odd = at_ref[1] == 1
+    near, far = near_ref[...].astype(F32), far_ref[...].astype(F32)
+    sides = [jnp.where(odd, near, far), jnp.where(odd, far, near)]
+    side_rays = rows_all * EDGE
+    side_pitch = side_rays + 2 * EDGE * EDGE
+    halo_ref[...] = jnp.zeros(halo_ref.shape, F32)
+    for b in range(blocks):
+        for i, side in enumerate(sides):
+            q = i * side_pitch + EDGE * EDGE
+            halo_ref[b, q : q + side_rays, :] = side[b * side_rays : (b + 1) * side_rays]
     step = cfg["chunk"]
     for first in range(0, count, step):
         xs = [own_ref[b, first : first + step, :] for b in range(blocks)]
@@ -103,9 +123,9 @@
         for k in range(step // LANES):
             at = 4 * ((pad + first) // LANES + k)
             dep_own[at : at + 4, :] = depth_rows(depth[k * LANES : (k + 1) * LANES])
-    xs = [halo_ref[b] for b in range(blocks)]
+    xs = [halo_ref[b].astype(BF16) for b in range(blocks)]
     colour, depth = field_rays(xs, tiled, wmid_ref, whead_ref, samples, enc)
-    col_halo[...] = colour.astype(BF16)
+    col_halo[...] = colour
     hrays = depth.shape[0]
     for k in range(cfg["hchunks"]):
         part = depth[k * LANES : min((k + 1) * LANES, hrays)]
@@ -113,14 +133,17 @@
             part = jnp.concatenate([part, jnp.zeros((LANES - part.shape[0], LANES), F32)], axis=0)
         dep_halo[4 * k : 4 * k + 4, :] = depth_rows(part)
     n_own, n_halo, n_dep = cfg["n_own"], cfg["n_halo"], cfg["n_dep"]
-    place = place_ref[0]
+    place = at_ref[0]
+    half = n_halo // 2
     for s in range(groups):
         dest = cfg["dest"](place, s)
         out = outs[s]
         start = pl.multiple_of(dest * (rows_dev * cols), LANES)
         out[0:n_own, :] = col_own[pl.ds(start, n_own), :]
-        start = pl.multiple_of(dest * (rows_dev * 2 * EDGE), 16)
-        out[n_own : n_own + n_halo, :] = col_halo[pl.ds(start, n_halo), :]
+        for i in range(2):
+            start = pl.multiple_of(i * side_pitch + dest * (rows_dev * EDGE), 8)
+            q = n_own + i * half
+            out[q : q + half, :] = col_halo[pl.ds(start, half), :].astype(BF16)
         start = pl.multiple_of(dest * (4 * rows_dev * cols // LANES), 8)
         at = n_own + n_halo
         out[at : at + n_dep, :] = dep_own[pl.ds(start, n_dep), :].astype(BF16)
@@ -171,8 +194,9 @@
         stack = jnp.concatenate([own_rows[s][4 * k : 4 * k + 4] for s in range(groups)], axis=0)
         factors.append(jnp.exp(-dot(earlier[0], stack.astype(BF16))))
     lane = lax.broadcasted_iota(jnp.int32, (nb, LANES), 1)
-    on_left = (lane & (2 * EDGE - 1)) < EDGE
+    side_pitch = (cfg["rows_all"] + 2 * EDGE) * EDGE
     for k in range(cfg["hchunks"]):
+        on_left = lane + k * LANES < side_pitch
         stack = jnp.concatenate(
             [halo_rows[s][4 * k : 4 * k + 4] for s in range(groups)], axis=0
         ).astype(BF16)
@@ -208,12 +232,13 @@
             comp[q : q + cols, :] = mixed[t * cols : (t + 1) * cols]
     for k in range(cfg["hchunks"]):
         rep[k * LANES : (k + 1) * LANES, :] = spread(chunks + k)
-    start = pl.multiple_of(place * (rows_dev * 2 * EDGE), 16)
-    mixed = mix(rep[pl.ds(start, n_halo), :], n_own, n_halo)
-    for r in range(rows_in):
-        q = base + r * pitch + LEAD
-        comp[q - EDGE : q, :] = mixed[r * 2 * EDGE : r * 2 * EDGE + EDGE]
-        comp[q + cols : q + cols + EDGE, :] = mixed[r * 2 * EDGE + EDGE : (r + 1) * 2 * EDGE]
+    size = n_halo // 2
+    for i in range(2):
+        start = pl.multiple_of(i * side_pitch + place * (rows_dev * EDGE), 8)
+        mixed = mix(rep[pl.ds(start, size), :], n_own + i * size, size)
+        for r in range(rows_in):
+            q = base + r * pitch + LEAD + (cols if i else -EDGE)
+            comp[q : q + EDGE, :] = mixed[r * EDGE : (r + 1) * EDGE]
 
     n_in = rows_in * pitch
     lane = lax.broadcasted_iota(jnp.int32, (n_in, LANES), 1)
@@ -305,64 +330,110 @@
     for r in range(rows_dev):
         for u in range(4):
             for p in range(colours):
-                at = r * 16 + u * colours + p
+                at = r * 16 + u * 4 + p
                 out_ref[p, 4 * r + u : 4 * r + u + 1, :] = image[at : at + 1, :]
 
 
-def phase_taps():
-    t = np.zeros((2, 3, 3), np.float32)
-    for p in range(2):
-        for a in range(3):
-            t[p, (p + a - 1) // 2 + 1, a] = 1
-    return t
-
-
-def decoder_weights(w_conv, w_color):
-    feat = w_conv.shape[-1]
-    w = w_conv.reshape(w_conv.shape[0], 9, feat, feat)
-    t = phase_taps()
-
-    def build(table, kernel):
-        n, k = table.shape[:2]
-        made = jnp.einsum(
-            "nkt,toc->nokc", jnp.asarray(table, BF16), kernel, preferred_element_type=F32
-        )
-        return made.astype(BF16).reshape(n * feat, k * feat)
-
-    t0 = np.zeros((2, 2, 3, 4, 3, 3), np.float32)
-    t0[:, :, :, :3] = np.einsum("pda,qfe->pqdfae", t, t)
-    w0 = build(t0.reshape(4, 12, 9), w[0])
-    t1 = np.zeros((2, 2, 4, 6, 3, 3), np.float32)
+def phase_taps(p, d):
+    return [a for a in range(3) if (p + a - 1) // 2 + 1 == d]
+
+
+def weights_kernel(conv_ref, colour_ref, after_ref, w0_ref, w1_ref, w2_ref, w3_ref):
+    feat = conv_ref.shape[1]
+    r = lax.broadcasted_iota(jnp.int32, (feat, LANES), 0)
+    lane = lax.broadcasted_iota(jnp.int32, (feat, LANES), 1)
+    twice = jnp.where((lane == r) | (lane == r + feat), 1.0, 0.0).astype(BF16)
+    low = lane < feat
+    zero = jnp.zeros((feat, LANES), F32)
+    taps = [
+        dot(conv_ref[k * 9 * feat : (k + 1) * 9 * feat, :], twice) for k in range(4)
+    ]
+
+    def tap(k, a, e):
+        at = (a * 3 + e) * feat
+        return taps[k][at : at + feat]
+
+    def pair(left, right):
+        if left is None and right is None:
+            return zero
+        if left is right:
+            return left
+        return jnp.where(low, zero if left is None else left, zero if right is None else right)
+
+    def put(ref, n, j, tile):
+        ref[n * feat : (n + 1) * feat, j * LANES : (j + 1) * LANES] = tile.astype(BF16)
+
+    for k in (0, 2):
+        sums = {}
+        for p in range(2):
+            for q in range(2):
+                for d in range(3):
+                    for f in range(3):
+                        parts = [tap(k, a, e) for a in phase_taps(p, d) for e in phase_taps(q, f)]
+                        sums[p, q, d, f] = functools.reduce(jnp.add, parts) if parts else None
+        for p in range(2):
+            for q in range(2):
+                n = 2 * p + q
+                for d in range(3):
+                    row = [sums[p, q, d, f] for f in range(3)]
+                    layouts = [[None] + row, row + [None]]
+                    refs = [w2_ref.at[0], w2_ref.at[1]] if k == 2 else [None, w0_ref]
+                    for ref, blocks in zip(refs, layouts):
+                        if ref is not None:
+                            put(ref, n, 2 * d, pair(blocks[0], blocks[1]))
+                            put(ref, n, 2 * d + 1, pair(blocks[2], blocks[3]))
+
+    def pick(table, a, e):
+        return table(a, e) if 0 <= a < 3 and 0 <= e < 3 else None
+
     for p in range(2):
         for q in range(2):
-            for a in range(3):
-                for e in range(3):
-                    t1[p, q, p + a, q + e + 1, a, e] = 1
-    w1 = build(t1.reshape(4, 24, 9), w[1])
-    both = []
-    for pc in range(2):
-        t2 = np.zeros((2, 2, 3, 4, 3, 3), np.float32)
-        t2[:, :, :, 1 - pc : 4 - pc] = np.einsum("pda,qfe->pqdfae", t, t)
-        both.append(build(t2.reshape(4, 12, 9), w[2]))
-    w2 = jnp.stack(both)
-    colours = w_color.shape[0]
-    mixed = jnp.einsum(
-        "po,aeoc->paec",
-        w_color.astype(F32),
-        w_conv[3].astype(F32),
-        precision=lax.Precision.HIGHEST,
-    )
-    rows = []
-    for v in range(4):
-        for u in range(4):
-            own = jnp.pad(mixed, ((0, 0), (u, 3 - u), (v + 1, 4 - v), (0, 0)))
-            rows.append(own)
-        rows.append(jnp.zeros((16 - 4 * colours,) + rows[-1].shape[1:], F32))
-    w3 = jnp.concatenate(rows, axis=0)
-    w3 = w3.reshape(w3.shape[0], -1)
-    high = w3.astype(BF16)
-    low = (w3 - high.astype(F32)).astype(BF16)
-    return w0, w1, w2, jnp.concatenate([high, low], axis=0)
+            for row in range(4):
+                for j in range(3):
+                    blocks = [
+                        pick(lambda a, e: tap(1, a, e), row - p, c - 1 - q)
+                        for c in (2 * j, 2 * j + 1)
+                    ]
+                    put(w1_ref, 2 * p + q, row * 3 + j, pair(*blocks))
+
+    colours = colour_ref.shape[0]
+    given = colour_ref[...].astype(F32)
+    sub = lax.broadcasted_iota(jnp.int32, (8, feat), 0)
+    mixer = jnp.zeros((8, feat), F32)
+    for p in range(colours):
+        mixer = jnp.where((sub & 3) == p, given[p : p + 1], mixer)
+    mixer = mixer.astype(BF16)
+    mixed = {
+        (a, e): dot(mixer, tap(3, a, e).astype(BF16)) for a in range(3) for e in range(3)
+    }
+    lane = lax.broadcasted_iota(jnp.int32, (8, LANES), 1) < feat
+    upper = lax.broadcasted_iota(jnp.int32, (8, LANES), 0) < 4
+    blank = jnp.zeros((8, LANES), F32)
+
+    def choose(mask, x, y):
+        if x is None and y is None:
+            return None
+        return jnp.where(mask, blank if x is None else x, blank if y is None else y)
+
+    for row in range(6):
+        for j in range(4):
+            pieces = []
+            for v in range(4):
+                for u in (0, 2):
+                    halves = [
+                        choose(
+                            lane,
+                            pick(lambda a, e: mixed[a, e], row - w, 2 * j - 1 - v),
+                            pick(lambda a, e: mixed[a, e], row - w, 2 * j - v),
+                        )
+                        for w in (u, u + 1)
+                    ]
+                    made = choose(upper, *halves)
+                    pieces.append(blank if made is None else made)
+            tile = jnp.concatenate(pieces, axis=0)
+            high, low16 = split16(tile)
+            at = (row * 4 + j) * LANES
+            w3_ref[:, at : at + LANES] = jnp.concatenate([high, low16], axis=0).astype(BF16)
 
 
 def body(samples_in, block_order, seam_link, w_in, w_mid, w_feat, w_density, w_conv, w_color):
@@ -412,19 +483,11 @@
         swap_far += [(i, i + 1), (i + 1, i)]
     far = lax.ppermute(far, "patch", swap_far)
     near = lax.ppermute(near, "patch", swap_near)
-    from_left = jnp.where(odd, near, far)
-    from_right = jnp.where(odd, far, near)
     edges = blk_dev * rows_all * EDGE
-    halo = jnp.concatenate(
-        [
-            from_left[:edges].reshape(blk_dev, rows_all, EDGE, width),
-            from_right[:edges].reshape(blk_dev, rows_all, EDGE, width),
-        ],
-        axis=2,
-    )
-    halo = jnp.pad(halo, ((0, 0), (EDGE, EDGE), (0, 0), (0, 0))).reshape(blk_dev, hrays, width)
-    order_l = from_left[edges, : nb + 1].astype(jnp.int32)
-    order_r = from_right[edges, : nb + 1].astype(jnp.int32)
+    from_left = jnp.where(odd, near[edges], far[edges])
+    from_right = jnp.where(odd, far[edges], near[edges])
+    order_l = from_left[: nb + 1].astype(jnp.int32)
+    order_r = from_right[: nb + 1].astype(jnp.int32)
     flags = jnp.stack(
         [
             place,
@@ -439,33 +502,36 @@
     ).astype(jnp.int32)
     info = jnp.concatenate([flags, block_order[0], order_l[:nb], order_r[:nb]])
 
-    heads = []
-    for b in range(blk_dev):
-        dens = jnp.broadcast_to(w_density[b][:, None], (w_density.shape[1], feat))
-        blank = jnp.zeros_like(dens)
-        parts = [blank] * (2 * blk_dev)
-        parts[b] = w_feat[b]
-        parts[blk_dev + b] = dens
-        heads.append(jnp.concatenate(parts, axis=1))
-    whead = jnp.stack(heads)
-
     size = n_own + n_halo + n_dep + n_tail
+    params = pltpu.CompilerParams(vmem_limit_bytes=32 * 1024 * 1024)
     smem = pl.BlockSpec(memory_space=pltpu.SMEM)
     vmem = pl.BlockSpec(memory_space=pltpu.VMEM)
     bufs = pl.pallas_call(
         functools.partial(field_kernel, cfg),
-        out_shape=[jax.ShapeDtypeStruct((size, LANES), BF16)] * groups,
-        in_specs=[smem] + [vmem] * 5,
+        out_shape=[pltpu.VMEM((size, LANES), BF16)] * groups,
+        in_specs=[smem] + [vmem] * 7,
         out_specs=[vmem] * groups,
         scratch_shapes=[
             pltpu.VMEM((count + 2 * EDGE * cols, LANES), BF16),
-            pltpu.VMEM((hrays, LANES), BF16),
+            pltpu.VMEM((hrays, LANES), F32),
             pltpu.VMEM((4 * (count + 2 * EDGE * cols) // LANES, LANES), F32),
             pltpu.VMEM((n_tail, LANES), F32),
             pltpu.VMEM((blk_dev, width, w_in.shape[2]), BF16),
+            pltpu.VMEM((blk_dev, w_feat.shape[1], 2 * LANES), BF16),
+            pltpu.VMEM((blk_dev, hrays, width), F32),
         ],
+        compiler_params=params,
         name="field",
-    )(jnp.reshape(place, (1,)), samples_in.reshape(blk_dev, count, width), halo, w_in, w_mid, whead)
+    )(
+        jnp.stack([place, patch & 1]),
+        samples_in.reshape(blk_dev, count, width),
+        near,
+        far,
+        w_in,
+        w_mid,
+        w_feat,
+        w_density,
+    )
 
     got = [bufs[0]]
     for s in range(1, groups):
@@ -475,7 +541,20 @@
             route = [(i, (i + s) % groups) for i in range(groups)]
         got.append(lax.ppermute(bufs[s], "block", route))
 
-    w0, w1, w2, w3 = decoder_weights(w_conv, w_color)
+    w0, w1, w2, w3 = pl.pallas_call(
+        weights_kernel,
+        out_shape=[
+            pltpu.VMEM((4 * feat, 12 * feat), BF16),
+            pltpu.VMEM((4 * feat, 24 * feat), BF16),
+            pltpu.VMEM((2, 4 * feat, 12 * feat), BF16),
+            pltpu.VMEM((2 * feat, 48 * feat), BF16),
+        ],
+        in_specs=[vmem, vmem, pl.BlockSpec(memory_space=pl.ANY)],
+        out_specs=[vmem] * 4,
+        compiler_params=params,
+        cost_estimate=pl.CostEstimate(flops=10**8, bytes_accessed=10**6, transcendentals=0),
+        name="weights",
+    )(w_conv.reshape(-1, feat), w_color, bufs[0])
     pitch = cfg["pitch"]
     rows_in, rows_mid = rows_dev + 2 * EDGE, rows_dev + 2
     return pl.pallas_call(
@@ -492,6 +571,7 @@
             pltpu.VMEM((hchunks * LANES, groups * LANES), F32),
             pltpu.SMEM((nb,), jnp.int32),
         ],
+        compiler_params=params,
         name="decoder",
     )(info, w0, w1, w2, w3, *got)
 

time: 52.2 us -> 37.5 us (0.72)
  the two profiles are of different devices: /device:TPU:7 before, /device:TPU:17 now
where the time goes in v2:
time: 37.5 us; the launch traced here: 37.1 us
  Pallas kernels  14.3 us (38%)
  waiting for transfers between devices  8.19 us (22%)
  starting transfers between devices  7.19 us (19%)
  local copies, waits for them, and re-layouts  4.89 us (13%)
  between operations  1.41 us (4%)
  other arithmetic  1.1 us (3%)
    pallas_call x1, Pallas kernels, body(): pl.pallas_call(functools.partial(field_kernel, cfg), out_shape=[pltpu.VME...  7.97 us
    pallas_call x1, Pallas kernels, body(): pl.pallas_call(functools.partial(decoder_kernel, cfg), out_shape=jax.Shap...  5.84 us
    ppermute x3, waiting for transfers between devices, body(): got.append(lax.ppermute(bufs[s], 'block', route))  5.05 us
    unnamed x17, local copies, waits for them, and re-layouts  4.21 us
    ppermute x3, starting transfers between devices, body(): got.append(lax.ppermute(bufs[s], 'block', route))  3.88 us
    ppermute x1, waiting for transfers between devices, body(): far = lax.ppermute(far, 'patch', swap_far)  3.14 us
    ppermute x1, starting transfers between devices, body(): far = lax.ppermute(far, 'patch', swap_far)  2.04 us
    ppermute x1, starting transfers between devices, body(): near = lax.ppermute(near, 'patch', swap_near)  1.28 us
  transfers between devices with their start and end apart: 5, of which 3 were waited for; matrix products, arithmetic and copies ran while one was open for 1% of the time, Pallas kernels for 1%

profile of v2, /device:TPU:17, one launch (start us, length us, event | category | flops | bytes accessed | tf_op | source)
XLA Modules:
  0.0 37.1 jit_solution(11631371520081032557)
XLA Ops:
  0.7 0.0 copy-start.7
  0.7 0.6 %copy-done.7 = s32[1,8]{1,0:T(1,128)S(1)} copy-done((s32[1,8]{1,0:T(1,128)S(1)}, s32[1,8]{1,0:T(1,128)}, u32[]{:S(2)}) %copy-start.7) | copy-done | bytes 56
  1.3 0.1 fusion.5
  1.4 0.9 %broadcast_select_fusion.1 = (bf16[2,16,2,128]{3,2,1,0:T(2,128)(2,1)S(1)}, bf16[2,16,2,128]{3,2,1,0:T(2,128)(2,1)S(1)}) fusion(pred[]{:T(512)S(6)} %eq.3, bf16[2,16,64,128]{3,2,1,0:T(8,128)(2,1)} %param.9), kind=kLoop, calls=%fused_computation.1 | loop fusion | flops 16384 | bytes 65537 | tf_op jit(solution)/shard_map/jit(_where)/select_n | solution.py:478
  2.3 0.0 copy-start.6
  2.3 1.3 %collective-permute-start = (bf16[80,128]{1,0:T(8,128)(2,1)S(1)}, bf16[80,128]{1,0:T(8,128)(2,1)S(1)}, u32[]{:S(2)}, u32[]{:S(2)}) collective-permute-start(bf16[80,128]{1,0:T(8,128)(2,1)S(1)} %get-tuple-element.25), channel_id=1, source_target_pairs={{0,1},{1,0},{2,3},{3,2},{4,5},{5,4},{6,7},{7,6},{8,9},{9,8},{10,11... | collective-permute-start | bytes 61448 | tf_op jit(solution)/shard_map/ppermute | solution.py:485
  3.6 2.0 %collective-permute-start.1 = (bf16[80,128]{1,0:T(8,128)(2,1)S(1)}, bf16[80,128]{1,0:T(8,128)(2,1)S(1)}, u32[]{:S(2)}, u32[]{:S(2)}) collective-permute-start(bf16[80,128]{1,0:T(8,128)(2,1)S(1)} %get-tuple-element.26), channel_id=1, source_target_pairs={{1,2},{2,1},{3,4},{4,3},{5,6},{6,5},{9,10},{10,9},{11,12},{12,11},... | collective-permute-start | bytes 61448 | tf_op jit(solution)/shard_map/ppermute | solution.py:484
  5.7 0.1 pad_add_fusion.at_ref
  5.7 0.0 copy-done.6
  5.7 0.0 copy-start.3
  5.7 0.1 copy.10.wf_ref
  5.9 0.0 collective-permute-done.near_ref
  5.9 3.1 %collective-permute-done.1.far_ref = bf16[80,128]{1,0:T(8,128)(2,1)S(1)} collective-permute-done((bf16[80,128]{1,0:T(8,128)(2,1)S(1)}, bf16[80,128]{1,0:T(8,128)(2,1)S(1)}, u32[]{:S(2)}, u32[]{:S(2)}) %collective-permute-start.1) | collective-permute-done | bytes 20512 | tf_op jit(solution)/shard_map/ppermute | solution.py:484
  9.0 0.6 %slice.45 = s32[1,1]{1,0:T(1,128)} slice(s32[1,9]{1,0:T(1,128)S(1)} %slice_convert_fusion), slice={[0:1], [8:9]} | slice | bytes 8 | tf_op jit(solution)/shard_map/slice | solution.py:494
  9.6 0.0 copy-start.5
  9.6 0.0 copy-done.3
  9.6 0.7 %copy-done.5 = bf16[2,256]{1,0:T(2,128)(2,1)S(1)} copy-done((bf16[2,256]{1,0:T(2,128)(2,1)S(1)}, bf16[2,256]{1,0:T(2,128)(2,1)}, u32[]{:S(2)}) %copy-start.5) | copy-done | bytes 1048
  10.3 1.0 %copy-done = bf16[2,16,64,128]{3,2,1,0:T(8,128)(2,1)S(1)} copy-done((bf16[2,16,64,128]{3,2,1,0:T(8,128)(2,1)S(1)}, bf16[2,16,64,128]{3,2,1,0:T(8,128)(2,1)}, u32[]{:S(2)}) %copy-start) | copy-done | bytes 524312
  11.4 1.0 %copy-done.2 = bf16[2,2,256,256]{3,2,1,0:T(8,128)(2,1)S(1)} copy-done((bf16[2,2,256,256]{3,2,1,0:T(8,128)(2,1)S(1)}, bf16[2,2,256,256]{3,2,1,0:T(8,128)(2,1)}, u32[]{:S(2)}) %copy-start.2) | copy-done | bytes 524312
  12.4 8.0 %field.1 = (bf16[576,128]{1,0:T(8,128)(2,1)S(1)}, bf16[576,128]{1,0:T(8,128)(2,1)S(1)}, bf16[576,128]{1,0:T(8,128)(2,1)S(1)}, bf16[576,128]{1,0:T(8,128)(2,1)S(1)}) custom-call(s32[2]{0:T(128)S(1)} %pad_add_fusion.at_ref, bf16[2,1024,128]{2,1,0:T(8,128)(2,1)S(1)} %bitcast.20, bf16[80,128]{1,0:T(8,128)(2,1)S(1)} %collective-permute-done.near_ref, ...), custom_call_target="tpu_custom_call" | custom-call | tf_op jit(solution)/shard_map/field/pallas_call | solution.py:509
  20.4 2.2 %collective-permute-start.2 = (bf16[576,128]{1,0:T(8,128)(2,1)S(1)}, bf16[576,128]{1,0:T(8,128)(2,1)S(1)}, u32[]{:S(2)}, u32[]{:S(2)}) collective-permute-start(bf16[576,128]{1,0:T(8,128)(2,1)S(1)} %get-tuple-element.18), channel_id=1, source_target_pairs={{0,8},{8,0},{16,24},{24,16},{1,9},{9,1},{17,25},{25,17},{2,10},{10... | collective-permute-start | bytes 442376 | tf_op jit(solution)/shard_map/ppermute | solution.py:542
  22.6 1.2 %collective-permute-start.3 = (bf16[576,128]{1,0:T(8,128)(2,1)S(1)}, bf16[576,128]{1,0:T(8,128)(2,1)S(1)}, u32[]{:S(2)}, u32[]{:S(2)}) collective-permute-start(bf16[576,128]{1,0:T(8,128)(2,1)S(1)} %get-tuple-element.19), channel_id=1, source_target_pairs={{0,16},{8,24},{16,0},{24,8},{1,17},{9,25},{17,1},{25,9},{2,18},{10... | collective-permute-start | bytes 442376 | tf_op jit(solution)/shard_map/ppermute | solution.py:542
  23.8 0.5 %collective-permute-start.4 = (bf16[576,128]{1,0:T(8,128)(2,1)S(1)}, bf16[576,128]{1,0:T(8,128)(2,1)S(1)}, u32[]{:S(2)}, u32[]{:S(2)}) collective-permute-start(bf16[576,128]{1,0:T(8,128)(2,1)S(1)} %get-tuple-element.20), channel_id=1, source_target_pairs={{0,24},{8,16},{16,8},{24,0},{1,25},{9,17},{17,9},{25,1},{2,26},{10... | collective-permute-start | bytes 442376 | tf_op jit(solution)/shard_map/ppermute | solution.py:542
  24.9 0.1 concatenate.26.info_ref
  25.0 0.0 copy-start.4
  25.0 0.0 copy-done.1
  25.0 0.7 %copy-done.4 = bf16[3,64]{1,0:T(4,128)(2,1)S(1)} copy-done((bf16[3,64]{1,0:T(4,128)(2,1)S(1)}, bf16[3,64]{1,0:T(4,128)(2,1)}, u32[]{:S(2)}) %copy-start.4) | copy-done | bytes 408
  25.7 0.5 %weights.1 = (bf16[256,768]{1,0:T(8,128)(2,1)S(1)}, bf16[256,1536]{1,0:T(8,128)(2,1)S(1)}, bf16[2,256,768]{2,1,0:T(8,128)(2,1)S(1)}, bf16[128,3072]{1,0:T(8,128)(2,1)S(1)}) custom-call(bf16[2304,64]{1,0:T(8,128)(2,1)S(1)} %bitcast.21, bf16[3,64]{1,0:T(4,128)(2,1)S(1)} %copy-done.4, bf16[576,128]{1,0:T(8,128)(2,1)S(1)} %get-tuple-element.13.after_ref.rest_0_), custom_call_target="tpu_custom_call" | custom-call | flops 100000000 | bytes 1000000 | tf_op jit(solution)/shard_map/weights/pallas_call | solution.py:544
  26.2 0.0 collective-permute-done.2.rest_1_
  26.2 1.6 %collective-permute-done.3.rest_2_ = bf16[576,128]{1,0:T(8,128)(2,1)S(1)} collective-permute-done((bf16[576,128]{1,0:T(8,128)(2,1)S(1)}, bf16[576,128]{1,0:T(8,128)(2,1)S(1)}, u32[]{:S(2)}, u32[]{:S(2)}) %collective-permute-start.3) | collective-permute-done | bytes 147488 | tf_op jit(solution)/shard_map/ppermute | solution.py:542
  27.9 3.4 %collective-permute-done.4.rest_3_ = bf16[576,128]{1,0:T(8,128)(2,1)S(1)} collective-permute-done((bf16[576,128]{1,0:T(8,128)(2,1)S(1)}, bf16[576,128]{1,0:T(8,128)(2,1)S(1)}, u32[]{:S(2)}, u32[]{:S(2)}) %collective-permute-start.4) | collective-permute-done | bytes 147488 | tf_op jit(solution)/shard_map/ppermute | solution.py:542
  31.3 5.8 %decoder.1 = f32[3,16,256]{2,1,0:T(8,128)} custom-call(s32[32]{0:T(128)S(1)} %concatenate.26.info_ref, bf16[256,768]{1,0:T(8,128)(2,1)S(1)} %get-tuple-element.14.w0_ref, bf16[256,1536]{1,0:T(8,128)(2,1)S(1)} %get-tuple-element.15.w1_ref, bf16[2,256,768]{2,1,0:T(8,128)(2,1)S(1)} %get-tuple-element.16.w2_ref, bf16[128,3072]{1,0:T(8,128)(2,1)S(1)} %get-tuple-element.17.w3_ref, ...), custom_call_target="tpu_custom_call" | custom-call | tf_op jit(solution)/shard_map/decoder/pallas_call | solution.py:560
  (10 shorter events, 0.0 us)
Async XLA Ops:
  0.7 0.7 %copy-start.7 = (s32[1,8]{1,0:T(1,128)S(1)}, s32[1,8]{1,0:T(1,128)}, u32[]{:S(2)}) copy-start(s32[1,8]{1,0:T(1,128)} %param.10) | copy-start | bytes 100
  2.3 3.4 %copy-start.6 = (bf16[2,256,64]{1,2,0:T(8,128)(2,1)S(1)}, bf16[2,256,64]{1,2,0:T(8,128)(2,1)}, u32[]{:S(2)}) copy-start(bf16[2,256,64]{1,2,0:T(8,128)(2,1)} %param.14) | copy-start | bytes 196612
  2.3 3.5 %collective-permute-start = (bf16[80,128]{1,0:T(8,128)(2,1)S(1)}, bf16[80,128]{1,0:T(8,128)(2,1)S(1)}, u32[]{:S(2)}, u32[]{:S(2)}) collective-permute-start(bf16[80,128]{1,0:T(8,128)(2,1)S(1)} %get-tuple-element.25), channel_id=1, source_target_pairs={{0,1},{1,0},{2,3},{3,2},{4,5},{5,4},{6,7},{7,6},{8,9},{9,8},{10,11... | collective-permute-start | bytes 61448 | tf_op jit(solution)/shard_map/ppermute | solution.py:485
  3.6 5.4 %collective-permute-start.1 = (bf16[80,128]{1,0:T(8,128)(2,1)S(1)}, bf16[80,128]{1,0:T(8,128)(2,1)S(1)}, u32[]{:S(2)}, u32[]{:S(2)}) collective-permute-start(bf16[80,128]{1,0:T(8,128)(2,1)S(1)} %get-tuple-element.26), channel_id=1, source_target_pairs={{1,2},{2,1},{3,4},{4,3},{5,6},{6,5},{9,10},{10,9},{11,12},{12,11},... | collective-permute-start | bytes 61448 | tf_op jit(solution)/shard_map/ppermute | solution.py:484
  5.7 3.9 %copy-start.3 = (bf16[2,32,256]{2,1,0:T(8,128)(2,1)S(1)}, bf16[2,32,256]{2,1,0:T(8,128)(2,1)}, u32[]{:S(2)}) copy-start(bf16[2,32,256]{2,1,0:T(8,128)(2,1)} %win_ref.1) | copy-start | bytes 98308
  9.6 0.7 %copy-start.5 = (bf16[2,256]{1,0:T(2,128)(2,1)S(1)}, bf16[2,256]{1,0:T(2,128)(2,1)}, u32[]{:S(2)}) copy-start(bf16[2,256]{1,0:T(2,128)(2,1)} %wd_ref.1) | copy-start | bytes 3076
  10.3 1.0 %copy-start = (bf16[2,16,64,128]{3,2,1,0:T(8,128)(2,1)S(1)}, bf16[2,16,64,128]{3,2,1,0:T(8,128)(2,1)}, u32[]{:S(2)}) copy-start(bf16[2,16,64,128]{3,2,1,0:T(8,128)(2,1)} %param.9) | copy-start | bytes 1572868
  11.4 1.0 %copy-start.2 = (bf16[2,2,256,256]{3,2,1,0:T(8,128)(2,1)S(1)}, bf16[2,2,256,256]{3,2,1,0:T(8,128)(2,1)}, u32[]{:S(2)}) copy-start(bf16[2,2,256,256]{3,2,1,0:T(8,128)(2,1)} %wmid_ref.1) | copy-start | bytes 1572868
  12.4 12.6 %copy-start.1 = (bf16[4,3,3,64,64]{4,3,2,1,0:T(8,128)(2,1)S(1)}, bf16[4,3,3,64,64]{4,3,2,1,0:T(8,128)(2,1)}, u32[]{:S(2)}) copy-start(bf16[4,3,3,64,64]{4,3,2,1,0:T(8,128)(2,1)} %param.16) | copy-start | bytes 884740
  20.4 5.9 %collective-permute-start.2 = (bf16[576,128]{1,0:T(8,128)(2,1)S(1)}, bf16[576,128]{1,0:T(8,128)(2,1)S(1)}, u32[]{:S(2)}, u32[]{:S(2)}) collective-permute-start(bf16[576,128]{1,0:T(8,128)(2,1)S(1)} %get-tuple-element.18), channel_id=1, source_target_pairs={{0,8},{8,0},{16,24},{24,16},{1,9},{9,1},{17,25},{25,17},{2,10},{10... | collective-permute-start | bytes 442376 | tf_op jit(solution)/shard_map/ppermute | solution.py:542
  22.6 5.3 %collective-permute-start.3 = (bf16[576,128]{1,0:T(8,128)(2,1)S(1)}, bf16[576,128]{1,0:T(8,128)(2,1)S(1)}, u32[]{:S(2)}, u32[]{:S(2)}) collective-permute-start(bf16[576,128]{1,0:T(8,128)(2,1)S(1)} %get-tuple-element.19), channel_id=1, source_target_pairs={{0,16},{8,24},{16,0},{24,8},{1,17},{9,25},{17,1},{25,9},{2,18},{10... | collective-permute-start | bytes 442376 | tf_op jit(solution)/shard_map/ppermute | solution.py:542
  23.8 7.5 %collective-permute-start.4 = (bf16[576,128]{1,0:T(8,128)(2,1)S(1)}, bf16[576,128]{1,0:T(8,128)(2,1)S(1)}, u32[]{:S(2)}, u32[]{:S(2)}) collective-permute-start(bf16[576,128]{1,0:T(8,128)(2,1)S(1)} %get-tuple-element.20), channel_id=1, source_target_pairs={{0,24},{8,16},{16,8},{24,0},{1,25},{9,17},{17,9},{25,1},{2,26},{10... | collective-permute-start | bytes 442376 | tf_op jit(solution)/shard_map/ppermute | solution.py:542
  25.0 0.7 %copy-start.4 = (bf16[3,64]{1,0:T(4,128)(2,1)S(1)}, bf16[3,64]{1,0:T(4,128)(2,1)}, u32[]{:S(2)}) copy-start(bf16[3,64]{1,0:T(4,128)(2,1)} %colour_ref.1) | copy-start | bytes 1156

commit v3 on v2

--- a/solution.py
+++ b/solution.py
@@ -7,6 +7,7 @@
 from jax.experimental.pallas import tpu as pltpu
 from jax.sharding import PartitionSpec as P
 
+
 STEP = 0.03
 LANES = 128
 EDGE = 2
@@ -24,7 +25,7 @@
 
 
 def relu16(x):
-    return jnp.maximum(x, 0.0).astype(BF16)
+    return jnp.maximum(x.astype(BF16), jnp.zeros((), BF16))
 
 
 def softplus(v):
@@ -33,129 +34,277 @@
     return jnp.maximum(v, 0.0) + tail
 
 
-def fade(optical):
-    through = jnp.exp(-optical)
+def stopped(optical):
     small = optical * (1.0 - optical * (0.5 - optical * (1.0 / 6.0 - optical * (1.0 / 24.0))))
-    return through, jnp.where(optical < 0.0625, small, 1.0 - through)
-
-
-def field_rays(xs, win, wmid, whead, samples, enc):
+    return jnp.where(optical < 0.0625, small, 1.0 - jnp.exp(-optical))
+
+
+def split16(x):
+    high = x.astype(BF16).astype(F32)
+    return high, x - high
+
+
+def one_hot(shape, test):
+    r = lax.broadcasted_iota(jnp.int32, shape, 0)
+    c = lax.broadcasted_iota(jnp.int32, shape, 1)
+    return jnp.where(test(r, c), 1.0, 0.0).astype(BF16)
+
+
+def field_heads(xs, tiled, wmid, whead, spread, samples, enc):
     rays = xs[0].shape[0]
     lane = lax.broadcasted_iota(jnp.int32, xs[0].shape, 1)
-    total = None
+    heads = [None] * samples
     for b, x in enumerate(xs):
         zero = jnp.zeros_like(x)
         parts = [
             jnp.where((lane >= s * enc) & (lane < (s + 1) * enc), x, zero) for s in range(samples)
         ]
-        hidden = relu16(dot(jnp.concatenate(parts, axis=0), win[b]))
+        hidden = relu16(dot(jnp.concatenate(parts, axis=0), tiled[b]))
         hidden = relu16(dot(hidden, wmid[b, 0]))
         hidden = relu16(dot(hidden, wmid[b, 1]))
-        head = dot(hidden, whead[b])
-        total = head if total is None else total + head
-    left = jnp.ones((rays, LANES), F32)
-    colour = jnp.zeros((rays, LANES), F32)
-    depth = jnp.zeros((rays, LANES), F32)
+        for s in range(samples):
+            made = dot(hidden[s * rays : (s + 1) * rays], whead[b, s])
+            heads[s] = made if b == 0 else heads[s] + made
+    return heads
+
+
+def field_mix(heads, spread):
+    samples, rays = len(heads), heads[0].shape[0]
+    logit = heads[0][:, LANES:]
+    for s in range(1, samples):
+        logit = logit + heads[s][:, LANES:]
+    optical = STEP * softplus(logit)
+    group = LANES // samples
+    lane = lax.broadcasted_iota(jnp.int32, (rays, LANES), 1)
+    depth, before = optical, jnp.zeros((rays, LANES), F32)
+    for s in range(1, samples):
+        moved = pltpu.roll(optical, s * group, 1)
+        depth = depth + moved
+        before = before + jnp.where(lane >= s * group, moved, 0.0)
+    weight = jnp.exp(-before) * stopped(optical)
+    high, low = split16(weight)
+    wide = dot(jnp.concatenate([high.astype(BF16), low.astype(BF16)], axis=1), spread[...])
+    colour = None
     for s in range(samples):
-        own = total[s * rays : (s + 1) * rays]
-        optical = STEP * softplus(own[:, LANES:])
-        through, stop = fade(optical)
-        colour = colour + (left * stop) * own[:, :LANES]
-        left = left * through
-        depth = depth + optical
+        term = wide[:, s * LANES : (s + 1) * LANES] * heads[s][:, :LANES]
+        colour = term if colour is None else colour + term
     return colour, depth
 
 
-def split16(x):
-    high = x.astype(BF16).astype(F32)
-    return high, x - high
-
-
-def depth_rows(depth):
+def depth_rows(depth, step):
     turned = depth.T
-    pair = jnp.concatenate([turned[0:1], turned[LANES // 2 : LANES // 2 + 1]], axis=0)
+    pair = jnp.concatenate([turned[0:1], turned[step : step + 1]], axis=0)
     high, low = split16(pair)
     return jnp.concatenate([high, low], axis=0)
 
 
-def field_kernel(cfg, at_ref, own_ref, near_ref, far_ref, win_ref, wmid_ref, wf_ref, wd_ref, *rest):
-    groups, samples, enc = cfg["groups"], cfg["samples"], cfg["enc"]
-    outs = rest[:groups]
-    col_own, col_halo, dep_own, dep_halo, tiled, whead_ref, halo_ref = rest[groups:]
-    cols, rows_all, rows_dev = cfg["cols"], cfg["rows_all"], cfg["rows_dev"]
+def edges_kernel(
+    cfg, at_ref, order_hbm, seam_hbm, own_hbm, win_hbm, wd_hbm,
+    own_ref, win_ref, wd_ref, near_ref, far_ref,
+    left, right, order_ref, seam_ref, sems,
+):
+    cols, rows_all = cfg["cols"], cfg["rows_all"]
     blocks = own_ref.shape[0]
-    pad = EDGE * cols
-    count = rows_all * cols
+    small = [
+        pltpu.make_async_copy(order_hbm, order_ref, sems.at[2]),
+        pltpu.make_async_copy(seam_hbm, seam_ref, sems.at[3]),
+    ]
+    for copy in small:
+        copy.start()
+    load = pltpu.make_async_copy(own_hbm, own_ref, sems.at[0])
+    load.start()
+    more = [
+        pltpu.make_async_copy(win_hbm, win_ref, sems.at[1]),
+        pltpu.make_async_copy(wd_hbm, wd_ref, sems.at[4]),
+    ]
+    for copy in more:
+        copy.start()
+    nb = cfg["nb"]
+    lane = lax.broadcasted_iota(jnp.int32, (16, LANES), 1)
+    for copy in small:
+        copy.wait()
+    meta = jnp.where(lane == nb, seam_ref[0], 0)
+    for k in range(nb):
+        meta = jnp.where(lane == k, order_ref[0, k], meta)
+    meta = meta.astype(F32).astype(BF16)
+    load.wait()
+    size = blocks * rows_all * EDGE
+    for b in range(blocks):
+        for r in range(rows_all):
+            q = (b * rows_all + r) * EDGE
+            left[q : q + EDGE, :] = own_ref[b, r * cols : r * cols + 16, :].astype(F32)[:EDGE]
+            last = own_ref[b, (r + 1) * cols - 16 : (r + 1) * cols, :].astype(F32)
+            right[q : q + EDGE, :] = last[16 - EDGE :]
+    odd = at_ref[1] == 1
+    near_ref[:size, :] = jnp.where(odd, left[...], right[...]).astype(BF16)
+    far_ref[:size, :] = jnp.where(odd, right[...], left[...]).astype(BF16)
+    near_ref[size:, :] = meta
+    far_ref[size:, :] = meta
+    for copy in more:
+        copy.wait()
+
+
+def field_chunks(cfg, own_ref, nets, col_own, dep_own, pieces):
+    pad = EDGE * cfg["cols"]
+    blocks = own_ref.shape[0]
+
+    def start(chunk):
+        xs = [
+            jnp.concatenate([own_ref[b, pl.ds(at, LANES), :] for at in chunk], axis=0)
+            for b in range(blocks)
+        ]
+        return field_heads(xs, *nets, cfg["samples"], cfg["enc"])
+
+    def finish(chunk, heads):
+        colour, depth = field_mix(heads, nets[3])
+        for k, at in enumerate(chunk):
+            rows = slice(k * LANES, (k + 1) * LANES)
+            col_own[pl.ds(pl.multiple_of(at + pad, LANES), LANES), :] = colour[rows].astype(BF16)
+            q = pl.multiple_of((at + pad) // LANES * 8, 8)
+            dep_own[pl.ds(q, 4), :] = depth_rows(depth[rows], cfg["repeat"])
+
+    waiting = None
+    for chunk in pieces:
+        heads = start(chunk)
+        if waiting is not None:
+            finish(*waiting)
+        waiting = (chunk, heads)
+    finish(*waiting)
+
+
+def grouped(items, n):
+    return [items[i : i + n] for i in range(0, len(items), n)]
+
+
+def row_pieces(cfg, place, near):
+    per = LANES // cfg["cols"]
+    chip = place >> 1
+    if cfg["groups"] == 4:
+        first = jnp.where(chip == 0, 0, cfg["rows_all"] - cfg["n_near"])
+    else:
+        first = chip * (2 * cfg["rows_dev"]) + EDGE
+    n = cfg["n_near"] if near else cfg["rows_all"] - cfg["n_near"]
+    first = first if near else first + cfg["n_near"]
+    starts = []
+    for k in range(n // per):
+        row = lax.rem(first + k * per, cfg["rows_all"])
+        starts.append(pl.multiple_of(row * cfg["cols"], LANES))
+    return starts
+
+
+def field_kernel(
+    cfg, at_ref, own_ref, win_ref, wmid_hbm, wf_ref, wd_ref,
+    col_own, dep_own, tiled, whead, spread, wmid_ref, sem,
+):
+    load = pltpu.make_async_copy(wmid_hbm, wmid_ref, sem)
+    load.start()
+    samples, enc = cfg["samples"], cfg["enc"]
+    blocks = own_ref.shape[0]
+    pad = EDGE * cfg["cols"]
+    count = cfg["rows_all"] * cfg["cols"]
     col_own[0:pad, :] = jnp.zeros((pad, LANES), BF16)
     col_own[pad + count :, :] = jnp.zeros((pad, LANES), BF16)
-    dep_own[...] = jnp.zeros(dep_own.shape, F32)
-    dep_halo[...] = jnp.zeros(dep_halo.shape, F32)
+    ends = 8 * pad // LANES
+    dep_own[0:ends, :] = jnp.zeros((ends, LANES), F32)
+    dep_own[dep_own.shape[0] - ends :, :] = jnp.zeros((ends, LANES), F32)
     for b in range(blocks):
         for s in range(samples):
             tiled[b, s * enc : (s + 1) * enc, :] = win_ref[b]
     feat, width = wf_ref.shape[2], wf_ref.shape[1]
+    repeat = cfg["repeat"]
     dens = wd_ref[...].astype(F32)
+    group = lax.broadcasted_iota(jnp.int32, (width, LANES), 1) // repeat
     for b in range(blocks):
-        r = lax.broadcasted_iota(jnp.int32, (feat, 2 * LANES), 0)
-        c = lax.broadcasted_iota(jnp.int32, (feat, 2 * LANES), 1)
-        lift = jnp.where(c - b * feat == r, 1.0, 0.0).astype(BF16)
+        lift = one_hot((feat, LANES), lambda r, c: c - b * feat == r)
         r = lax.broadcasted_iota(jnp.int32, (width, width), 0)
         c = lax.broadcasted_iota(jnp.int32, (width, width), 1)
         diag = jnp.where(r == c, dens[b : b + 1], 0.0).astype(BF16)
-        c = lax.broadcasted_iota(jnp.int32, (width, 2 * LANES), 1)
-        repeat = jnp.where((c - LANES) // feat == b, 1.0, 0.0).astype(BF16)
-        whead_ref[b] = (dot(wf_ref[b], lift) + dot(diag, repeat)).astype(BF16)
+        features = dot(wf_ref[b], lift).astype(BF16)
+        column = dot(diag, jnp.ones((width, LANES), BF16))
+        for s in range(samples):
+            whead[b, s, :, :LANES] = features
+            whead[b, s, :, LANES:] = jnp.where(group == s * blocks + b, column, 0.0).astype(BF16)
+    spread[...] = one_hot(
+        spread.shape, lambda r, c: (r & (LANES - 1)) == c // (LANES // blocks) * repeat
+    )
+    load.wait()
+    nets = (tiled, wmid_ref, whead, spread)
+    pieces = row_pieces(cfg, at_ref[0], False)
+    field_chunks(cfg, own_ref, nets, col_own, dep_own, grouped(pieces, cfg["chunk"]))
+
+
+def pack(cfg, place, s, out, col_own, dep_own, col_halo, dep_halo):
+    n_own, n_halo, n_dep = cfg["n_own"], cfg["n_halo"], cfg["n_dep"]
+    cols, rows_dev = cfg["cols"], cfg["rows_dev"]
+    half = n_halo // 2
+    dest = place ^ s
+    start = pl.multiple_of(dest * (rows_dev * cols), LANES)
+    out[0:n_own, :] = col_own[pl.ds(start, n_own), :]
+    for i in range(2):
+        start = pl.multiple_of(i * cfg["side_pitch"] + dest * (rows_dev * EDGE), 8)
+        q = n_own + i * half
+        out[q : q + half, :] = col_halo[pl.ds(start, half), :].astype(BF16)
+    start = pl.multiple_of(dest * (8 * rows_dev * cols // LANES), 8)
+    at = n_own + n_halo
+    groups = n_dep // 4
+    rows = dep_own[pl.ds(start, 8 * groups), :]
+    rows = jnp.concatenate([rows[8 * k : 8 * k + 4] for k in range(groups)], axis=0)
+    out[at : at + n_dep, :] = rows.astype(BF16)
+    out[at + n_dep :, :] = dep_halo[...].astype(BF16)
+
+
+def halo_kernel(
+    cfg, at_ref, near_ref, far_ref, tiled, wmid_ref, whead, spread, col_own, dep_own, *rest
+):
+    outs = rest[: cfg["groups"] - 2]
+    col_halo, dep_halo, meta, halo_ref = rest[cfg["groups"] - 2 :]
+    samples, enc, rows_all = cfg["samples"], cfg["enc"], cfg["rows_all"]
+    blocks = halo_ref.shape[0]
     odd = at_ref[1] == 1
     near, far = near_ref[...].astype(F32), far_ref[...].astype(F32)
     sides = [jnp.where(odd, near, far), jnp.where(odd, far, near)]
     side_rays = rows_all * EDGE
-    side_pitch = side_rays + 2 * EDGE * EDGE
     halo_ref[...] = jnp.zeros(halo_ref.shape, F32)
     for b in range(blocks):
         for i, side in enumerate(sides):
-            q = i * side_pitch + EDGE * EDGE
+            q = i * cfg["side_pitch"] + EDGE * EDGE
             halo_ref[b, q : q + side_rays, :] = side[b * side_rays : (b + 1) * side_rays]
-    step = cfg["chunk"]
-    for first in range(0, count, step):
-        xs = [own_ref[b, first : first + step, :] for b in range(blocks)]
-        colour, depth = field_rays(xs, tiled, wmid_ref, whead_ref, samples, enc)
-        col_own[pad + first : pad + first + step, :] = colour.astype(BF16)
-        for k in range(step // LANES):
-            at = 4 * ((pad + first) // LANES + k)
-            dep_own[at : at + 4, :] = depth_rows(depth[k * LANES : (k + 1) * LANES])
+    for i, side in enumerate(sides):
+        meta[8 * i : 8 * i + 8, :] = side[blocks * side_rays : blocks * side_rays + 8]
     xs = [halo_ref[b].astype(BF16) for b in range(blocks)]
-    colour, depth = field_rays(xs, tiled, wmid_ref, whead_ref, samples, enc)
+    heads = field_heads(xs, tiled, wmid_ref, whead, spread, samples, enc)
+    colour, depth = field_mix(heads, spread)
     col_halo[...] = colour
+    dep_halo[...] = jnp.zeros(dep_halo.shape, F32)
     hrays = depth.shape[0]
     for k in range(cfg["hchunks"]):
         part = depth[k * LANES : min((k + 1) * LANES, hrays)]
         if part.shape[0] < LANES:
             part = jnp.concatenate([part, jnp.zeros((LANES - part.shape[0], LANES), F32)], axis=0)
-        dep_halo[4 * k : 4 * k + 4, :] = depth_rows(part)
-    n_own, n_halo, n_dep = cfg["n_own"], cfg["n_halo"], cfg["n_dep"]
-    place = at_ref[0]
-    half = n_halo // 2
-    for s in range(groups):
-        dest = cfg["dest"](place, s)
-        out = outs[s]
-        start = pl.multiple_of(dest * (rows_dev * cols), LANES)
-        out[0:n_own, :] = col_own[pl.ds(start, n_own), :]
-        for i in range(2):
-            start = pl.multiple_of(i * side_pitch + dest * (rows_dev * EDGE), 8)
-            q = n_own + i * half
-            out[q : q + half, :] = col_halo[pl.ds(start, half), :].astype(BF16)
-        start = pl.multiple_of(dest * (4 * rows_dev * cols // LANES), 8)
-        at = n_own + n_halo
-        out[at : at + n_dep, :] = dep_own[pl.ds(start, n_dep), :].astype(BF16)
-        out[at + n_dep :, :] = dep_halo[...].astype(BF16)
+        dep_halo[4 * k : 4 * k + 4, :] = depth_rows(part, cfg["repeat"])
+    for s in range(2, cfg["groups"]):
+        pack(cfg, at_ref[0], s, outs[s - 2], col_own, dep_own, col_halo, dep_halo)
+
+
+def near_kernel(
+    cfg, at_ref, own_ref, tiled, wmid_ref, whead, spread, col_in, dep_in, col_halo, dep_halo,
+    meta_in, out_own, out_mate, meta, col_own, dep_own,
+):
+    meta[...] = meta_in[...]
+    col_own[...] = col_in[...]
+    dep_own[...] = dep_in[...]
+    nets = (tiled, wmid_ref, whead, spread)
+    pieces = row_pieces(cfg, at_ref[0], True)
+    field_chunks(cfg, own_ref, nets, col_own, dep_own, grouped(pieces, cfg["chunk"]))
+    pack(cfg, at_ref[0], 0, out_own, col_own, dep_own, col_halo, dep_halo)
+    pack(cfg, at_ref[0], 1, out_mate, col_own, dep_own, col_halo, dep_halo)
 
 
 def decoder_kernel(cfg, info_ref, w0_ref, w1_ref, w2_ref, w3_ref, *rest):
     groups, nb = cfg["groups"], cfg["nb"]
     bufs = rest[:groups]
     out_ref = rest[groups]
-    comp, x0, sa, xa, xc, rep = rest[groups + 1 : groups + 7]
-    rank_ref = rest[groups + 7]
+    comp, x0, sa, xa, sc, xc, rep, rank_ref = rest[groups + 1 :]
     cols, rows_dev, pitch = cfg["cols"], cfg["rows_dev"], cfg["pitch"]
     n_own, n_halo, n_dep = cfg["n_own"], cfg["n_halo"], cfg["n_dep"]
     rows_in = rows_dev + 2 * EDGE
@@ -177,7 +326,7 @@
         lane = lax.broadcasted_iota(jnp.int32, (nb, wide), 1)
         sub = lax.broadcasted_iota(jnp.int32, (nb, wide), 0)
         for s in range(groups):
-            source = cfg["source"](place, s)
+            source = place ^ s
             for i in range(per_dev):
                 rank = rank_ref[source * per_dev + i]
                 at = s * 2 * per_dev + i
@@ -253,14 +402,19 @@
     mask = jnp.where(pos < LEAD, left_open, jnp.where(pos >= LEAD + cols, right_open, 1.0))
     mask = mask * jnp.where(q < pitch, top_open, jnp.where(q >= mid - pitch, bottom_open, 1.0))
 
-    def windows(ref, pieces):
-        return jnp.concatenate(
-            [ref[r * pitch : r * pitch + n, a:b] for r, n, a, b in pieces], axis=1
-        )
+    def convolve(ref, pieces, n, weights):
+        made = []
+        for h in range(2):
+            lhs = jnp.concatenate(
+                [ref[r * pitch + h * n // 2 : r * pitch + (h + 1) * n // 2, a:b] for r, a, b in pieces],
+                axis=1,
+            )
+            made.append(dot_t(lhs, weights))
+        return jnp.concatenate(made, axis=0)
 
     wide = 2 * LANES
-    lhs = windows(x0, [(d, mid, 0, wide) for d in range(3)])
-    value = jnp.maximum(dot_t(lhs, w0_ref[...]), 0.0) * mask
+    value = convolve(x0, [(d, 0, wide) for d in range(3)], mid, w0_ref[...])
+    value = jnp.maximum(value, 0.0) * mask
 
     sa[0:8, :] = jnp.zeros((8, wide), F32)
     sa[8 + mid :, :] = jnp.zeros((8, wide), F32)
@@ -278,34 +432,34 @@
                 ].astype(BF16)
 
     lay_out(value)
-    lhs = windows(
-        xa, [(0, mid, three, 2 * three), (1, mid, 0, 2 * three), (2, mid, 0, three)]
-    )
-    value = jnp.maximum(dot_t(lhs, w1_ref[...]), 0.0) * mask
+    value = convolve(
+        xa, [(0, three, 2 * three), (1, 0, 2 * three), (2, 0, three)], mid, w1_ref[...]
+    )
+    value = jnp.maximum(value, 0.0) * mask
     lay_out(value)
     for pr in range(2):
         for pc in range(2):
             where = [(0, 1), (1, 0), (1, 1)] if pr == 0 else [(1, 0), (1, 1), (2, 0)]
-            lhs = windows(
-                xa,
-                [(d, mid, p * three + pc * LANES, p * three + pc * LANES + wide) for d, p in where],
+            at = [p * three + pc * LANES for _, p in where]
+            value = convolve(
+                xa, [(d, c, c + wide) for (d, _), c in zip(where, at)], mid, w2_ref[pc]
             )
-            value = jnp.maximum(dot_t(lhs, w2_ref[pc]), 0.0) * mask
-            sa[8 : 8 + mid, :] = value
+            value = jnp.maximum(value, 0.0) * mask
+            own = sc.at[2 * pr + pc]
+            own[8 : 8 + mid, :] = value
             for rr in range(2):
                 at = (2 * pr + rr) * 4 * LANES
                 tile = value[:, rr * LANES : (rr + 1) * LANES]
                 xc[:, at + (1 + pc) * LANES : at + (2 + pc) * LANES] = tile.astype(BF16)
                 slot, move = (3, 9) if pc == 0 else (0, 7)
-                xc[:, at + slot * LANES : at + (slot + 1) * LANES] = sa[
+                xc[:, at + slot * LANES : at + (slot + 1) * LANES] = own[
                     move : move + mid, rr * LANES : (rr + 1) * LANES
                 ].astype(BF16)
     n_out = rows_dev * pitch
     four = 4 * LANES
-    lhs = windows(
-        xc, [(0, n_out, 3 * four, 4 * four), (1, n_out, 0, 4 * four), (2, n_out, 0, four)]
-    )
-    final = dot_t(lhs, w3_ref[...])
+    final = convolve(
+        xc, [(0, 3 * four, 4 * four), (1, 0, 4 * four), (2, 0, four)], n_out, w3_ref[...]
+    )
     final = final + pltpu.roll(final, half, 1)
     rays = jnp.concatenate(
         [final[r * pitch + LEAD : r * pitch + LEAD + cols] for r in range(rows_dev)], axis=0
@@ -445,49 +599,141 @@
     feat = w_feat.shape[2]
     rows_dev = rows_all // groups
     count = rows_all * cols
-    power = groups & (groups - 1) == 0
     hrays = (rows_all + 2 * EDGE) * 2 * EDGE
     hchunks = -(-hrays // LANES)
     n_own = (rows_dev + 2 * EDGE) * cols
     n_halo = (rows_dev + 2 * EDGE) * 2 * EDGE
     n_dep = 4 * n_own // LANES
     n_tail = 16
+    samples = width // enc
     cfg = dict(
         groups=groups,
         nb=nb,
-        samples=width // enc,
+        samples=samples,
         enc=enc,
+        repeat=LANES // (samples * blk_dev),
         cols=cols,
         rows_all=rows_all,
         rows_dev=rows_dev,
+        n_near=2 * rows_dev - (EDGE if groups == 4 else 2 * EDGE),
+        side_pitch=hrays // 2,
         pitch=cols + 16,
-        chunk=2 * LANES,
+        chunk=2,
         n_own=n_own,
         n_halo=n_halo,
         n_dep=n_dep,
         hchunks=hchunks,
-        dest=(lambda p, s: p ^ s) if power else (lambda p, s: lax.rem(p + s, groups)),
-        source=(lambda p, s: p ^ s) if power else (lambda p, s: lax.rem(p + groups - s, groups)),
-    )
-
-    odd = (patch & 1) == 1
-    edge_l = samples_in[:, :, :EDGE].reshape(-1, width)
-    edge_r = samples_in[:, :, cols - EDGE :].reshape(-1, width)
-    meta = jnp.concatenate([block_order[0], seam_link]).astype(BF16)
-    meta = jnp.pad(meta[None, :], ((0, 15), (0, width - nb - 1)))
-    near = jnp.concatenate([jnp.where(odd, edge_l, edge_r), meta], axis=0)
-    far = jnp.concatenate([jnp.where(odd, edge_r, edge_l), meta], axis=0)
+    )
+    smem = pl.BlockSpec(memory_space=pltpu.SMEM)
+    vmem = pl.BlockSpec(memory_space=pltpu.VMEM)
+    hbm = pl.BlockSpec(memory_space=pltpu.HBM)
+    params = pltpu.CompilerParams(vmem_limit_bytes=24 * 1024 * 1024)
+    here = jnp.stack([place, patch & 1])
+
+    def far_off(x):
+        return pltpu.with_memory_space_constraint(x, pltpu.HBM)
+
+
+    edges = blk_dev * rows_all * EDGE
+    own, win, dens, near, far = pl.pallas_call(
+        functools.partial(edges_kernel, cfg),
+        out_shape=[
+            pltpu.VMEM((blk_dev, count, width), BF16),
+            pltpu.VMEM(w_in.shape, BF16),
+            pltpu.VMEM(w_density.shape, BF16),
+            pltpu.VMEM((edges + 16, width), BF16),
+            pltpu.VMEM((edges + 16, width), BF16),
+        ],
+        in_specs=[smem] + [hbm] * 5,
+        out_specs=[vmem] * 5,
+        scratch_shapes=[
+            pltpu.VMEM((edges, width), F32),
+            pltpu.VMEM((edges, width), F32),
+            pltpu.SMEM(block_order.shape, jnp.int32),
+            pltpu.SMEM(seam_link.shape, jnp.int32),
+            pltpu.SemaphoreType.DMA((5,)),
+        ],
+        compiler_params=params,
+        name="edges",
+    )(
+        here,
+        far_off(block_order),
+        seam_link,
+        far_off(samples_in.reshape(blk_dev, count, width)),
+        far_off(w_in),
+        far_off(w_density),
+    )
     swap_near = [(i, i ^ 1) for i in range(patches) if i ^ 1 < patches]
     swap_far = []
     for i in range(1, patches - 1, 2):
         swap_far += [(i, i + 1), (i + 1, i)]
     far = lax.ppermute(far, "patch", swap_far)
     near = lax.ppermute(near, "patch", swap_near)
-    edges = blk_dev * rows_all * EDGE
-    from_left = jnp.where(odd, near[edges], far[edges])
-    from_right = jnp.where(odd, far[edges], near[edges])
-    order_l = from_left[: nb + 1].astype(jnp.int32)
-    order_r = from_right[: nb + 1].astype(jnp.int32)
+
+    rays_flops = 2 * 2 * blk_dev * samples * w_mid.shape[2] * (3 * w_mid.shape[2])
+    far_rays = (rows_all - cfg["n_near"]) * cols
+    col_own, dep_own, tiled, whead, spread, wmid = pl.pallas_call(
+        functools.partial(field_kernel, cfg),
+        out_shape=[
+            pltpu.VMEM((count + 2 * EDGE * cols, LANES), BF16),
+            pltpu.VMEM((8 * (count + 2 * EDGE * cols) // LANES, LANES), F32),
+            pltpu.VMEM((blk_dev, width, w_in.shape[2]), BF16),
+            pltpu.VMEM((blk_dev, samples, w_feat.shape[1], 2 * LANES), BF16),
+            pltpu.VMEM((2 * LANES, samples * LANES), BF16),
+            pltpu.VMEM(w_mid.shape, BF16),
+        ],
+        in_specs=[smem, vmem, vmem, hbm, vmem, vmem],
+        out_specs=[vmem] * 6,
+        scratch_shapes=[pltpu.SemaphoreType.DMA],
+        compiler_params=params,
+        cost_estimate=pl.CostEstimate(
+            flops=far_rays * rays_flops, bytes_accessed=10**6, transcendentals=0
+        ),
+        name="field",
+    )(here, own, win, far_off(w_mid), w_feat, dens)
+
+    size = n_own + n_halo + n_dep + n_tail
+    shape = pltpu.VMEM((size, LANES), BF16)
+    *bufs, col_halo, dep_halo, meta = pl.pallas_call(
+        functools.partial(halo_kernel, cfg),
+        out_shape=[shape] * (groups - 2)
+        + [
+            pltpu.VMEM((hrays, LANES), F32),
+            pltpu.VMEM((n_tail, LANES), F32),
+            pltpu.VMEM((16, LANES), F32),
+        ],
+        in_specs=[smem] + [vmem] * 8,
+        out_specs=[vmem] * (groups + 1),
+        scratch_shapes=[pltpu.VMEM((blk_dev, hrays, width), F32)],
+        compiler_params=params,
+        name="halo",
+    )(here, near, far, tiled, wmid, whead, spread, col_own, dep_own)
+    got = []
+    for s in range(2, groups):
+        got.append(lax.ppermute(bufs[s - 2], "block", [(i, i ^ s) for i in range(groups)]))
+
+    near_rows = pl.pallas_call(
+        functools.partial(near_kernel, cfg),
+        out_shape=[shape] * 2 + [pltpu.VMEM((16, LANES), F32)],
+        in_specs=[smem] + [vmem] * 10,
+        out_specs=[vmem] * 3,
+        scratch_shapes=[
+            pltpu.VMEM(col_own.shape, BF16),
+            pltpu.VMEM(dep_own.shape, F32),
+        ],
+        compiler_params=params,
+        cost_estimate=pl.CostEstimate(
+            flops=cfg["n_near"] * cols * rays_flops, bytes_accessed=10**6, transcendentals=0
+        ),
+        name="near",
+    )
+    mine, mate, meta = near_rows(
+        here, own, tiled, wmid, whead, spread, col_own, dep_own, col_halo, dep_halo, meta
+    )
+    got = [mine, lax.ppermute(mate, "block", [(i, i ^ 1) for i in range(groups)])] + got
+
+    order_l = meta[0, : nb + 1].astype(jnp.int32)
+    order_r = meta[8, : nb + 1].astype(jnp.int32)
     flags = jnp.stack(
         [
             place,
@@ -502,45 +748,6 @@
     ).astype(jnp.int32)
     info = jnp.concatenate([flags, block_order[0], order_l[:nb], order_r[:nb]])
 
-    size = n_own + n_halo + n_dep + n_tail
-    params = pltpu.CompilerParams(vmem_limit_bytes=32 * 1024 * 1024)
-    smem = pl.BlockSpec(memory_space=pltpu.SMEM)
-    vmem = pl.BlockSpec(memory_space=pltpu.VMEM)
-    bufs = pl.pallas_call(
-        functools.partial(field_kernel, cfg),
-        out_shape=[pltpu.VMEM((size, LANES), BF16)] * groups,
-        in_specs=[smem] + [vmem] * 7,
-        out_specs=[vmem] * groups,
-        scratch_shapes=[
-            pltpu.VMEM((count + 2 * EDGE * cols, LANES), BF16),
-            pltpu.VMEM((hrays, LANES), F32),
-            pltpu.VMEM((4 * (count + 2 * EDGE * cols) // LANES, LANES), F32),
-            pltpu.VMEM((n_tail, LANES), F32),
-            pltpu.VMEM((blk_dev, width, w_in.shape[2]), BF16),
-            pltpu.VMEM((blk_dev, w_feat.shape[1], 2 * LANES), BF16),
-            pltpu.VMEM((blk_dev, hrays, width), F32),
-        ],
-        compiler_params=params,
-        name="field",
-    )(
-        jnp.stack([place, patch & 1]),
-        samples_in.reshape(blk_dev, count, width),
-        near,
-        far,
-        w_in,
-        w_mid,
-        w_feat,
-        w_density,
-    )
-
-    got = [bufs[0]]
-    for s in range(1, groups):
-        if power:
-            route = [(i, i ^ s) for i in range(groups)]
-        else:
-            route = [(i, (i + s) % groups) for i in range(groups)]
-        got.append(lax.ppermute(bufs[s], "block", route))
-
     w0, w1, w2, w3 = pl.pallas_call(
         weights_kernel,
         out_shape=[
@@ -554,7 +761,7 @@
         compiler_params=params,
         cost_estimate=pl.CostEstimate(flops=10**8, bytes_accessed=10**6, transcendentals=0),
         name="weights",
-    )(w_conv.reshape(-1, feat), w_color, bufs[0])
+    )(w_conv.reshape(-1, feat), w_color, mine)
     pitch = cfg["pitch"]
     rows_in, rows_mid = rows_dev + 2 * EDGE, rows_dev + 2
     return pl.pallas_call(
@@ -567,6 +774,7 @@
             pltpu.VMEM((rows_in * pitch, 2 * LANES), BF16),
             pltpu.VMEM((rows_mid * pitch + 16, 2 * LANES), F32),
             pltpu.VMEM(((rows_mid + 2) * pitch, 6 * LANES), BF16),
+            pltpu.VMEM((4, rows_mid * pitch + 16, 2 * LANES), F32),
             pltpu.VMEM((rows_mid * pitch, 16 * LANES), BF16),
             pltpu.VMEM((hchunks * LANES, groups * LANES), F32),
             pltpu.SMEM((nb,), jnp.int32),

time: 37.5 us -> 32.9 us (0.88)
  the two profiles are of different devices: /device:TPU:17 before, /device:TPU:3 now
where the time goes in v3:
time: 32.9 us; the launch traced here: 32.6 us
  Pallas kernels  17 us (52%)
  starting transfers between devices  7.38 us (22%)
  waiting for transfers between devices  4.4 us (13%)
  local copies, waits for them, and re-layouts  2.2 us (7%)
  between operations  1.53 us (5%)
    pallas_call x1, Pallas kernels, body(): pl.pallas_call(functools.partial(field_kernel, cfg), out_shape=[pltpu.VME...  5.21 us
    pallas_call x1, Pallas kernels, body(): pl.pallas_call(functools.partial(decoder_kernel, cfg), out_shape=jax.Shap...  5.05 us
    ppermute x2, waiting for transfers between devices, body(): lax.ppermute(bufs[s - 2], 'block', [(i, i ^ s) for i in range(groups)])  4.39 us
    ppermute x1, starting transfers between devices, body(): far = lax.ppermute(far, 'patch', swap_far)  4.36 us
    pallas_call x1, Pallas kernels, body(): near_rows(here, own, tiled, wmid, whead, spread, col_own, dep_own, col_ha...  2.93 us
    pallas_call x1, Pallas kernels, body(): pl.pallas_call(functools.partial(edges_kernel, cfg), out_shape=[pltpu.VME...  1.66 us
    ppermute x2, starting transfers between devices, body(): lax.ppermute(bufs[s - 2], 'block', [(i, i ^ s) for i in range(groups)])  1.65 us
    pallas_call x1, Pallas kernels, body(): pl.pallas_call(functools.partial(halo_kernel, cfg), out_shape=[shape] * (...  1.65 us
  transfers between devices with their start and end apart: 5, of which 2 were waited for; matrix products, arithmetic and copies ran while one was open for 3% of the time, Pallas kernels for 18%

profile of v3, /device:TPU:3, one launch (start us, length us, event | category | flops | bytes accessed | tf_op | source)
XLA Modules:
  0.0 32.6 jit_solution(712820803411384985)
XLA Ops:
  0.7 0.1 pad_add_fusion.at_ref
  0.7 0.0 copy-start.4
  0.7 1.7 %edges.1 = (bf16[2,1024,128]{2,1,0:T(8,128)(2,1)S(1)}, bf16[2,32,256]{2,1,0:T(8,128)(2,1)S(1)}, bf16[2,256]{1,0:T(2,128)(2,1)S(1)}, bf16[80,128]{1,0:T(8,128)(2,1)S(1)}, bf16[80,128]{1,0:T(8,128)(2,1)S(1)}) custom-call(s32[2]{0:T(128)S(1)} %pad_add_fusion.at_ref, s32[1,8]{1,0:T(1,128)} %order_hbm.1, s32[1]{0:T(128)} %copy.11.seam_hbm, ...), custom_call_target="tpu_custom_call" | custom-call | tf_op jit(solution)/shard_map/edges/pallas_call | solution.py:638
  2.4 0.0 copy-start.2
  2.4 0.1 collective-permute-start
  2.5 4.4 %collective-permute-start.1 = (bf16[80,128]{1,0:T(8,128)(2,1)S(1)}, bf16[80,128]{1,0:T(8,128)(2,1)S(1)}, u32[]{:S(2)}, u32[]{:S(2)}) collective-permute-start(bf16[80,128]{1,0:T(8,128)(2,1)S(1)} %get-tuple-element.38), channel_id=1, source_target_pairs={{1,2},{2,1},{3,4},{4,3},{5,6},{6,5},{9,10},{10,9},{11,12},{12,11},... | collective-permute-start | bytes 61448 | tf_op jit(solution)/shard_map/ppermute | solution.py:670
  6.9 0.0 copy-done.4
  6.9 0.1 copy.10.wf_ref
  7.0 5.2 %field.1 = (bf16[1280,128]{1,0:T(8,128)(2,1)S(1)}, f32[80,128]{1,0:T(8,128)S(1)}, bf16[2,128,256]{2,1,0:T(8,128)(2,1)S(1)}, bf16[2,4,256,256]{3,2,1,0:T(8,128)(2...) custom-call(s32[2]{0:T(128)S(1)} %pad_add_fusion.at_ref, ...), custom_call_target="tpu_custom_call" | custom-call | flops 4026531840 | bytes 1000000 | tf_op jit(solution)/shard_map/field/pallas_call | solution.py:675
  12.2 0.0 copy-done.2
  12.2 0.0 collective-permute-done.near_ref
  12.3 0.0 collective-permute-done.1.far_ref
  12.3 0.0 copy-start.3
  12.3 1.6 %halo.1 = (bf16[576,128]{1,0:T(8,128)(2,1)S(1)}, bf16[576,128]{1,0:T(8,128)(2,1)S(1)}, f32[80,128]{1,0:T(8,128)S(1)}, f32[16,128]{1,0:T(8,128)S(1)}, f32[16,128]{1,0:T(8,128)S(1)}) custom-call(s32[2]{0:T(128)S(1)} %pad_add_fusion.at_ref, bf16[80,128]{1,0:T(8,128)(2,1)S(1)} %collective-permute-done.near_ref, ...), custom_call_target="tpu_custom_call" | custom-call | tf_op jit(solution)/shard_map/halo/pallas_call | solution.py:697
  13.9 0.0 copy-done.3
  13.9 0.0 copy-start
  13.9 2.9 %near.1 = (bf16[576,128]{1,0:T(8,128)(2,1)S(1)}, bf16[576,128]{1,0:T(8,128)(2,1)S(1)}, f32[16,128]{1,0:T(8,128)S(1)}) custom-call(s32[2]{0:T(128)S(1)} %pad_add_fusion.at_ref, bf16[2,1024,128]{2,1,0:T(8,128)(2,1)S(1)} %copy-done.3, bf16[2,128,256]{2,1,0:T(8,128)(2,1)S(1)} %get-tuple-element.31.tiled, ...), custom_call_target="tpu_custom_call" | custom-call | flops 2415919104 | bytes 1000000 | tf_op jit(solution)/shard_map/near/pallas_call | solution.py:730
  16.9 1.3 %collective-permute-start.2 = (bf16[576,128]{1,0:T(8,128)(2,1)S(1)}, bf16[576,128]{1,0:T(8,128)(2,1)S(1)}, u32[]{:S(2)}, u32[]{:S(2)}) collective-permute-start(bf16[576,128]{1,0:T(8,128)(2,1)S(1)} %get-tuple-element.48), channel_id=1, source_target_pairs={{0,8},{8,0},{16,24},{24,16},{1,9},{9,1},{17,25},{25,17},{2,10},{10... | collective-permute-start | bytes 442376 | tf_op jit(solution)/shard_map/ppermute | solution.py:733
  18.2 0.7 %slice.23 = s32[1,1]{1,0:T(1,128)} slice(s32[1,9]{1,0:T(1,128)S(1)} %get-tuple-element.52), slice={[0:1], [8:9]} | slice | bytes 8 | tf_op jit(solution)/shard_map/slice | solution.py:740
  18.8 1.2 %collective-permute-start.3 = (bf16[576,128]{1,0:T(8,128)(2,1)S(1)}, bf16[576,128]{1,0:T(8,128)(2,1)S(1)}, u32[]{:S(2)}, u32[]{:S(2)}) collective-permute-start(bf16[576,128]{1,0:T(8,128)(2,1)S(1)} %get-tuple-element.49), channel_id=1, source_target_pairs={{0,16},{8,24},{16,0},{24,8},{1,17},{9,25},{17,1},{25,9},{2,18},{10... | collective-permute-start | bytes 442376 | tf_op jit(solution)/shard_map/ppermute | solution.py:713
  20.1 0.4 %collective-permute-start.4 = (bf16[576,128]{1,0:T(8,128)(2,1)S(1)}, bf16[576,128]{1,0:T(8,128)(2,1)S(1)}, u32[]{:S(2)}, u32[]{:S(2)}) collective-permute-start(bf16[576,128]{1,0:T(8,128)(2,1)S(1)} %get-tuple-element.50), channel_id=1, source_target_pairs={{0,24},{8,16},{16,8},{24,0},{1,25},{9,17},{17,9},{25,1},{2,26},{10... | collective-permute-start | bytes 442376 | tf_op jit(solution)/shard_map/ppermute | solution.py:713
  21.2 0.0 copy-start.5
  21.2 0.6 %copy-done.5 = s32[1,8]{1,0:T(1,128)S(1)} copy-done((s32[1,8]{1,0:T(1,128)S(1)}, s32[1,8]{1,0:T(1,128)}, u32[]{:S(2)}) %copy-start.5) | copy-done | bytes 56
  21.9 0.1 concatenate.3.info_ref
  21.9 0.0 copy-start.1
  21.9 0.0 copy-done
  21.9 0.7 %copy-done.1 = bf16[3,64]{1,0:T(4,128)(2,1)S(1)} copy-done((bf16[3,64]{1,0:T(4,128)(2,1)S(1)}, bf16[3,64]{1,0:T(4,128)(2,1)}, u32[]{:S(2)}) %copy-start.1) | copy-done | bytes 408
  22.6 0.5 %weights.1 = (bf16[256,768]{1,0:T(8,128)(2,1)S(1)}, bf16[256,1536]{1,0:T(8,128)(2,1)S(1)}, bf16[2,256,768]{2,1,0:T(8,128)(2,1)S(1)}, bf16[128,3072]{1,0:T(8,128)(2,1)S(1)}) custom-call(bf16[2304,64]{1,0:T(8,128)(2,1)S(1)} %bitcast.16, bf16[3,64]{1,0:T(4,128)(2,1)S(1)} %copy-done.1, bf16[576,128]{1,0:T(8,128)(2,1)S(1)} %get-tuple-element.43.after_ref.rest_0_), custom_call_target="tpu_custom_call" | custom-call | flops 100000000 | bytes 1000000 | tf_op jit(solution)/shard_map/weights/pallas_call | solution.py:751
  23.2 0.0 collective-permute-done.2.rest_1_
  23.2 1.0 %collective-permute-done.3.rest_2_ = bf16[576,128]{1,0:T(8,128)(2,1)S(1)} collective-permute-done((bf16[576,128]{1,0:T(8,128)(2,1)S(1)}, bf16[576,128]{1,0:T(8,128)(2,1)S(1)}, u32[]{:S(2)}, u32[]{:S(2)}) %collective-permute-start.3) | collective-permute-done | bytes 147488 | tf_op jit(solution)/shard_map/ppermute | solution.py:713
  24.2 3.3 %collective-permute-done.4.rest_3_ = bf16[576,128]{1,0:T(8,128)(2,1)S(1)} collective-permute-done((bf16[576,128]{1,0:T(8,128)(2,1)S(1)}, bf16[576,128]{1,0:T(8,128)(2,1)S(1)}, u32[]{:S(2)}, u32[]{:S(2)}) %collective-permute-start.4) | collective-permute-done | bytes 147488 | tf_op jit(solution)/shard_map/ppermute | solution.py:713
  27.6 5.0 %decoder.1 = f32[3,16,256]{2,1,0:T(8,128)} custom-call(s32[32]{0:T(128)S(1)} %concatenate.3.info_ref, bf16[256,768]{1,0:T(8,128)(2,1)S(1)} %get-tuple-element.44.w0_ref, bf16[256,1536]{1,0:T(8,128)(2,1)S(1)} %get-tuple-element.45.w1_ref, bf16[2,256,768]{2,1,0:T(8,128)(2,1)S(1)} %get-tuple-element.46.w2_ref, bf16[128,3072]{1,0:T(8,128)(2,1)S(1)} %get-tuple-element.47.w3_ref, ...), custom_call_target="tpu_custom_call" | custom-call | tf_op jit(solution)/shard_map/decoder/pallas_call | solution.py:767
  (3 shorter events, 0.0 us)
Async XLA Ops:
  0.7 6.1 %copy-start.4 = (bf16[2,256,64]{1,2,0:T(8,128)(2,1)S(1)}, bf16[2,256,64]{1,2,0:T(8,128)(2,1)}, u32[]{:S(2)}) copy-start(bf16[2,256,64]{1,2,0:T(8,128)(2,1)} %param.14) | copy-start | bytes 196612
  2.4 9.8 %copy-start.2 = (bf16[2,1024,128]{2,1,0:T(8,128)(2,1)}, bf16[2,1024,128]{2,1,0:T(8,128)(2,1)S(1)}, u32[]{:S(2)}) copy-start(bf16[2,1024,128]{2,1,0:T(8,128)(2,1)S(1)} %get-tuple-element.28.own_ref) | copy-start | bytes 1572868
  2.4 9.8 %collective-permute-start = (bf16[80,128]{1,0:T(8,128)(2,1)S(1)}, bf16[80,128]{1,0:T(8,128)(2,1)S(1)}, u32[]{:S(2)}, u32[]{:S(2)}) collective-permute-start(bf16[80,128]{1,0:T(8,128)(2,1)S(1)} %get-tuple-element.37), channel_id=1, source_target_pairs={{0,1},{1,0},{2,3},{3,2},{4,5},{5,4},{6,7},{7,6},{8,9},{9,8},{10,11... | collective-permute-start | bytes 61448 | tf_op jit(solution)/shard_map/ppermute | solution.py:671
  2.5 9.8 %collective-permute-start.1 = (bf16[80,128]{1,0:T(8,128)(2,1)S(1)}, bf16[80,128]{1,0:T(8,128)(2,1)S(1)}, u32[]{:S(2)}, u32[]{:S(2)}) collective-permute-start(bf16[80,128]{1,0:T(8,128)(2,1)S(1)} %get-tuple-element.38), channel_id=1, source_target_pairs={{1,2},{2,1},{3,4},{4,3},{5,6},{6,5},{9,10},{10,9},{11,12},{12,11},... | collective-permute-start | bytes 61448 | tf_op jit(solution)/shard_map/ppermute | solution.py:670
  12.3 1.7 %copy-start.3 = (bf16[2,1024,128]{2,1,0:T(8,128)(2,1)S(1)}, bf16[2,1024,128]{2,1,0:T(8,128)(2,1)}, u32[]{:S(2)}) copy-start(bf16[2,1024,128]{2,1,0:T(8,128)(2,1)} %copy-done.2) | copy-start | bytes 1572868
  13.9 8.0 %copy-start = (bf16[4,3,3,64,64]{4,3,2,1,0:T(8,128)(2,1)S(1)}, bf16[4,3,3,64,64]{4,3,2,1,0:T(8,128)(2,1)}, u32[]{:S(2)}) copy-start(bf16[4,3,3,64,64]{4,3,2,1,0:T(8,128)(2,1)} %param.16) | copy-start | bytes 884740
  16.9 6.3 %collective-permute-start.2 = (bf16[576,128]{1,0:T(8,128)(2,1)S(1)}, bf16[576,128]{1,0:T(8,128)(2,1)S(1)}, u32[]{:S(2)}, u32[]{:S(2)}) collective-permute-start(bf16[576,128]{1,0:T(8,128)(2,1)S(1)} %get-tuple-element.48), channel_id=1, source_target_pairs={{0,8},{8,0},{16,24},{24,16},{1,9},{9,1},{17,25},{25,17},{2,10},{10... | collective-permute-start | bytes 442376 | tf_op jit(solution)/shard_map/ppermute | solution.py:733
  18.8 5.4 %collective-permute-start.3 = (bf16[576,128]{1,0:T(8,128)(2,1)S(1)}, bf16[576,128]{1,0:T(8,128)(2,1)S(1)}, u32[]{:S(2)}, u32[]{:S(2)}) collective-permute-start(bf16[576,128]{1,0:T(8,128)(2,1)S(1)} %get-tuple-element.49), channel_id=1, source_target_pairs={{0,16},{8,24},{16,0},{24,8},{1,17},{9,25},{17,1},{25,9},{2,18},{10... | collective-permute-start | bytes 442376 | tf_op jit(solution)/shard_map/ppermute | solution.py:713
  20.1 7.5 %collective-permute-start.4 = (bf16[576,128]{1,0:T(8,128)(2,1)S(1)}, bf16[576,128]{1,0:T(8,128)(2,1)S(1)}, u32[]{:S(2)}, u32[]{:S(2)}) collective-permute-start(bf16[576,128]{1,0:T(8,128)(2,1)S(1)} %get-tuple-element.50), channel_id=1, source_target_pairs={{0,24},{8,16},{16,8},{24,0},{1,25},{9,17},{17,9},{25,1},{2,26},{10... | collective-permute-start | bytes 442376 | tf_op jit(solution)/shard_map/ppermute | solution.py:713
  21.2 0.7 %copy-start.5 = (s32[1,8]{1,0:T(1,128)S(1)}, s32[1,8]{1,0:T(1,128)}, u32[]{:S(2)}) copy-start(s32[1,8]{1,0:T(1,128)} %order_hbm.1) | copy-start | bytes 100
  21.9 0.7 %copy-start.1 = (bf16[3,64]{1,0:T(4,128)(2,1)S(1)}, bf16[3,64]{1,0:T(4,128)(2,1)}, u32[]{:S(2)}) copy-start(bf16[3,64]{1,0:T(4,128)(2,1)} %colour_ref.1) | copy-start | bytes 1156

commit v4 on v3

--- a/solution.py
+++ b/solution.py
@@ -99,23 +99,25 @@
 
 
 def edges_kernel(
-    cfg, at_ref, order_hbm, seam_hbm, own_hbm, win_hbm, wd_hbm,
-    own_ref, win_ref, wd_ref, near_ref, far_ref,
-    left, right, order_ref, seam_ref, sems,
+    cfg, order_hbm, seam_hbm, own_hbm, *rest
 ):
+    n = (len(rest) - 8) // 2
+    sources, targets = rest[:n], rest[n + 1 : 2 * n + 1]
+    own_ref = rest[n]
+    meta_ref, near_ref, far_ref, left, right, order_ref, seam_ref, sems = rest[2 * n + 1 :]
     cols, rows_all = cfg["cols"], cfg["rows_all"]
     blocks = own_ref.shape[0]
     small = [
-        pltpu.make_async_copy(order_hbm, order_ref, sems.at[2]),
-        pltpu.make_async_copy(seam_hbm, seam_ref, sems.at[3]),
+        pltpu.make_async_copy(order_hbm, order_ref, sems.at[n + 1]),
+        pltpu.make_async_copy(seam_hbm, seam_ref, sems.at[n + 2]),
     ]
     for copy in small:
         copy.start()
     load = pltpu.make_async_copy(own_hbm, own_ref, sems.at[0])
     load.start()
     more = [
-        pltpu.make_async_copy(win_hbm, win_ref, sems.at[1]),
-        pltpu.make_async_copy(wd_hbm, wd_ref, sems.at[4]),
+        pltpu.make_async_copy(source, target, sems.at[1 + i])
+        for i, (source, target) in enumerate(zip(sources, targets))
     ]
     for copy in more:
         copy.start()
@@ -135,7 +137,8 @@
             left[q : q + EDGE, :] = own_ref[b, r * cols : r * cols + 16, :].astype(F32)[:EDGE]
             last = own_ref[b, (r + 1) * cols - 16 : (r + 1) * cols, :].astype(F32)
             right[q : q + EDGE, :] = last[16 - EDGE :]
-    odd = at_ref[1] == 1
+    meta_ref[...] = meta
+    odd = (lax.axis_index("patch") & 1) == 1
     near_ref[:size, :] = jnp.where(odd, left[...], right[...]).astype(BF16)
     far_ref[:size, :] = jnp.where(odd, right[...], left[...]).astype(BF16)
     near_ref[size:, :] = meta
@@ -193,11 +196,8 @@
 
 
 def field_kernel(
-    cfg, at_ref, own_ref, win_ref, wmid_hbm, wf_ref, wd_ref,
-    col_own, dep_own, tiled, whead, spread, wmid_ref, sem,
+    cfg, own_ref, win_ref, wmid_ref, wf_ref, wd_ref, col_own, dep_own, tiled, whead, spread
 ):
-    load = pltpu.make_async_copy(wmid_hbm, wmid_ref, sem)
-    load.start()
     samples, enc = cfg["samples"], cfg["enc"]
     blocks = own_ref.shape[0]
     pad = EDGE * cfg["cols"]
@@ -227,9 +227,8 @@
     spread[...] = one_hot(
         spread.shape, lambda r, c: (r & (LANES - 1)) == c // (LANES // blocks) * repeat
     )
-    load.wait()
     nets = (tiled, wmid_ref, whead, spread)
-    pieces = row_pieces(cfg, at_ref[0], False)
+    pieces = row_pieces(cfg, lax.axis_index("block"), False)
     field_chunks(cfg, own_ref, nets, col_own, dep_own, grouped(pieces, cfg["chunk"]))
 
 
@@ -254,13 +253,13 @@
 
 
 def halo_kernel(
-    cfg, at_ref, near_ref, far_ref, tiled, wmid_ref, whead, spread, col_own, dep_own, *rest
+    cfg, near_ref, far_ref, tiled, wmid_ref, whead, spread, col_own, dep_own, *rest
 ):
     outs = rest[: cfg["groups"] - 2]
     col_halo, dep_halo, meta, halo_ref = rest[cfg["groups"] - 2 :]
     samples, enc, rows_all = cfg["samples"], cfg["enc"], cfg["rows_all"]
     blocks = halo_ref.shape[0]
-    odd = at_ref[1] == 1
+    odd = (lax.axis_index("patch") & 1) == 1
     near, far = near_ref[...].astype(F32), far_ref[...].astype(F32)
     sides = [jnp.where(odd, near, far), jnp.where(odd, far, near)]
     side_rays = rows_all * EDGE
@@ -283,28 +282,52 @@
             part = jnp.concatenate([part, jnp.zeros((LANES - part.shape[0], LANES), F32)], axis=0)
         dep_halo[4 * k : 4 * k + 4, :] = depth_rows(part, cfg["repeat"])
     for s in range(2, cfg["groups"]):
-        pack(cfg, at_ref[0], s, outs[s - 2], col_own, dep_own, col_halo, dep_halo)
+        pack(cfg, lax.axis_index("block"), s, outs[s - 2], col_own, dep_own, col_halo, dep_halo)
+
+
+def earlier_blocks(cfg, place, order, rows):
+    groups, nb = cfg["groups"], cfg["nb"]
+    per = nb // groups
+    sub = lax.broadcasted_iota(jnp.int32, (rows, LANES), 0)
+    lane = lax.broadcasted_iota(jnp.int32, (rows, LANES), 1)
+    hit = (jnp.broadcast_to(order, (rows, LANES)) == sub.astype(F32)) & (lane < nb)
+    rank = jnp.sum(jnp.where(hit, lane.astype(F32), 0.0), axis=1, keepdims=True)
+    rank = jnp.broadcast_to(rank, (rows, LANES))
+    block = ((lane // (2 * per)) ^ place) * per + lane % per
+    other = jnp.sum(jnp.where(sub == block, rank, 0.0), axis=0, keepdims=True)
+    return jnp.where(other < rank, 1.0, 0.0)
 
 
 def near_kernel(
-    cfg, at_ref, own_ref, tiled, wmid_ref, whead, spread, col_in, dep_in, col_halo, dep_halo,
-    meta_in, out_own, out_mate, meta, col_own, dep_own,
+    cfg, own_ref, tiled, wmid_ref, whead, spread, col_in, dep_in, col_halo, dep_halo,
+    meta_sides, meta_own, out_own, out_mate, earlier, flags, col_own, dep_own,
 ):
-    meta[...] = meta_in[...]
+    nb, patch = cfg["nb"], lax.axis_index("patch")
+    mine = meta_own[...].astype(F32)[0:1]
+    sides = [mine, meta_sides[0:1, :], meta_sides[8:9, :]]
+    rows = earlier.shape[0] // 3
+    for i, order in enumerate(sides):
+        made = earlier_blocks(cfg, lax.axis_index("block"), order, rows)
+        earlier[i * rows : (i + 1) * rows, :] = made.astype(BF16)
+    lane = lax.broadcasted_iota(jnp.int32, (1, LANES), 1)
+    for i, (order, there) in enumerate([(sides[1], patch > 0), (mine, patch < cfg["patches"] - 1)]):
+        seam = jnp.sum(jnp.where(lane == nb, order, 0.0), axis=1, keepdims=True)
+        seam = jnp.where(there, seam, 0.0)
+        flags[8 * i : 8 * i + 8, :] = jnp.broadcast_to(seam, (8, LANES))
     col_own[...] = col_in[...]
     dep_own[...] = dep_in[...]
     nets = (tiled, wmid_ref, whead, spread)
-    pieces = row_pieces(cfg, at_ref[0], True)
+    pieces = row_pieces(cfg, lax.axis_index("block"), True)
     field_chunks(cfg, own_ref, nets, col_own, dep_own, grouped(pieces, cfg["chunk"]))
-    pack(cfg, at_ref[0], 0, out_own, col_own, dep_own, col_halo, dep_halo)
-    pack(cfg, at_ref[0], 1, out_mate, col_own, dep_own, col_halo, dep_halo)
-
-
-def decoder_kernel(cfg, info_ref, w0_ref, w1_ref, w2_ref, w3_ref, *rest):
+    pack(cfg, lax.axis_index("block"), 0, out_own, col_own, dep_own, col_halo, dep_halo)
+    pack(cfg, lax.axis_index("block"), 1, out_mate, col_own, dep_own, col_halo, dep_halo)
+
+
+def decoder_kernel(cfg, earlier_ref, flags_ref, w0_ref, w1_ref, w2_ref, w3_ref, *rest):
     groups, nb = cfg["groups"], cfg["nb"]
     bufs = rest[:groups]
     out_ref = rest[groups]
-    comp, x0, sa, xa, sc, xc, rep, rank_ref = rest[groups + 1 :]
+    comp, x0, sa, xa, sc, xc, rep = rest[groups + 1 :]
     cols, rows_dev, pitch = cfg["cols"], cfg["rows_dev"], cfg["pitch"]
     n_own, n_halo, n_dep = cfg["n_own"], cfg["n_halo"], cfg["n_dep"]
     rows_in = rows_dev + 2 * EDGE
@@ -312,27 +335,14 @@
     mid = rows_mid * pitch
     half = LANES // 2
     per_dev = nb // groups
-    place = info_ref[0]
-    left_open, right_open = info_ref[1].astype(F32), info_ref[2].astype(F32)
-    top_open, bottom_open = info_ref[3].astype(F32), info_ref[4].astype(F32)
-
-    earlier = []
-    for side in range(3):
-        for k in range(nb):
-            rank_ref[info_ref[8 + side * nb + k]] = k
-        wide = 2 * per_dev * groups
-        row = jnp.zeros((nb, wide), jnp.int32)
-        column = jnp.zeros((nb, wide), jnp.int32)
-        lane = lax.broadcasted_iota(jnp.int32, (nb, wide), 1)
-        sub = lax.broadcasted_iota(jnp.int32, (nb, wide), 0)
-        for s in range(groups):
-            source = place ^ s
-            for i in range(per_dev):
-                rank = rank_ref[source * per_dev + i]
-                at = s * 2 * per_dev + i
-                row = jnp.where((lane == at) | (lane == at + per_dev), rank, row)
-                column = jnp.where(sub == s * per_dev + i, rank, column)
-        earlier.append(jnp.where(row < column, 1.0, 0.0).astype(BF16))
+    place = lax.axis_index("block")
+    left_open, right_open = flags_ref[0:1, :], flags_ref[8:9, :]
+    top_open = jnp.where(place > 0, 1.0, 0.0)
+    bottom_open = jnp.where(place < groups - 1, 1.0, 0.0)
+
+    sides = earlier_ref.shape[0] // 3
+    stacked = 2 * per_dev * groups
+    earlier = [earlier_ref[i * sides : i * sides + nb, :stacked] for i in range(3)]
 
     at = n_own + n_halo
     own_rows = [bufs[s][at : at + n_dep, :].astype(F32) for s in range(groups)]
@@ -361,7 +371,8 @@
     def spread(k):
         r = lax.broadcasted_iota(jnp.int32, (LANES, groups * LANES), 0)
         c = lax.broadcasted_iota(jnp.int32, (LANES, groups * LANES), 1)
-        pick = jnp.where(r - k * nb == c // half, 1.0, 0.0).astype(BF16)
+        block = ((c // LANES) ^ place) * per_dev + (c & (LANES - 1)) // half
+        pick = jnp.where(r - k * nb == block, 1.0, 0.0).astype(BF16)
         return dot(high, pick) + dot(low, pick)
 
     def mix(weights, lo, n):
@@ -399,6 +410,8 @@
     pos = q
     for r in range(1, rows_mid):
         pos = pos - jnp.where(q >= r * pitch, pitch, 0)
+    left_open = jnp.concatenate([left_open, left_open], axis=1)
+    right_open = jnp.concatenate([right_open, right_open], axis=1)
     mask = jnp.where(pos < LEAD, left_open, jnp.where(pos >= LEAD + cols, right_open, 1.0))
     mask = mask * jnp.where(q < pitch, top_open, jnp.where(q >= mid - pitch, bottom_open, 1.0))
 
@@ -592,8 +605,7 @@
 
 def body(samples_in, block_order, seam_link, w_in, w_mid, w_feat, w_density, w_conv, w_color):
     blk_dev, rows_all, cols, width = samples_in.shape
-    groups, place = lax.axis_size("block"), lax.axis_index("block")
-    patches, patch = lax.axis_size("patch"), lax.axis_index("patch")
+    groups, patches = lax.axis_size("block"), lax.axis_size("patch")
     nb = block_order.shape[1]
     enc = w_in.shape[1]
     feat = w_feat.shape[2]
@@ -609,6 +621,7 @@
     cfg = dict(
         groups=groups,
         nb=nb,
+        patches=patches,
         samples=samples,
         enc=enc,
         repeat=LANES // (samples * blk_dev),
@@ -624,44 +637,41 @@
         n_dep=n_dep,
         hchunks=hchunks,
     )
-    smem = pl.BlockSpec(memory_space=pltpu.SMEM)
     vmem = pl.BlockSpec(memory_space=pltpu.VMEM)
     hbm = pl.BlockSpec(memory_space=pltpu.HBM)
-    params = pltpu.CompilerParams(vmem_limit_bytes=24 * 1024 * 1024)
-    here = jnp.stack([place, patch & 1])
+    params = pltpu.CompilerParams(vmem_limit_bytes=16 * 1024 * 1024)
 
     def far_off(x):
         return pltpu.with_memory_space_constraint(x, pltpu.HBM)
 
 
     edges = blk_dev * rows_all * EDGE
-    own, win, dens, near, far = pl.pallas_call(
+    early = [w_in, w_mid, w_density, w_color]
+    own, win, wmid, dens, colour, meta_own, near, far = pl.pallas_call(
         functools.partial(edges_kernel, cfg),
-        out_shape=[
-            pltpu.VMEM((blk_dev, count, width), BF16),
-            pltpu.VMEM(w_in.shape, BF16),
-            pltpu.VMEM(w_density.shape, BF16),
+        out_shape=[pltpu.VMEM((blk_dev, count, width), BF16)]
+        + [pltpu.VMEM(x.shape, BF16) for x in early]
+        + [
+            pltpu.VMEM((16, width), BF16),
             pltpu.VMEM((edges + 16, width), BF16),
             pltpu.VMEM((edges + 16, width), BF16),
         ],
-        in_specs=[smem] + [hbm] * 5,
-        out_specs=[vmem] * 5,
+        in_specs=[hbm] * (3 + len(early)),
+        out_specs=[vmem] * (4 + len(early)),
         scratch_shapes=[
             pltpu.VMEM((edges, width), F32),
             pltpu.VMEM((edges, width), F32),
             pltpu.SMEM(block_order.shape, jnp.int32),
             pltpu.SMEM(seam_link.shape, jnp.int32),
-            pltpu.SemaphoreType.DMA((5,)),
+            pltpu.SemaphoreType.DMA((3 + len(early),)),
         ],
         compiler_params=params,
         name="edges",
     )(
-        here,
         far_off(block_order),
         seam_link,
         far_off(samples_in.reshape(blk_dev, count, width)),
-        far_off(w_in),
-        far_off(w_density),
+        *[far_off(x) for x in early],
     )
     swap_near = [(i, i ^ 1) for i in range(patches) if i ^ 1 < patches]
     swap_far = []
@@ -672,7 +682,7 @@
 
     rays_flops = 2 * 2 * blk_dev * samples * w_mid.shape[2] * (3 * w_mid.shape[2])
     far_rays = (rows_all - cfg["n_near"]) * cols
-    col_own, dep_own, tiled, whead, spread, wmid = pl.pallas_call(
+    col_own, dep_own, tiled, whead, spread = pl.pallas_call(
         functools.partial(field_kernel, cfg),
         out_shape=[
             pltpu.VMEM((count + 2 * EDGE * cols, LANES), BF16),
@@ -680,17 +690,15 @@
             pltpu.VMEM((blk_dev, width, w_in.shape[2]), BF16),
             pltpu.VMEM((blk_dev, samples, w_feat.shape[1], 2 * LANES), BF16),
             pltpu.VMEM((2 * LANES, samples * LANES), BF16),
-            pltpu.VMEM(w_mid.shape, BF16),
         ],
-        in_specs=[smem, vmem, vmem, hbm, vmem, vmem],
-        out_specs=[vmem] * 6,
-        scratch_shapes=[pltpu.SemaphoreType.DMA],
+        in_specs=[vmem] * 5,
+        out_specs=[vmem] * 5,
         compiler_params=params,
         cost_estimate=pl.CostEstimate(
             flops=far_rays * rays_flops, bytes_accessed=10**6, transcendentals=0
         ),
         name="field",
-    )(here, own, win, far_off(w_mid), w_feat, dens)
+    )(own, win, wmid, w_feat, dens)
 
     size = n_own + n_halo + n_dep + n_tail
     shape = pltpu.VMEM((size, LANES), BF16)
@@ -702,21 +710,22 @@
             pltpu.VMEM((n_tail, LANES), F32),
             pltpu.VMEM((16, LANES), F32),
         ],
-        in_specs=[smem] + [vmem] * 8,
+        in_specs=[vmem] * 8,
         out_specs=[vmem] * (groups + 1),
         scratch_shapes=[pltpu.VMEM((blk_dev, hrays, width), F32)],
         compiler_params=params,
         name="halo",
-    )(here, near, far, tiled, wmid, whead, spread, col_own, dep_own)
+    )(near, far, tiled, wmid, whead, spread, col_own, dep_own)
     got = []
     for s in range(2, groups):
         got.append(lax.ppermute(bufs[s - 2], "block", [(i, i ^ s) for i in range(groups)]))
 
     near_rows = pl.pallas_call(
         functools.partial(near_kernel, cfg),
-        out_shape=[shape] * 2 + [pltpu.VMEM((16, LANES), F32)],
-        in_specs=[smem] + [vmem] * 10,
-        out_specs=[vmem] * 3,
+        out_shape=[shape] * 2
+        + [pltpu.VMEM((48, LANES), BF16), pltpu.VMEM((16, LANES), F32)],
+        in_specs=[vmem] * 11,
+        out_specs=[vmem] * 4,
         scratch_shapes=[
             pltpu.VMEM(col_own.shape, BF16),
             pltpu.VMEM(dep_own.shape, F32),
@@ -727,26 +736,10 @@
         ),
         name="near",
     )
-    mine, mate, meta = near_rows(
-        here, own, tiled, wmid, whead, spread, col_own, dep_own, col_halo, dep_halo, meta
+    mine, mate, earlier, flags = near_rows(
+        own, tiled, wmid, whead, spread, col_own, dep_own, col_halo, dep_halo, meta, meta_own
     )
     got = [mine, lax.ppermute(mate, "block", [(i, i ^ 1) for i in range(groups)])] + got
-
-    order_l = meta[0, : nb + 1].astype(jnp.int32)
-    order_r = meta[8, : nb + 1].astype(jnp.int32)
-    flags = jnp.stack(
-        [
-            place,
-            order_l[nb] * (patch > 0),
-            seam_link[0] * (patch < patches - 1),
-            place > 0,
-            place < groups - 1,
-            place * 0,
-            place * 0,
-            place * 0,
-        ]
-    ).astype(jnp.int32)
-    info = jnp.concatenate([flags, block_order[0], order_l[:nb], order_r[:nb]])
 
     w0, w1, w2, w3 = pl.pallas_call(
         weights_kernel,
@@ -761,13 +754,13 @@
         compiler_params=params,
         cost_estimate=pl.CostEstimate(flops=10**8, bytes_accessed=10**6, transcendentals=0),
         name="weights",
-    )(w_conv.reshape(-1, feat), w_color, mine)
+    )(w_conv.reshape(-1, feat), colour, mine)
     pitch = cfg["pitch"]
     rows_in, rows_mid = rows_dev + 2 * EDGE, rows_dev + 2
     return pl.pallas_call(
         functools.partial(decoder_kernel, cfg),
         out_shape=jax.ShapeDtypeStruct((w_color.shape[0], 4 * rows_dev, 4 * cols), F32),
-        in_specs=[smem] + [vmem] * (4 + groups),
+        in_specs=[vmem] * (6 + groups),
         out_specs=vmem,
         scratch_shapes=[
             pltpu.VMEM(((rows_in + 2) * pitch, LANES), F32),
@@ -777,11 +770,10 @@
             pltpu.VMEM((4, rows_mid * pitch + 16, 2 * LANES), F32),
             pltpu.VMEM((rows_mid * pitch, 16 * LANES), BF16),
             pltpu.VMEM((hchunks * LANES, groups * LANES), F32),
-            pltpu.SMEM((nb,), jnp.int32),
         ],
         compiler_params=params,
         name="decoder",
-    )(info, w0, w1, w2, w3, *got)
+    )(earlier, flags, w0, w1, w2, w3, *got)
 
 
 def solution(mesh):

time: 32.9 us -> 28.6 us (0.87)
  the two profiles are of different devices: /device:TPU:3 before, /device:TPU:19 now
where the time goes in v4:
time: 28.6 us; the launch traced here: 28.5 us
  Pallas kernels  13.7 us (48%)
  starting transfers between devices  7.45 us (26%)
  waiting for transfers between devices  6.48 us (23%)
  between operations  0.75 us (3%)
    ppermute x2, waiting for transfers between devices, body(): lax.ppermute(bufs[s - 2], 'block', [(i, i ^ s) for i in range(groups)])  6.47 us
    pallas_call x1, Pallas kernels, body(): pl.pallas_call(functools.partial(decoder_kernel, cfg), out_shape=jax.Shap...  4.46 us
    ppermute x1, starting transfers between devices, body(): far = lax.ppermute(far, 'patch', swap_far)  4.12 us
    pallas_call x1, Pallas kernels, body(): pl.pallas_call(functools.partial(field_kernel, cfg), out_shape=[pltpu.VME...  3.82 us
    pallas_call x1, Pallas kernels, body(): near_rows(own, tiled, wmid, whead, spread, col_own, dep_own, col_halo, de...  2.43 us
    ppermute x2, starting transfers between devices, body(): lax.ppermute(bufs[s - 2], 'block', [(i, i ^ s) for i in range(groups)])  1.71 us
    pallas_call x1, Pallas kernels, body(): pl.pallas_call(functools.partial(edges_kernel, cfg), out_shape=[pltpu.VME...  1.32 us
    ppermute x1, starting transfers between devices, body(): lax.ppermute(mate, 'block', [(i, i ^ 1) for i in range(groups)])  1.3 us
  transfers between devices with their start and end apart: 5, of which 2 were waited for; matrix products, arithmetic and copies ran while one was open for 0% of the time, Pallas kernels for 15%

profile of v4, /device:TPU:19, one launch (start us, length us, event | category | flops | bytes accessed | tf_op | source)
XLA Modules:
  0.0 28.5 jit_solution(7926710731432403735)
XLA Ops:
  0.7 0.0 copy-start.1
  0.7 1.3 %edges.1 = (bf16[2,1024,128]{2,1,0:T(8,128)(2,1)S(1)}, bf16[2,32,256]{2,1,0:T(8,128)(2,1)S(1)}, bf16[2,2,256,256]{3,2,1,0:T(8,128)(2,1)S(1)}, bf16[2,256]{1,0:T(...) custom-call(s32[1,8]{1,0:T(1,128)} %order_hbm.1, ...), custom_call_target="tpu_custom_call" | custom-call | tf_op jit(solution)/shard_map/edges/pallas_call | solution.py:650
  2.0 0.3 %collective-permute-start = (bf16[80,128]{1,0:T(8,128)(2,1)S(1)}, bf16[80,128]{1,0:T(8,128)(2,1)S(1)}, u32[]{:S(2)}, u32[]{:S(2)}) collective-permute-start(bf16[80,128]{1,0:T(8,128)(2,1)S(1)} %get-tuple-element.40), channel_id=1, source_target_pairs={{0,1},{1,0},{2,3},{3,2},{4,5},{5,4},{6,7},{7,6},{8,9},{9,8},{10,11... | collective-permute-start | bytes 61448 | tf_op jit(solution)/shard_map/ppermute | solution.py:681
  2.3 4.1 %collective-permute-start.1 = (bf16[80,128]{1,0:T(8,128)(2,1)S(1)}, bf16[80,128]{1,0:T(8,128)(2,1)S(1)}, u32[]{:S(2)}, u32[]{:S(2)}) collective-permute-start(bf16[80,128]{1,0:T(8,128)(2,1)S(1)} %get-tuple-element.41), channel_id=1, source_target_pairs={{1,2},{2,1},{3,4},{4,3},{5,6},{6,5},{9,10},{10,9},{11,12},{12,11},... | collective-permute-start | bytes 61448 | tf_op jit(solution)/shard_map/ppermute | solution.py:680
  6.4 0.0 copy-done.1
  6.4 0.1 copy.10.wf_ref
  6.6 3.8 %field.1 = (bf16[1280,128]{1,0:T(8,128)(2,1)S(1)}, f32[80,128]{1,0:T(8,128)S(1)}, bf16[2,128,256]{2,1,0:T(8,128)(2,1)S(1)}, bf16[2,4,256,256]{3,2,1,0:T(8,128)(2,1)S(1)}, bf16[256,512]{1,0:T(8,128)(2,1)S(1)}) custom-call(bf16[2,1024,128]{2,1,0:T(8,128)(2,1)S(1)} %get-tuple-element.31.own_ref, bf16[2,32,256]{2,1,0:T(8,128)(2,1)S(1)} %get-tuple-element.32.win_ref, ...), custom_call_target="tpu_custom_call" | custom-call | flops 4026531840 | bytes 1000000 | tf_op jit(solution)/shard_map/field/pallas_call | solution.py:685
  10.4 0.0 collective-permute-done.near_ref
  10.4 0.0 collective-permute-done.1.far_ref
  10.4 1.1 %halo.1 = (bf16[576,128]{1,0:T(8,128)(2,1)S(1)}, bf16[576,128]{1,0:T(8,128)(2,1)S(1)}, f32[80,128]{1,0:T(8,128)S(1)}, f32[16,128]{1,0:T(8,128)S(1)}, f32[16,128]{1,0:T(8,128)S(1)}) custom-call(bf16[80,128]{1,0:T(8,128)(2,1)S(1)} %collective-permute-done.near_ref, bf16[80,128]{1,0:T(8,128)(2,1)S(1)} %collective-permute-done.1.far_ref, ...), custom_call_target="tpu_custom_call" | custom-call | tf_op jit(solution)/shard_map/halo/pallas_call | solution.py:705
  11.5 0.0 copy-start
  11.5 2.4 %near.1 = (bf16[576,128]{1,0:T(8,128)(2,1)S(1)}, bf16[576,128]{1,0:T(8,128)(2,1)S(1)}, bf16[48,128]{1,0:T(8,128)(2,1)S(1)}, f32[16,128]{1,0:T(8,128)S(1)}) custom-call(bf16[2,1024,128]{2,1,0:T(8,128)(2,1)S(1)} %get-tuple-element.31.own_ref, bf16[2,128,256]{2,1,0:T(8,128)(2,1)S(1)} %get-tuple-element.35.tiled, ...), custom_call_target="tpu_custom_call" | custom-call | flops 2415919104 | bytes 1000000 | tf_op jit(solution)/shard_map/near/pallas_call | solution.py:739
  14.0 1.3 %collective-permute-start.2 = (bf16[576,128]{1,0:T(8,128)(2,1)S(1)}, bf16[576,128]{1,0:T(8,128)(2,1)S(1)}, u32[]{:S(2)}, u32[]{:S(2)}) collective-permute-start(bf16[576,128]{1,0:T(8,128)(2,1)S(1)} %get-tuple-element.54), channel_id=1, source_target_pairs={{0,8},{8,0},{16,24},{24,16},{1,9},{9,1},{17,25},{25,17},{2,10},{10... | collective-permute-start | bytes 442376 | tf_op jit(solution)/shard_map/ppermute | solution.py:742
  15.3 1.2 %collective-permute-start.3 = (bf16[576,128]{1,0:T(8,128)(2,1)S(1)}, bf16[576,128]{1,0:T(8,128)(2,1)S(1)}, u32[]{:S(2)}, u32[]{:S(2)}) collective-permute-start(bf16[576,128]{1,0:T(8,128)(2,1)S(1)} %get-tuple-element.55), channel_id=1, source_target_pairs={{0,16},{8,24},{16,0},{24,8},{1,17},{9,25},{17,1},{25,9},{2,18},{10... | collective-permute-start | bytes 442376 | tf_op jit(solution)/shard_map/ppermute | solution.py:721
  16.5 0.5 %collective-permute-start.4 = (bf16[576,128]{1,0:T(8,128)(2,1)S(1)}, bf16[576,128]{1,0:T(8,128)(2,1)S(1)}, u32[]{:S(2)}, u32[]{:S(2)}) collective-permute-start(bf16[576,128]{1,0:T(8,128)(2,1)S(1)} %get-tuple-element.56), channel_id=1, source_target_pairs={{0,24},{8,16},{16,8},{24,0},{1,25},{9,17},{17,9},{25,1},{2,26},{10... | collective-permute-start | bytes 442376 | tf_op jit(solution)/shard_map/ppermute | solution.py:721
  17.0 0.0 copy-done
  17.0 0.5 %weights.1 = (bf16[256,768]{1,0:T(8,128)(2,1)S(1)}, bf16[256,1536]{1,0:T(8,128)(2,1)S(1)}, bf16[2,256,768]{2,1,0:T(8,128)(2,1)S(1)}, bf16[128,3072]{1,0:T(8,128)(2,1)S(1)}) custom-call(bf16[2304,64]{1,0:T(8,128)(2,1)S(1)} %bitcast.2, bf16[3,64]{1,0:T(4,128)(2,1)S(1)} %get-tuple-element.48.colour_ref, bf16[576,128]{1,0:T(8,128)(2,1)S(1)} %get-tuple-element.49.after_ref.rest_0_), custom_call_target="tpu_custom_call" | custom-call | flops 100000000 | bytes 1000000 | tf_op jit(solution)/shard_map/weights/pallas_call | solution.py:744
  17.5 0.0 collective-permute-done.2.rest_1_
  17.5 3.1 %collective-permute-done.3.rest_2_ = bf16[576,128]{1,0:T(8,128)(2,1)S(1)} collective-permute-done((bf16[576,128]{1,0:T(8,128)(2,1)S(1)}, bf16[576,128]{1,0:T(8,128)(2,1)S(1)}, u32[]{:S(2)}, u32[]{:S(2)}) %collective-permute-start.3) | collective-permute-done | bytes 147488 | tf_op jit(solution)/shard_map/ppermute | solution.py:721
  20.6 3.4 %collective-permute-done.4.rest_3_ = bf16[576,128]{1,0:T(8,128)(2,1)S(1)} collective-permute-done((bf16[576,128]{1,0:T(8,128)(2,1)S(1)}, bf16[576,128]{1,0:T(8,128)(2,1)S(1)}, u32[]{:S(2)}, u32[]{:S(2)}) %collective-permute-start.4) | collective-permute-done | bytes 147488 | tf_op jit(solution)/shard_map/ppermute | solution.py:721
  24.0 4.5 %decoder.1 = f32[3,16,256]{2,1,0:T(8,128)} custom-call(bf16[48,128]{1,0:T(8,128)(2,1)S(1)} %get-tuple-element.46.earlier_ref, f32[16,128]{1,0:T(8,128)S(1)} %get-tuple-element.47.flags_ref, bf16[256,768]{1,0:T(8,128)(2,1)S(1)} %get-tuple-element.50.w0_ref, bf16[256,1536]{1,0:T(8,128)(2,1)S(1)} %get-tuple-element.51.w1_ref, ...), custom_call_target="tpu_custom_call" | custom-call | tf_op jit(solution)/shard_map/decoder/pallas_call | solution.py:760
Async XLA Ops:
  0.7 5.8 %copy-start.1 = (bf16[2,256,64]{1,2,0:T(8,128)(2,1)S(1)}, bf16[2,256,64]{1,2,0:T(8,128)(2,1)}, u32[]{:S(2)}) copy-start(bf16[2,256,64]{1,2,0:T(8,128)(2,1)} %param.14) | copy-start | bytes 196612
  2.0 8.4 %collective-permute-start = (bf16[80,128]{1,0:T(8,128)(2,1)S(1)}, bf16[80,128]{1,0:T(8,128)(2,1)S(1)}, u32[]{:S(2)}, u32[]{:S(2)}) collective-permute-start(bf16[80,128]{1,0:T(8,128)(2,1)S(1)} %get-tuple-element.40), channel_id=1, source_target_pairs={{0,1},{1,0},{2,3},{3,2},{4,5},{5,4},{6,7},{7,6},{8,9},{9,8},{10,11... | collective-permute-start | bytes 61448 | tf_op jit(solution)/shard_map/ppermute | solution.py:681
  2.3 8.1 %collective-permute-start.1 = (bf16[80,128]{1,0:T(8,128)(2,1)S(1)}, bf16[80,128]{1,0:T(8,128)(2,1)S(1)}, u32[]{:S(2)}, u32[]{:S(2)}) collective-permute-start(bf16[80,128]{1,0:T(8,128)(2,1)S(1)} %get-tuple-element.41), channel_id=1, source_target_pairs={{1,2},{2,1},{3,4},{4,3},{5,6},{6,5},{9,10},{10,9},{11,12},{12,11},... | collective-permute-start | bytes 61448 | tf_op jit(solution)/shard_map/ppermute | solution.py:680
  11.5 5.5 %copy-start = (bf16[4,3,3,64,64]{4,3,2,1,0:T(8,128)(2,1)S(1)}, bf16[4,3,3,64,64]{4,3,2,1,0:T(8,128)(2,1)}, u32[]{:S(2)}) copy-start(bf16[4,3,3,64,64]{4,3,2,1,0:T(8,128)(2,1)} %param.16) | copy-start | bytes 884740
  14.0 3.6 %collective-permute-start.2 = (bf16[576,128]{1,0:T(8,128)(2,1)S(1)}, bf16[576,128]{1,0:T(8,128)(2,1)S(1)}, u32[]{:S(2)}, u32[]{:S(2)}) collective-permute-start(bf16[576,128]{1,0:T(8,128)(2,1)S(1)} %get-tuple-element.54), channel_id=1, source_target_pairs={{0,8},{8,0},{16,24},{24,16},{1,9},{9,1},{17,25},{25,17},{2,10},{10... | collective-permute-start | bytes 442376 | tf_op jit(solution)/shard_map/ppermute | solution.py:742
  15.3 5.3 %collective-permute-start.3 = (bf16[576,128]{1,0:T(8,128)(2,1)S(1)}, bf16[576,128]{1,0:T(8,128)(2,1)S(1)}, u32[]{:S(2)}, u32[]{:S(2)}) collective-permute-start(bf16[576,128]{1,0:T(8,128)(2,1)S(1)} %get-tuple-element.55), channel_id=1, source_target_pairs={{0,16},{8,24},{16,0},{24,8},{1,17},{9,25},{17,1},{25,9},{2,18},{10... | collective-permute-start | bytes 442376 | tf_op jit(solution)/shard_map/ppermute | solution.py:721
  16.5 7.5 %collective-permute-start.4 = (bf16[576,128]{1,0:T(8,128)(2,1)S(1)}, bf16[576,128]{1,0:T(8,128)(2,1)S(1)}, u32[]{:S(2)}, u32[]{:S(2)}) collective-permute-start(bf16[576,128]{1,0:T(8,128)(2,1)S(1)} %get-tuple-element.56), channel_id=1, source_target_pairs={{0,24},{8,16},{16,8},{24,0},{1,25},{9,17},{17,9},{25,1},{2,26},{10... | collective-permute-start | bytes 442376 | tf_op jit(solution)/shard_map/ppermute | solution.py:721

commit v5 on v4

--- a/solution.py
+++ b/solution.py
@@ -101,10 +101,10 @@
 def edges_kernel(
     cfg, order_hbm, seam_hbm, own_hbm, *rest
 ):
-    n = (len(rest) - 8) // 2
+    n = (len(rest) - 9) // 2
     sources, targets = rest[:n], rest[n + 1 : 2 * n + 1]
     own_ref = rest[n]
-    meta_ref, near_ref, far_ref, left, right, order_ref, seam_ref, sems = rest[2 * n + 1 :]
+    meta_ref, near_ref, far_ref, spread, left, right, order_ref, seam_ref, sems = rest[2 * n + 1 :]
     cols, rows_all = cfg["cols"], cfg["rows_all"]
     blocks = own_ref.shape[0]
     small = [
@@ -123,6 +123,10 @@
         copy.start()
     nb = cfg["nb"]
     lane = lax.broadcasted_iota(jnp.int32, (16, LANES), 1)
+    spread[...] = one_hot(
+        spread.shape,
+        lambda r, c: (r & (LANES - 1)) == c // (LANES // blocks) * cfg["repeat"],
+    )
     for copy in small:
         copy.wait()
     meta = jnp.where(lane == nb, seam_ref[0], 0)
@@ -147,7 +151,7 @@
         copy.wait()
 
 
-def field_chunks(cfg, own_ref, nets, col_own, dep_own, pieces):
+def field_chunks(cfg, own_ref, nets, col_own, dep_own, pieces, extra=None):
     pad = EDGE * cfg["cols"]
     blocks = own_ref.shape[0]
 
@@ -172,7 +176,9 @@
         if waiting is not None:
             finish(*waiting)
         waiting = (chunk, heads)
+    made = None if extra is None else field_heads(extra, *nets, cfg["samples"], cfg["enc"])
     finish(*waiting)
+    return made
 
 
 def grouped(items, n):
@@ -196,7 +202,7 @@
 
 
 def field_kernel(
-    cfg, own_ref, win_ref, wmid_ref, wf_ref, wd_ref, col_own, dep_own, tiled, whead, spread
+    cfg, own_ref, win_ref, wmid_ref, wf_ref, wd_ref, spread, col_own, dep_own, tiled, whead
 ):
     samples, enc = cfg["samples"], cfg["enc"]
     blocks = own_ref.shape[0]
@@ -224,11 +230,8 @@
         for s in range(samples):
             whead[b, s, :, :LANES] = features
             whead[b, s, :, LANES:] = jnp.where(group == s * blocks + b, column, 0.0).astype(BF16)
-    spread[...] = one_hot(
-        spread.shape, lambda r, c: (r & (LANES - 1)) == c // (LANES // blocks) * repeat
-    )
     nets = (tiled, wmid_ref, whead, spread)
-    pieces = row_pieces(cfg, lax.axis_index("block"), False)
+    pieces = row_pieces(cfg, lax.axis_index("block"), False)[:-1]
     field_chunks(cfg, own_ref, nets, col_own, dep_own, grouped(pieces, cfg["chunk"]))
 
 
@@ -253,11 +256,13 @@
 
 
 def halo_kernel(
-    cfg, near_ref, far_ref, tiled, wmid_ref, whead, spread, col_own, dep_own, *rest
+    cfg, near_ref, far_ref, own_ref, tiled, wmid_ref, whead, spread, col_in, dep_in, *rest
 ):
     outs = rest[: cfg["groups"] - 2]
-    col_halo, dep_halo, meta, halo_ref = rest[cfg["groups"] - 2 :]
-    samples, enc, rows_all = cfg["samples"], cfg["enc"], cfg["rows_all"]
+    col_halo, dep_halo, meta, col_own, dep_own, halo_ref = rest[cfg["groups"] - 2 :]
+    col_own[...] = col_in[...]
+    dep_own[...] = dep_in[...]
+    rows_all = cfg["rows_all"]
     blocks = halo_ref.shape[0]
     odd = (lax.axis_index("patch") & 1) == 1
     near, far = near_ref[...].astype(F32), far_ref[...].astype(F32)
@@ -271,7 +276,9 @@
     for i, side in enumerate(sides):
         meta[8 * i : 8 * i + 8, :] = side[blocks * side_rays : blocks * side_rays + 8]
     xs = [halo_ref[b].astype(BF16) for b in range(blocks)]
-    heads = field_heads(xs, tiled, wmid_ref, whead, spread, samples, enc)
+    nets = (tiled, wmid_ref, whead, spread)
+    pieces = row_pieces(cfg, lax.axis_index("block"), False)[-1:]
+    heads = field_chunks(cfg, own_ref, nets, col_own, dep_own, [pieces], xs)
     colour, depth = field_mix(heads, spread)
     col_halo[...] = colour
     dep_halo[...] = jnp.zeros(dep_halo.shape, F32)
@@ -323,7 +330,7 @@
     pack(cfg, lax.axis_index("block"), 1, out_mate, col_own, dep_own, col_halo, dep_halo)
 
 
-def decoder_kernel(cfg, earlier_ref, flags_ref, w0_ref, w1_ref, w2_ref, w3_ref, *rest):
+def decoder_kernel(cfg, earlier_ref, flags_ref, mask_ref, pick_ref, w0_ref, w1_ref, w2_ref, w3_ref, *rest):
     groups, nb = cfg["groups"], cfg["nb"]
     bufs = rest[:groups]
     out_ref = rest[groups]
@@ -337,9 +344,6 @@
     per_dev = nb // groups
     place = lax.axis_index("block")
     left_open, right_open = flags_ref[0:1, :], flags_ref[8:9, :]
-    top_open = jnp.where(place > 0, 1.0, 0.0)
-    bottom_open = jnp.where(place < groups - 1, 1.0, 0.0)
-
     sides = earlier_ref.shape[0] // 3
     stacked = 2 * per_dev * groups
     earlier = [earlier_ref[i * sides : i * sides + nb, :stacked] for i in range(3)]
@@ -362,18 +366,20 @@
         from_left = jnp.exp(-dot(earlier[1], stack)) * left_open
         from_right = jnp.exp(-dot(earlier[2], stack)) * right_open
         factors.append(jnp.where(on_left, from_left, from_right))
-    used = len(factors) * nb
-    factors.append(jnp.zeros((LANES - used, LANES), F32))
+    steps = len(factors)
+    factors.append(jnp.zeros((LANES - steps * nb, LANES), F32))
     turned = jnp.concatenate(factors, axis=0).T
-    high, low = split16(turned)
-    high, low = high.astype(BF16), low.astype(BF16)
+    lhs = []
+    for k in range(steps):
+        high, low = split16(pltpu.roll(turned, (LANES - k * nb) % LANES, 1) if k else turned)
+        lhs.append(jnp.concatenate([high.astype(BF16), low.astype(BF16)], axis=1))
+    lane = lax.broadcasted_iota(jnp.int32, (2 * LANES, groups * LANES), 1)
+    block = ((lane // LANES) ^ place) * per_dev + (lane & (LANES - 1)) // half
+    sub = lax.broadcasted_iota(jnp.int32, (2 * LANES, groups * LANES), 0) & (LANES - 1)
+    wide = dot(jnp.concatenate(lhs, axis=0), jnp.where(sub == block, 1.0, 0.0).astype(BF16))
 
     def spread(k):
-        r = lax.broadcasted_iota(jnp.int32, (LANES, groups * LANES), 0)
-        c = lax.broadcasted_iota(jnp.int32, (LANES, groups * LANES), 1)
-        block = ((c // LANES) ^ place) * per_dev + (c & (LANES - 1)) // half
-        pick = jnp.where(r - k * nb == block, 1.0, 0.0).astype(BF16)
-        return dot(high, pick) + dot(low, pick)
+        return wide[k * LANES : (k + 1) * LANES]
 
     def mix(weights, lo, n):
         acc = None
@@ -406,14 +412,7 @@
     x0[:, 0:LANES] = here.astype(BF16)
     x0[:, LANES : 2 * LANES] = comp[base + 1 : base + 1 + n_in, :].astype(BF16)
 
-    q = lax.broadcasted_iota(jnp.int32, (mid, 2 * LANES), 0)
-    pos = q
-    for r in range(1, rows_mid):
-        pos = pos - jnp.where(q >= r * pitch, pitch, 0)
-    left_open = jnp.concatenate([left_open, left_open], axis=1)
-    right_open = jnp.concatenate([right_open, right_open], axis=1)
-    mask = jnp.where(pos < LEAD, left_open, jnp.where(pos >= LEAD + cols, right_open, 1.0))
-    mask = mask * jnp.where(q < pitch, top_open, jnp.where(q >= mid - pitch, bottom_open, 1.0))
+    mask = mask_ref[...]
 
     def convolve(ref, pieces, n, weights):
         made = []
@@ -431,47 +430,47 @@
 
     sa[0:8, :] = jnp.zeros((8, wide), F32)
     sa[8 + mid :, :] = jnp.zeros((8, wide), F32)
-    three = 3 * LANES
-    xa[0:pitch, :] = jnp.zeros((pitch, 2 * three), BF16)
-    xa[pitch + mid :, :] = jnp.zeros((pitch, 2 * three), BF16)
+    xa[0:pitch, :] = jnp.zeros((pitch, 2 * wide), BF16)
+    xa[pitch + mid :, :] = jnp.zeros((pitch, 2 * wide), BF16)
+    low = lax.broadcasted_iota(jnp.int32, (mid, LANES), 1) < half
+
+    def beside(after, before):
+        return jnp.where(low, after, before).astype(BF16)
 
     def lay_out(value):
         sa[8 : 8 + mid, :] = value
         for pr in range(2):
-            for d in range(3):
-                c = pr * three + d * LANES
-                xa[pitch : pitch + mid, c : c + LANES] = sa[
-                    7 + d : 7 + d + mid, pr * LANES : (pr + 1) * LANES
-                ].astype(BF16)
+            own = slice(pr * LANES, (pr + 1) * LANES)
+            xa[pitch : pitch + mid, pr * wide : pr * wide + LANES] = value[:, own].astype(BF16)
+            xa[pitch : pitch + mid, pr * wide + LANES : (pr + 1) * wide] = beside(
+                sa[9 : 9 + mid, own], sa[7 : 7 + mid, own]
+            )
 
     lay_out(value)
     value = convolve(
-        xa, [(0, three, 2 * three), (1, 0, 2 * three), (2, 0, three)], mid, w1_ref[...]
+        xa, [(0, wide, 2 * wide), (1, 0, 2 * wide), (2, 0, wide)], mid, w1_ref[...]
     )
     value = jnp.maximum(value, 0.0) * mask
     lay_out(value)
+    three = 3 * LANES
     for pr in range(2):
+        pieces = [(0, wide, 2 * wide), (1, 0, 2 * wide)] if pr == 0 else [(1, 0, 2 * wide), (2, 0, wide)]
+        both = convolve(xa, pieces, mid, w2_ref[...])
         for pc in range(2):
-            where = [(0, 1), (1, 0), (1, 1)] if pr == 0 else [(1, 0), (1, 1), (2, 0)]
-            at = [p * three + pc * LANES for _, p in where]
-            value = convolve(
-                xa, [(d, c, c + wide) for (d, _), c in zip(where, at)], mid, w2_ref[pc]
+            value = jnp.maximum(both[:, pc * wide : (pc + 1) * wide], 0.0) * mask
+            sc[2 * pr + pc, 8 : 8 + mid, :] = value
+            for rr in range(2):
+                at = (2 * pr + rr) * three + pc * LANES
+                xc[:, at : at + LANES] = value[:, rr * LANES : (rr + 1) * LANES].astype(BF16)
+        for rr in range(2):
+            own = slice(rr * LANES, (rr + 1) * LANES)
+            at = (2 * pr + rr) * three + 2 * LANES
+            xc[:, at : at + LANES] = beside(
+                sc[2 * pr, 9 : 9 + mid, own], sc[2 * pr + 1, 7 : 7 + mid, own]
             )
-            value = jnp.maximum(value, 0.0) * mask
-            own = sc.at[2 * pr + pc]
-            own[8 : 8 + mid, :] = value
-            for rr in range(2):
-                at = (2 * pr + rr) * 4 * LANES
-                tile = value[:, rr * LANES : (rr + 1) * LANES]
-                xc[:, at + (1 + pc) * LANES : at + (2 + pc) * LANES] = tile.astype(BF16)
-                slot, move = (3, 9) if pc == 0 else (0, 7)
-                xc[:, at + slot * LANES : at + (slot + 1) * LANES] = own[
-                    move : move + mid, rr * LANES : (rr + 1) * LANES
-                ].astype(BF16)
     n_out = rows_dev * pitch
-    four = 4 * LANES
     final = convolve(
-        xc, [(0, 3 * four, 4 * four), (1, 0, 4 * four), (2, 0, four)], n_out, w3_ref[...]
+        xc, [(0, 3 * three, 4 * three), (1, 0, 4 * three), (2, 0, three)], n_out, w3_ref[...]
     )
     final = final + pltpu.roll(final, half, 1)
     rays = jnp.concatenate(
@@ -487,10 +486,7 @@
         ],
         axis=0,
     )
-    r = lax.broadcasted_iota(jnp.int32, (4 * cols, 4 * cols), 0)
-    c = lax.broadcasted_iota(jnp.int32, (4 * cols, 4 * cols), 1)
-    place_of = (c & 3) * cols + (c >> 2)
-    pick = jnp.where(r == place_of, 1.0, 0.0).astype(BF16)
+    pick = pick_ref[...]
     high, low = split16(stack)
     image = dot(high.astype(BF16), pick) + dot(low.astype(BF16), pick)
     colours = out_ref.shape[0]
@@ -505,7 +501,9 @@
     return [a for a in range(3) if (p + a - 1) // 2 + 1 == d]
 
 
-def weights_kernel(conv_ref, colour_ref, after_ref, w0_ref, w1_ref, w2_ref, w3_ref):
+def weights_kernel(
+    cfg, conv_ref, colour_ref, flags_ref, w0_ref, w1_ref, w2_ref, w3_ref, mask_ref, pick_ref
+):
     feat = conv_ref.shape[1]
     r = lax.broadcasted_iota(jnp.int32, (feat, LANES), 0)
     lane = lax.broadcasted_iota(jnp.int32, (feat, LANES), 1)
@@ -543,12 +541,16 @@
                 n = 2 * p + q
                 for d in range(3):
                     row = [sums[p, q, d, f] for f in range(3)]
-                    layouts = [[None] + row, row + [None]]
-                    refs = [w2_ref.at[0], w2_ref.at[1]] if k == 2 else [None, w0_ref]
-                    for ref, blocks in zip(refs, layouts):
-                        if ref is not None:
-                            put(ref, n, 2 * d, pair(blocks[0], blocks[1]))
-                            put(ref, n, 2 * d + 1, pair(blocks[2], blocks[3]))
+                    if k == 0:
+                        makes = [(w0_ref, n, row + [None])]
+                    else:
+                        makes = [
+                            (w2_ref, n, [row[1], row[2], None, row[0]]),
+                            (w2_ref, 4 + n, row + [None]),
+                        ]
+                    for ref, at, blocks in makes:
+                        put(ref, at, 2 * d, pair(blocks[0], blocks[1]))
+                        put(ref, at, 2 * d + 1, pair(blocks[2], blocks[3]))
 
     def pick(table, a, e):
         return table(a, e) if 0 <= a < 3 and 0 <= e < 3 else None
@@ -556,12 +558,11 @@
     for p in range(2):
         for q in range(2):
             for row in range(4):
-                for j in range(3):
+                for j, at in enumerate([(2, 3), (4, 1)]):
                     blocks = [
-                        pick(lambda a, e: tap(1, a, e), row - p, c - 1 - q)
-                        for c in (2 * j, 2 * j + 1)
+                        pick(lambda a, e: tap(1, a, e), row - p, c - 1 - q) for c in at
                     ]
-                    put(w1_ref, 2 * p + q, row * 3 + j, pair(*blocks))
+                    put(w1_ref, 2 * p + q, row * 2 + j, pair(*blocks))
 
     colours = colour_ref.shape[0]
     given = colour_ref[...].astype(F32)
@@ -583,15 +584,15 @@
         return jnp.where(mask, blank if x is None else x, blank if y is None else y)
 
     for row in range(6):
-        for j in range(4):
+        for j, (c_left, c_right) in enumerate([(2, 3), (4, 5), (6, 1)]):
             pieces = []
             for v in range(4):
                 for u in (0, 2):
                     halves = [
                         choose(
                             lane,
-                            pick(lambda a, e: mixed[a, e], row - w, 2 * j - 1 - v),
-                            pick(lambda a, e: mixed[a, e], row - w, 2 * j - v),
+                            pick(lambda a, e: mixed[a, e], row - w, c_left - 1 - v),
+                            pick(lambda a, e: mixed[a, e], row - w, c_right - 1 - v),
                         )
                         for w in (u, u + 1)
                     ]
@@ -599,8 +600,28 @@
                     pieces.append(blank if made is None else made)
             tile = jnp.concatenate(pieces, axis=0)
             high, low16 = split16(tile)
-            at = (row * 4 + j) * LANES
+            at = (row * 3 + j) * LANES
             w3_ref[:, at : at + LANES] = jnp.concatenate([high, low16], axis=0).astype(BF16)
+
+    cols, pitch, rows_mid = cfg["cols"], cfg["pitch"], cfg["rows_dev"] + 2
+    place, mid = lax.axis_index("block"), rows_mid * pitch
+    left_open, right_open = flags_ref[0:1, :], flags_ref[8:9, :]
+    top_open = jnp.where(place > 0, 1.0, 0.0)
+    bottom_open = jnp.where(place < cfg["groups"] - 1, 1.0, 0.0)
+    q = lax.broadcasted_iota(jnp.int32, (mid, 2 * LANES), 0)
+    pos = q
+    for r in range(1, rows_mid):
+        pos = pos - jnp.where(q >= r * pitch, pitch, 0)
+    left_open = jnp.concatenate([left_open, left_open], axis=1)
+    right_open = jnp.concatenate([right_open, right_open], axis=1)
+    mask = jnp.where(pos < LEAD, left_open, jnp.where(pos >= LEAD + cols, right_open, 1.0))
+    mask = mask * jnp.where(q < pitch, top_open, jnp.where(q >= mid - pitch, bottom_open, 1.0))
+    mask_ref[...] = mask
+    r = lax.broadcasted_iota(jnp.int32, (4 * cols, 4 * cols), 0)
+    c = lax.broadcasted_iota(jnp.int32, (4 * cols, 4 * cols), 1)
+    place_of = (c & 3) * cols + (c >> 2)
+    pick = jnp.where(r == place_of, 1.0, 0.0).astype(BF16)
+    pick_ref[...] = pick
 
 
 def body(samples_in, block_order, seam_link, w_in, w_mid, w_feat, w_density, w_conv, w_color):
@@ -647,7 +668,7 @@
 
     edges = blk_dev * rows_all * EDGE
     early = [w_in, w_mid, w_density, w_color]
-    own, win, wmid, dens, colour, meta_own, near, far = pl.pallas_call(
+    own, win, wmid, dens, colour, meta_own, near, far, spread = pl.pallas_call(
         functools.partial(edges_kernel, cfg),
         out_shape=[pltpu.VMEM((blk_dev, count, width), BF16)]
         + [pltpu.VMEM(x.shape, BF16) for x in early]
@@ -655,9 +676,10 @@
             pltpu.VMEM((16, width), BF16),
             pltpu.VMEM((edges + 16, width), BF16),
             pltpu.VMEM((edges + 16, width), BF16),
+            pltpu.VMEM((2 * LANES, samples * LANES), BF16),
         ],
         in_specs=[hbm] * (3 + len(early)),
-        out_specs=[vmem] * (4 + len(early)),
+        out_specs=[vmem] * (5 + len(early)),
         scratch_shapes=[
             pltpu.VMEM((edges, width), F32),
             pltpu.VMEM((edges, width), F32),
@@ -682,40 +704,41 @@
 
     rays_flops = 2 * 2 * blk_dev * samples * w_mid.shape[2] * (3 * w_mid.shape[2])
     far_rays = (rows_all - cfg["n_near"]) * cols
-    col_own, dep_own, tiled, whead, spread = pl.pallas_call(
+    col_own, dep_own, tiled, whead = pl.pallas_call(
         functools.partial(field_kernel, cfg),
         out_shape=[
             pltpu.VMEM((count + 2 * EDGE * cols, LANES), BF16),
             pltpu.VMEM((8 * (count + 2 * EDGE * cols) // LANES, LANES), F32),
             pltpu.VMEM((blk_dev, width, w_in.shape[2]), BF16),
             pltpu.VMEM((blk_dev, samples, w_feat.shape[1], 2 * LANES), BF16),
-            pltpu.VMEM((2 * LANES, samples * LANES), BF16),
         ],
-        in_specs=[vmem] * 5,
-        out_specs=[vmem] * 5,
+        in_specs=[vmem] * 6,
+        out_specs=[vmem] * 4,
         compiler_params=params,
         cost_estimate=pl.CostEstimate(
             flops=far_rays * rays_flops, bytes_accessed=10**6, transcendentals=0
         ),
         name="field",
-    )(own, win, wmid, w_feat, dens)
+    )(own, win, wmid, w_feat, dens, spread)
 
     size = n_own + n_halo + n_dep + n_tail
     shape = pltpu.VMEM((size, LANES), BF16)
-    *bufs, col_halo, dep_halo, meta = pl.pallas_call(
+    *bufs, col_halo, dep_halo, meta, col_own, dep_own = pl.pallas_call(
         functools.partial(halo_kernel, cfg),
         out_shape=[shape] * (groups - 2)
         + [
             pltpu.VMEM((hrays, LANES), F32),
             pltpu.VMEM((n_tail, LANES), F32),
             pltpu.VMEM((16, LANES), F32),
+            pltpu.VMEM(col_own.shape, BF16),
+            pltpu.VMEM(dep_own.shape, F32),
         ],
-        in_specs=[vmem] * 8,
-        out_specs=[vmem] * (groups + 1),
+        in_specs=[vmem] * 9,
+        out_specs=[vmem] * (groups + 3),
         scratch_shapes=[pltpu.VMEM((blk_dev, hrays, width), F32)],
         compiler_params=params,
         name="halo",
-    )(near, far, tiled, wmid, whead, spread, col_own, dep_own)
+    )(near, far, own, tiled, wmid, whead, spread, col_own, dep_own)
     got = []
     for s in range(2, groups):
         got.append(lax.ppermute(bufs[s - 2], "block", [(i, i ^ s) for i in range(groups)]))
@@ -741,39 +764,41 @@
     )
     got = [mine, lax.ppermute(mate, "block", [(i, i ^ 1) for i in range(groups)])] + got
 
-    w0, w1, w2, w3 = pl.pallas_call(
-        weights_kernel,
+    pitch = cfg["pitch"]
+    rows_in, rows_mid = rows_dev + 2 * EDGE, rows_dev + 2
+    w0, w1, w2, w3, mask, pick = pl.pallas_call(
+        functools.partial(weights_kernel, cfg),
         out_shape=[
             pltpu.VMEM((4 * feat, 12 * feat), BF16),
-            pltpu.VMEM((4 * feat, 24 * feat), BF16),
-            pltpu.VMEM((2, 4 * feat, 12 * feat), BF16),
-            pltpu.VMEM((2 * feat, 48 * feat), BF16),
+            pltpu.VMEM((4 * feat, 16 * feat), BF16),
+            pltpu.VMEM((8 * feat, 12 * feat), BF16),
+            pltpu.VMEM((2 * feat, 36 * feat), BF16),
+            pltpu.VMEM((rows_mid * pitch, 2 * LANES), F32),
+            pltpu.VMEM((4 * cols, 4 * cols), BF16),
         ],
-        in_specs=[vmem, vmem, pl.BlockSpec(memory_space=pl.ANY)],
-        out_specs=[vmem] * 4,
+        in_specs=[vmem] * 3,
+        out_specs=[vmem] * 6,
         compiler_params=params,
         cost_estimate=pl.CostEstimate(flops=10**8, bytes_accessed=10**6, transcendentals=0),
         name="weights",
-    )(w_conv.reshape(-1, feat), colour, mine)
-    pitch = cfg["pitch"]
-    rows_in, rows_mid = rows_dev + 2 * EDGE, rows_dev + 2
+    )(w_conv.reshape(-1, feat), colour, flags)
     return pl.pallas_call(
         functools.partial(decoder_kernel, cfg),
         out_shape=jax.ShapeDtypeStruct((w_color.shape[0], 4 * rows_dev, 4 * cols), F32),
-        in_specs=[vmem] * (6 + groups),
+        in_specs=[vmem] * (8 + groups),
         out_specs=vmem,
         scratch_shapes=[
             pltpu.VMEM(((rows_in + 2) * pitch, LANES), F32),
             pltpu.VMEM((rows_in * pitch, 2 * LANES), BF16),
             pltpu.VMEM((rows_mid * pitch + 16, 2 * LANES), F32),
-            pltpu.VMEM(((rows_mid + 2) * pitch, 6 * LANES), BF16),
+            pltpu.VMEM(((rows_mid + 2) * pitch, 4 * LANES), BF16),
             pltpu.VMEM((4, rows_mid * pitch + 16, 2 * LANES), F32),
-            pltpu.VMEM((rows_mid * pitch, 16 * LANES), BF16),
+            pltpu.VMEM((rows_mid * pitch, 12 * LANES), BF16),
             pltpu.VMEM((hchunks * LANES, groups * LANES), F32),
         ],
         compiler_params=params,
         name="decoder",
-    )(earlier, flags, w0, w1, w2, w3, *got)
+    )(earlier, flags, mask, pick, w0, w1, w2, w3, *got)
 
 
 def solution(mesh):

time: 28.6 us -> 27.9 us (0.976)
  the two profiles are of different devices: /device:TPU:19 before, /device:TPU:17 now
where the time goes in v5:
time: 27.9 us; the launch traced here: 27.7 us
  Pallas kernels  13 us (47%)
  starting transfers between devices  7.19 us (26%)
  waiting for transfers between devices  6.65 us (24%)
  between operations  0.74 us (3%)
    ppermute x2, waiting for transfers between devices, body(): lax.ppermute(bufs[s - 2], 'block', [(i, i ^ s) for i in range(groups)])  6.41 us
    pallas_call x1, Pallas kernels, body(): pl.pallas_call(functools.partial(decoder_kernel, cfg), out_shape=jax.Shap...  3.87 us
    pallas_call x1, Pallas kernels, body(): pl.pallas_call(functools.partial(field_kernel, cfg), out_shape=[pltpu.VME...  2.98 us
    pallas_call x1, Pallas kernels, body(): near_rows(own, tiled, wmid, whead, spread, col_own, dep_own, col_halo, de...  2.39 us
    ppermute x1, starting transfers between devices, body(): lax.ppermute(mate, 'block', [(i, i ^ 1) for i in range(groups)])  2.17 us
    ppermute x1, starting transfers between devices, body(): far = lax.ppermute(far, 'patch', swap_far)  2.04 us
    pallas_call x1, Pallas kernels, body(): pl.pallas_call(functools.partial(halo_kernel, cfg), out_shape=[shape] * (...  1.88 us
    ppermute x2, starting transfers between devices, body(): lax.ppermute(bufs[s - 2], 'block', [(i, i ^ s) for i in range(groups)])  1.71 us
  transfers between devices with their start and end apart: 5, of which 3 were waited for; matrix products, arithmetic and copies ran while one was open for 0% of the time, Pallas kernels for 13%

profile of v5, /device:TPU:17, one launch (start us, length us, event | category | flops | bytes accessed | tf_op | source)
XLA Modules:
  0.0 27.7 jit_solution(3163401267904894841)
XLA Ops:
  0.7 0.0 copy-start.1
  0.7 1.3 %edges.1 = (bf16[2,1024,128]{2,1,0:T(8,128)(2,1)S(1)}, bf16[2,32,256]{2,1,0:T(8,128)(2,1)S(1)}, bf16[2,2,256,256]{3,2,1,0:T(8,128)(2,1)S(1)}, bf16[2,256]{1,0:T(...) custom-call(s32[1,8]{1,0:T(1,128)} %order_hbm.1, ...), custom_call_target="tpu_custom_call" | custom-call | tf_op jit(solution)/shard_map/edges/pallas_call | solution.py:671
  2.0 1.3 %collective-permute-start = (bf16[80,128]{1,0:T(8,128)(2,1)S(1)}, bf16[80,128]{1,0:T(8,128)(2,1)S(1)}, u32[]{:S(2)}, u32[]{:S(2)}) collective-permute-start(bf16[80,128]{1,0:T(8,128)(2,1)S(1)} %get-tuple-element.42), channel_id=1, source_target_pairs={{0,1},{1,0},{2,3},{3,2},{4,5},{5,4},{6,7},{7,6},{8,9},{9,8},{10,11... | collective-permute-start | bytes 61448 | tf_op jit(solution)/shard_map/ppermute | solution.py:703
  3.3 2.0 %collective-permute-start.1 = (bf16[80,128]{1,0:T(8,128)(2,1)S(1)}, bf16[80,128]{1,0:T(8,128)(2,1)S(1)}, u32[]{:S(2)}, u32[]{:S(2)}) collective-permute-start(bf16[80,128]{1,0:T(8,128)(2,1)S(1)} %get-tuple-element.43), channel_id=1, source_target_pairs={{1,2},{2,1},{3,4},{4,3},{5,6},{6,5},{9,10},{10,9},{11,12},{12,11},... | collective-permute-start | bytes 61448 | tf_op jit(solution)/shard_map/ppermute | solution.py:702
  5.3 0.0 copy-done.1
  5.3 0.1 copy.10.wf_ref
  5.4 3.0 %field.1 = (bf16[1280,128]{1,0:T(8,128)(2,1)S(1)}, f32[80,128]{1,0:T(8,128)S(1)}, bf16[2,128,256]{2,1,0:T(8,128)(2,1)S(1)}, bf16[2,4,256,256]{3,2,1,0:T(8,128)(2,1)S(1)}) custom-call(bf16[2,1024,128]{2,1,0:T(8,128)(2,1)S(1)} %get-tuple-element.35.own_ref, bf16[2,32,256]{2,1,0:T(8,128)(2,1)S(1)} %get-tuple-element.36.win_ref, ...), custom_call_target="tpu_custom_call" | custom-call | flops 4026531840 | bytes 1000000 | tf_op jit(solution)/shard_map/field/pallas_call | solution.py:707
  8.4 0.0 collective-permute-done.near_ref
  8.4 0.2 collective-permute-done.1.far_ref
  8.7 1.9 %halo.1 = (bf16[576,128]{1,0:T(8,128)(2,1)S(1)}, bf16[576,128]{1,0:T(8,128)(2,1)S(1)}, f32[80,128]{1,0:T(8,128)S(1)}, f32[16,128]{1,0:T(8,128)S(1)}, f32[16,128]...) custom-call(bf16[80,128]{1,0:T(8,128)(2,1)S(1)} %collective-permute-done.near_ref, ...), custom_call_target="tpu_custom_call" | custom-call | tf_op jit(solution)/shard_map/halo/pallas_call | solution.py:726
  10.6 0.0 copy-start
  10.6 2.4 %near.1 = (bf16[576,128]{1,0:T(8,128)(2,1)S(1)}, bf16[576,128]{1,0:T(8,128)(2,1)S(1)}, bf16[48,128]{1,0:T(8,128)(2,1)S(1)}, f32[16,128]{1,0:T(8,128)S(1)}) custom-call(bf16[2,1024,128]{2,1,0:T(8,128)(2,1)S(1)} %get-tuple-element.35.own_ref, bf16[2,128,256]{2,1,0:T(8,128)(2,1)S(1)} %get-tuple-element.40.tiled, ...), custom_call_target="tpu_custom_call" | custom-call | flops 2415919104 | bytes 1000000 | tf_op jit(solution)/shard_map/near/pallas_call | solution.py:762
  13.0 2.2 %collective-permute-start.2 = (bf16[576,128]{1,0:T(8,128)(2,1)S(1)}, bf16[576,128]{1,0:T(8,128)(2,1)S(1)}, u32[]{:S(2)}, u32[]{:S(2)}) collective-permute-start(bf16[576,128]{1,0:T(8,128)(2,1)S(1)} %get-tuple-element.62), channel_id=1, source_target_pairs={{0,8},{8,0},{16,24},{24,16},{1,9},{9,1},{17,25},{25,17},{2,10},{10... | collective-permute-start | bytes 442376 | tf_op jit(solution)/shard_map/ppermute | solution.py:765
  15.1 1.2 %collective-permute-start.3 = (bf16[576,128]{1,0:T(8,128)(2,1)S(1)}, bf16[576,128]{1,0:T(8,128)(2,1)S(1)}, u32[]{:S(2)}, u32[]{:S(2)}) collective-permute-start(bf16[576,128]{1,0:T(8,128)(2,1)S(1)} %get-tuple-element.63), channel_id=1, source_target_pairs={{0,16},{8,24},{16,0},{24,8},{1,17},{9,25},{17,1},{25,9},{2,18},{10... | collective-permute-start | bytes 442376 | tf_op jit(solution)/shard_map/ppermute | solution.py:744
  16.4 0.5 %collective-permute-start.4 = (bf16[576,128]{1,0:T(8,128)(2,1)S(1)}, bf16[576,128]{1,0:T(8,128)(2,1)S(1)}, u32[]{:S(2)}, u32[]{:S(2)}) collective-permute-start(bf16[576,128]{1,0:T(8,128)(2,1)S(1)} %get-tuple-element.64), channel_id=1, source_target_pairs={{0,24},{8,16},{16,8},{24,0},{1,25},{9,17},{17,9},{25,1},{2,26},{10... | collective-permute-start | bytes 442376 | tf_op jit(solution)/shard_map/ppermute | solution.py:744
  16.9 0.0 copy-done
  16.9 0.6 %weights.1 = (bf16[256,768]{1,0:T(8,128)(2,1)S(1)}, bf16[256,1024]{1,0:T(8,128)(2,1)S(1)}, bf16[512,768]{1,0:T(8,128)(2,1)S(1)}, bf16[128,2304]{1,0:T(8,128)(2,1...) custom-call(bf16[2304,64]{1,0:T(8,128)(2,1)S(1)} %bitcast.2, ...), custom_call_target="tpu_custom_call" | custom-call | flops 100000000 | bytes 1000000 | tf_op jit(solution)/shard_map/weights/pallas_call | solution.py:769
  17.5 0.0 collective-permute-done.2.rest_1_
  17.5 3.0 %collective-permute-done.3.rest_2_ = bf16[576,128]{1,0:T(8,128)(2,1)S(1)} collective-permute-done((bf16[576,128]{1,0:T(8,128)(2,1)S(1)}, bf16[576,128]{1,0:T(8,128)(2,1)S(1)}, u32[]{:S(2)}, u32[]{:S(2)}) %collective-permute-start.3) | collective-permute-done | bytes 147488 | tf_op jit(solution)/shard_map/ppermute | solution.py:744
  20.5 3.4 %collective-permute-done.4.rest_3_ = bf16[576,128]{1,0:T(8,128)(2,1)S(1)} collective-permute-done((bf16[576,128]{1,0:T(8,128)(2,1)S(1)}, bf16[576,128]{1,0:T(8,128)(2,1)S(1)}, u32[]{:S(2)}, u32[]{:S(2)}) %collective-permute-start.4) | collective-permute-done | bytes 147488 | tf_op jit(solution)/shard_map/ppermute | solution.py:744
  23.9 3.9 %decoder.1 = f32[3,16,256]{2,1,0:T(8,128)} custom-call(bf16[48,128]{1,0:T(8,128)(2,1)S(1)} %get-tuple-element.52.earlier_ref, f32[16,128]{1,0:T(8,128)S(1)} %get-tuple-element.53.flags_ref, f32[480,256]{1,0:T(8,128)S(1)} %get-tuple-element.55.mask_ref, bf16[256,256]{1,0:T(8,128)(2,1)S(1)} %get-tuple-element.56.pick_ref, ...), custom_call_target="tpu_custom_call" | custom-call | tf_op jit(solution)/shard_map/decoder/pallas_call | solution.py:785
Async XLA Ops:
  0.7 4.7 %copy-start.1 = (bf16[2,256,64]{1,2,0:T(8,128)(2,1)S(1)}, bf16[2,256,64]{1,2,0:T(8,128)(2,1)}, u32[]{:S(2)}) copy-start(bf16[2,256,64]{1,2,0:T(8,128)(2,1)} %param.14) | copy-start | bytes 196612
  2.0 6.4 %collective-permute-start = (bf16[80,128]{1,0:T(8,128)(2,1)S(1)}, bf16[80,128]{1,0:T(8,128)(2,1)S(1)}, u32[]{:S(2)}, u32[]{:S(2)}) collective-permute-start(bf16[80,128]{1,0:T(8,128)(2,1)S(1)} %get-tuple-element.42), channel_id=1, source_target_pairs={{0,1},{1,0},{2,3},{3,2},{4,5},{5,4},{6,7},{7,6},{8,9},{9,8},{10,11... | collective-permute-start | bytes 61448 | tf_op jit(solution)/shard_map/ppermute | solution.py:703
  3.3 5.4 %collective-permute-start.1 = (bf16[80,128]{1,0:T(8,128)(2,1)S(1)}, bf16[80,128]{1,0:T(8,128)(2,1)S(1)}, u32[]{:S(2)}, u32[]{:S(2)}) collective-permute-start(bf16[80,128]{1,0:T(8,128)(2,1)S(1)} %get-tuple-element.43), channel_id=1, source_target_pairs={{1,2},{2,1},{3,4},{4,3},{5,6},{6,5},{9,10},{10,9},{11,12},{12,11},... | collective-permute-start | bytes 61448 | tf_op jit(solution)/shard_map/ppermute | solution.py:702
  10.6 6.3 %copy-start = (bf16[4,3,3,64,64]{4,3,2,1,0:T(8,128)(2,1)S(1)}, bf16[4,3,3,64,64]{4,3,2,1,0:T(8,128)(2,1)}, u32[]{:S(2)}) copy-start(bf16[4,3,3,64,64]{4,3,2,1,0:T(8,128)(2,1)} %param.16) | copy-start | bytes 884740
  13.0 4.5 %collective-permute-start.2 = (bf16[576,128]{1,0:T(8,128)(2,1)S(1)}, bf16[576,128]{1,0:T(8,128)(2,1)S(1)}, u32[]{:S(2)}, u32[]{:S(2)}) collective-permute-start(bf16[576,128]{1,0:T(8,128)(2,1)S(1)} %get-tuple-element.62), channel_id=1, source_target_pairs={{0,8},{8,0},{16,24},{24,16},{1,9},{9,1},{17,25},{25,17},{2,10},{10... | collective-permute-start | bytes 442376 | tf_op jit(solution)/shard_map/ppermute | solution.py:765
  15.1 5.3 %collective-permute-start.3 = (bf16[576,128]{1,0:T(8,128)(2,1)S(1)}, bf16[576,128]{1,0:T(8,128)(2,1)S(1)}, u32[]{:S(2)}, u32[]{:S(2)}) collective-permute-start(bf16[576,128]{1,0:T(8,128)(2,1)S(1)} %get-tuple-element.63), channel_id=1, source_target_pairs={{0,16},{8,24},{16,0},{24,8},{1,17},{9,25},{17,1},{25,9},{2,18},{10... | collective-permute-start | bytes 442376 | tf_op jit(solution)/shard_map/ppermute | solution.py:744
  16.4 7.5 %collective-permute-start.4 = (bf16[576,128]{1,0:T(8,128)(2,1)S(1)}, bf16[576,128]{1,0:T(8,128)(2,1)S(1)}, u32[]{:S(2)}, u32[]{:S(2)}) collective-permute-start(bf16[576,128]{1,0:T(8,128)(2,1)S(1)} %get-tuple-element.64), channel_id=1, source_target_pairs={{0,24},{8,16},{16,8},{24,0},{1,25},{9,17},{17,9},{25,1},{2,26},{10... | collective-permute-start | bytes 442376 | tf_op jit(solution)/shard_map/ppermute | solution.py:744

commit v6 on v5

--- a/solution.py
+++ b/solution.py
@@ -101,22 +101,25 @@
 def edges_kernel(
     cfg, order_hbm, seam_hbm, own_hbm, *rest
 ):
-    n = (len(rest) - 9) // 2
-    sources, targets = rest[:n], rest[n + 1 : 2 * n + 1]
-    own_ref = rest[n]
-    meta_ref, near_ref, far_ref, spread, left, right, order_ref, seam_ref, sems = rest[2 * n + 1 :]
+    n = (len(rest) - 10) // 2
+    sources, targets = rest[:n], rest[n : 2 * n]
+    meta_ref, near_ref, far_ref, spread, ends, left, right, order_ref, seam_ref, sems = rest[2 * n :]
     cols, rows_all = cfg["cols"], cfg["rows_all"]
-    blocks = own_ref.shape[0]
+    blocks = own_hbm.shape[0]
     small = [
         pltpu.make_async_copy(order_hbm, order_ref, sems.at[n + 1]),
         pltpu.make_async_copy(seam_hbm, seam_ref, sems.at[n + 2]),
     ]
     for copy in small:
         copy.start()
-    load = pltpu.make_async_copy(own_hbm, own_ref, sems.at[0])
-    load.start()
+    loads = [
+        pltpu.make_async_copy(own_hbm.at[:, :, pl.ds(at, 8), :], ends.at[i], sems.at[n + 3 + i])
+        for i, at in enumerate((0, cols - 8))
+    ]
+    for copy in loads:
+        copy.start()
     more = [
-        pltpu.make_async_copy(source, target, sems.at[1 + i])
+        pltpu.make_async_copy(source, target, sems.at[i])
         for i, (source, target) in enumerate(zip(sources, targets))
     ]
     for copy in more:
@@ -133,14 +136,14 @@
     for k in range(nb):
         meta = jnp.where(lane == k, order_ref[0, k], meta)
     meta = meta.astype(F32).astype(BF16)
-    load.wait()
+    for copy in loads:
+        copy.wait()
     size = blocks * rows_all * EDGE
     for b in range(blocks):
         for r in range(rows_all):
             q = (b * rows_all + r) * EDGE
-            left[q : q + EDGE, :] = own_ref[b, r * cols : r * cols + 16, :].astype(F32)[:EDGE]
-            last = own_ref[b, (r + 1) * cols - 16 : (r + 1) * cols, :].astype(F32)
-            right[q : q + EDGE, :] = last[16 - EDGE :]
+            left[q : q + EDGE, :] = ends[0, b, r].astype(F32)[:EDGE]
+            right[q : q + EDGE, :] = ends[1, b, r].astype(F32)[8 - EDGE :]
     meta_ref[...] = meta
     odd = (lax.axis_index("patch") & 1) == 1
     near_ref[:size, :] = jnp.where(odd, left[...], right[...]).astype(BF16)
@@ -667,11 +670,10 @@
 
 
     edges = blk_dev * rows_all * EDGE
-    early = [w_in, w_mid, w_density, w_color]
-    own, win, wmid, dens, colour, meta_own, near, far, spread = pl.pallas_call(
+    early = [w_in, w_density, w_color]
+    win, dens, colour, meta_own, near, far, spread = pl.pallas_call(
         functools.partial(edges_kernel, cfg),
-        out_shape=[pltpu.VMEM((blk_dev, count, width), BF16)]
-        + [pltpu.VMEM(x.shape, BF16) for x in early]
+        out_shape=[pltpu.VMEM(x.shape, BF16) for x in early]
         + [
             pltpu.VMEM((16, width), BF16),
             pltpu.VMEM((edges + 16, width), BF16),
@@ -679,22 +681,25 @@
             pltpu.VMEM((2 * LANES, samples * LANES), BF16),
         ],
         in_specs=[hbm] * (3 + len(early)),
-        out_specs=[vmem] * (5 + len(early)),
+        out_specs=[vmem] * (4 + len(early)),
         scratch_shapes=[
+            pltpu.VMEM((2, blk_dev, rows_all, 8, width), BF16),
             pltpu.VMEM((edges, width), F32),
             pltpu.VMEM((edges, width), F32),
             pltpu.SMEM(block_order.shape, jnp.int32),
             pltpu.SMEM(seam_link.shape, jnp.int32),
-            pltpu.SemaphoreType.DMA((3 + len(early),)),
+            pltpu.SemaphoreType.DMA((5 + len(early),)),
         ],
         compiler_params=params,
+        cost_estimate=pl.CostEstimate(flops=4 * 10**9, bytes_accessed=10**6, transcendentals=0),
         name="edges",
     )(
         far_off(block_order),
         seam_link,
-        far_off(samples_in.reshape(blk_dev, count, width)),
+        far_off(samples_in),
         *[far_off(x) for x in early],
     )
+    own, wmid = samples_in.reshape(blk_dev, count, width), w_mid
     swap_near = [(i, i ^ 1) for i in range(patches) if i ^ 1 < patches]
     swap_far = []
     for i in range(1, patches - 1, 2):

time: 27.9 us -> 27.7 us (level)
  no operation moved by 1% of the time
where the time goes in v6:
time: 27.7 us; the launch traced here: 27.5 us
  Pallas kernels  12.8 us (46%)
  starting transfers between devices  7.18 us (26%)
  waiting for transfers between devices  6.62 us (24%)
  between operations  0.77 us (3%)
    ppermute x2, waiting for transfers between devices, body(): lax.ppermute(bufs[s - 2], 'block', [(i, i ^ s) for i in range(groups)])  6.4 us
    pallas_call x1, Pallas kernels, body(): pl.pallas_call(functools.partial(decoder_kernel, cfg), out_shape=jax.Shap...  3.88 us
    pallas_call x1, Pallas kernels, body(): pl.pallas_call(functools.partial(field_kernel, cfg), out_shape=[pltpu.VME...  2.98 us
    pallas_call x1, Pallas kernels, body(): near_rows(own, tiled, wmid, whead, spread, col_own, dep_own, col_halo, de...  2.39 us
    ppermute x1, starting transfers between devices, body(): lax.ppermute(mate, 'block', [(i, i ^ 1) for i in range(groups)])  2.16 us
    ppermute x1, starting transfers between devices, body(): far = lax.ppermute(far, 'patch', swap_far)  2.04 us
    pallas_call x1, Pallas kernels, body(): pl.pallas_call(functools.partial(halo_kernel, cfg), out_shape=[shape] * (...  1.89 us
    ppermute x2, starting transfers between devices, body(): lax.ppermute(bufs[s - 2], 'block', [(i, i ^ s) for i in range(groups)])  1.71 us
  transfers between devices with their start and end apart: 5, of which 3 were waited for; matrix products, arithmetic and copies ran while one was open for 0% of the time, Pallas kernels for 13%

profile of v6, /device:TPU:17, one launch (start us, length us, event | category | flops | bytes accessed | tf_op | source)
XLA Modules:
  0.0 27.5 jit_solution(4796866418196286237)
XLA Ops:
  0.7 0.0 copy-start.3
  0.7 0.0 copy-start.1
  0.7 0.0 copy-start.2
  0.7 1.1 %edges.1 = (bf16[2,32,256]{2,1,0:T(8,128)(2,1)S(1)}, bf16[2,256]{1,0:T(2,128)(2,1)S(1)}, bf16[3,64]{1,0:T(4,128)(2,1)S(1)}, bf16[16,128]{1,0:T(8,128)(2,1)S(1)},...) custom-call(s32[1,8]{1,0:T(1,128)} %order_hbm.1, s32[1]{0:T(128)S(6)} %copy.11.seam_hbm, ...), custom_call_target="tpu_custom_call" | custom-call | flops 4000000000 | bytes 1000000 | tf_op jit(solution)/shard_map/edges/pallas_call | solution.py:674
  1.8 1.3 %collective-permute-start = (bf16[80,128]{1,0:T(8,128)(2,1)S(1)}, bf16[80,128]{1,0:T(8,128)(2,1)S(1)}, u32[]{:S(2)}, u32[]{:S(2)}) collective-permute-start(bf16[80,128]{1,0:T(8,128)(2,1)S(1)} %get-tuple-element.38), channel_id=1, source_target_pairs={{0,1},{1,0},{2,3},{3,2},{4,5},{5,4},{6,7},{7,6},{8,9},{9,8},{10,11... | collective-permute-start | bytes 61448 | tf_op jit(solution)/shard_map/ppermute | solution.py:708
  3.0 2.0 %collective-permute-start.1 = (bf16[80,128]{1,0:T(8,128)(2,1)S(1)}, bf16[80,128]{1,0:T(8,128)(2,1)S(1)}, u32[]{:S(2)}, u32[]{:S(2)}) collective-permute-start(bf16[80,128]{1,0:T(8,128)(2,1)S(1)} %get-tuple-element.39), channel_id=1, source_target_pairs={{1,2},{2,1},{3,4},{4,3},{5,6},{6,5},{9,10},{10,9},{11,12},{12,11},... | collective-permute-start | bytes 61448 | tf_op jit(solution)/shard_map/ppermute | solution.py:707
  5.1 0.0 copy-done.3
  5.1 0.1 copy.10.wf_ref
  5.2 0.0 copy-done.1
  5.2 0.0 copy-done.2
  5.2 3.0 %field.1 = (bf16[1280,128]{1,0:T(8,128)(2,1)S(1)}, f32[80,128]{1,0:T(8,128)S(1)}, bf16[2,128,256]{2,1,0:T(8,128)(2,1)S(1)}, bf16[2,4,256,256]{3,2,1,0:T(8,128)(2,1)S(1)}) custom-call(bf16[2,1024,128]{2,1,0:T(8,128)(2,1)S(1)} %bitcast.3, bf16[2,32,256]{2,1,0:T(8,128)(2,1)S(1)} %get-tuple-element.33.win_ref, bf16[2,2,256,256]{3,2,1,0:T(8,128)(2,1)S(1)} %copy-done.2, ...), custom_call_target="tpu_custom_call" | custom-call | flops 4026531840 | bytes 1000000 | tf_op jit(solution)/shard_map/field/pallas_call | solution.py:712
  8.2 0.0 collective-permute-done.near_ref
  8.2 0.2 collective-permute-done.1.far_ref
  8.5 1.9 %halo.1 = (bf16[576,128]{1,0:T(8,128)(2,1)S(1)}, bf16[576,128]{1,0:T(8,128)(2,1)S(1)}, f32[80,128]{1,0:T(8,128)S(1)}, f32[16,128]{1,0:T(8,128)S(1)}, f32[16,128]...) custom-call(bf16[80,128]{1,0:T(8,128)(2,1)S(1)} %collective-permute-done.near_ref, ...), custom_call_target="tpu_custom_call" | custom-call | tf_op jit(solution)/shard_map/halo/pallas_call | solution.py:731
  10.3 0.0 copy-start
  10.4 2.4 %near.1 = (bf16[576,128]{1,0:T(8,128)(2,1)S(1)}, bf16[576,128]{1,0:T(8,128)(2,1)S(1)}, bf16[48,128]{1,0:T(8,128)(2,1)S(1)}, f32[16,128]{1,0:T(8,128)S(1)}) custom-call(bf16[2,1024,128]{2,1,0:T(8,128)(2,1)S(1)} %bitcast.5, bf16[2,128,256]{2,1,0:T(8,128)(2,1)S(1)} %get-tuple-element.36.tiled, bf16[2,2,256,256]{3,2,1,0:T(8,128)(2,1)S(1)} %copy-done.2, ...), custom_call_target="tpu_custom_call" | custom-call | flops 2415919104 | bytes 1000000 | tf_op jit(solution)/shard_map/near/pallas_call | solution.py:767
  12.8 2.2 %collective-permute-start.2 = (bf16[576,128]{1,0:T(8,128)(2,1)S(1)}, bf16[576,128]{1,0:T(8,128)(2,1)S(1)}, u32[]{:S(2)}, u32[]{:S(2)}) collective-permute-start(bf16[576,128]{1,0:T(8,128)(2,1)S(1)} %get-tuple-element.58), channel_id=1, source_target_pairs={{0,8},{8,0},{16,24},{24,16},{1,9},{9,1},{17,25},{25,17},{2,10},{10... | collective-permute-start | bytes 442376 | tf_op jit(solution)/shard_map/ppermute | solution.py:770
  14.9 1.2 %collective-permute-start.3 = (bf16[576,128]{1,0:T(8,128)(2,1)S(1)}, bf16[576,128]{1,0:T(8,128)(2,1)S(1)}, u32[]{:S(2)}, u32[]{:S(2)}) collective-permute-start(bf16[576,128]{1,0:T(8,128)(2,1)S(1)} %get-tuple-element.59), channel_id=1, source_target_pairs={{0,16},{8,24},{16,0},{24,8},{1,17},{9,25},{17,1},{25,9},{2,18},{10... | collective-permute-start | bytes 442376 | tf_op jit(solution)/shard_map/ppermute | solution.py:749
  16.2 0.5 %collective-permute-start.4 = (bf16[576,128]{1,0:T(8,128)(2,1)S(1)}, bf16[576,128]{1,0:T(8,128)(2,1)S(1)}, u32[]{:S(2)}, u32[]{:S(2)}) collective-permute-start(bf16[576,128]{1,0:T(8,128)(2,1)S(1)} %get-tuple-element.60), channel_id=1, source_target_pairs={{0,24},{8,16},{16,8},{24,0},{1,25},{9,17},{17,9},{25,1},{2,26},{10... | collective-permute-start | bytes 442376 | tf_op jit(solution)/shard_map/ppermute | solution.py:749
  16.6 0.0 copy-done
  16.6 0.6 %weights.1 = (bf16[256,768]{1,0:T(8,128)(2,1)S(1)}, bf16[256,1024]{1,0:T(8,128)(2,1)S(1)}, bf16[512,768]{1,0:T(8,128)(2,1)S(1)}, bf16[128,2304]{1,0:T(8,128)(2,1...) custom-call(bf16[2304,64]{1,0:T(8,128)(2,1)S(1)} %bitcast.2, ...), custom_call_target="tpu_custom_call" | custom-call | flops 100000000 | bytes 1000000 | tf_op jit(solution)/shard_map/weights/pallas_call | solution.py:774
  17.2 0.0 collective-permute-done.2.rest_1_
  17.2 3.0 %collective-permute-done.3.rest_2_ = bf16[576,128]{1,0:T(8,128)(2,1)S(1)} collective-permute-done((bf16[576,128]{1,0:T(8,128)(2,1)S(1)}, bf16[576,128]{1,0:T(8,128)(2,1)S(1)}, u32[]{:S(2)}, u32[]{:S(2)}) %collective-permute-start.3) | collective-permute-done | bytes 147488 | tf_op jit(solution)/shard_map/ppermute | solution.py:749
  20.2 3.4 %collective-permute-done.4.rest_3_ = bf16[576,128]{1,0:T(8,128)(2,1)S(1)} collective-permute-done((bf16[576,128]{1,0:T(8,128)(2,1)S(1)}, bf16[576,128]{1,0:T(8,128)(2,1)S(1)}, u32[]{:S(2)}, u32[]{:S(2)}) %collective-permute-start.4) | collective-permute-done | bytes 147488 | tf_op jit(solution)/shard_map/ppermute | solution.py:749
  23.6 3.9 %decoder.1 = f32[3,16,256]{2,1,0:T(8,128)} custom-call(bf16[48,128]{1,0:T(8,128)(2,1)S(1)} %get-tuple-element.48.earlier_ref, f32[16,128]{1,0:T(8,128)S(1)} %get-tuple-element.49.flags_ref, f32[480,256]{1,0:T(8,128)S(1)} %get-tuple-element.51.mask_ref, bf16[256,256]{1,0:T(8,128)(2,1)S(1)} %get-tuple-element.52.pick_ref, ...), custom_call_target="tpu_custom_call" | custom-call | tf_op jit(solution)/shard_map/decoder/pallas_call | solution.py:790
Async XLA Ops:
  0.7 4.4 %copy-start.3 = (bf16[2,256,64]{1,2,0:T(8,128)(2,1)S(1)}, bf16[2,256,64]{1,2,0:T(8,128)(2,1)}, u32[]{:S(2)}) copy-start(bf16[2,256,64]{1,2,0:T(8,128)(2,1)} %param.14) | copy-start | bytes 196612
  0.7 4.6 %copy-start.1 = (bf16[2,16,64,128]{3,2,1,0:T(8,128)(2,1)S(1)}, bf16[2,16,64,128]{3,2,1,0:T(8,128)(2,1)}, u32[]{:S(2)}) copy-start(bf16[2,16,64,128]{3,2,1,0:T(8,128)(2,1)} %own_hbm.1) | copy-start | bytes 1572868
  0.7 4.6 %copy-start.2 = (bf16[2,2,256,256]{3,2,1,0:T(8,128)(2,1)S(1)}, bf16[2,2,256,256]{3,2,1,0:T(8,128)(2,1)}, u32[]{:S(2)}) copy-start(bf16[2,2,256,256]{3,2,1,0:T(8,128)(2,1)} %wmid_ref.5) | copy-start | bytes 1572868
  1.8 6.5 %collective-permute-start = (bf16[80,128]{1,0:T(8,128)(2,1)S(1)}, bf16[80,128]{1,0:T(8,128)(2,1)S(1)}, u32[]{:S(2)}, u32[]{:S(2)}) collective-permute-start(bf16[80,128]{1,0:T(8,128)(2,1)S(1)} %get-tuple-element.38), channel_id=1, source_target_pairs={{0,1},{1,0},{2,3},{3,2},{4,5},{5,4},{6,7},{7,6},{8,9},{9,8},{10,11... | collective-permute-start | bytes 61448 | tf_op jit(solution)/shard_map/ppermute | solution.py:708
  3.0 5.4 %collective-permute-start.1 = (bf16[80,128]{1,0:T(8,128)(2,1)S(1)}, bf16[80,128]{1,0:T(8,128)(2,1)S(1)}, u32[]{:S(2)}, u32[]{:S(2)}) collective-permute-start(bf16[80,128]{1,0:T(8,128)(2,1)S(1)} %get-tuple-element.39), channel_id=1, source_target_pairs={{1,2},{2,1},{3,4},{4,3},{5,6},{6,5},{9,10},{10,9},{11,12},{12,11},... | collective-permute-start | bytes 61448 | tf_op jit(solution)/shard_map/ppermute | solution.py:707
  10.3 6.3 %copy-start = (bf16[4,3,3,64,64]{4,3,2,1,0:T(8,128)(2,1)S(1)}, bf16[4,3,3,64,64]{4,3,2,1,0:T(8,128)(2,1)}, u32[]{:S(2)}) copy-start(bf16[4,3,3,64,64]{4,3,2,1,0:T(8,128)(2,1)} %param.16) | copy-start | bytes 884740
  12.8 4.5 %collective-permute-start.2 = (bf16[576,128]{1,0:T(8,128)(2,1)S(1)}, bf16[576,128]{1,0:T(8,128)(2,1)S(1)}, u32[]{:S(2)}, u32[]{:S(2)}) collective-permute-start(bf16[576,128]{1,0:T(8,128)(2,1)S(1)} %get-tuple-element.58), channel_id=1, source_target_pairs={{0,8},{8,0},{16,24},{24,16},{1,9},{9,1},{17,25},{25,17},{2,10},{10... | collective-permute-start | bytes 442376 | tf_op jit(solution)/shard_map/ppermute | solution.py:770
  14.9 5.3 %collective-permute-start.3 = (bf16[576,128]{1,0:T(8,128)(2,1)S(1)}, bf16[576,128]{1,0:T(8,128)(2,1)S(1)}, u32[]{:S(2)}, u32[]{:S(2)}) collective-permute-start(bf16[576,128]{1,0:T(8,128)(2,1)S(1)} %get-tuple-element.59), channel_id=1, source_target_pairs={{0,16},{8,24},{16,0},{24,8},{1,17},{9,25},{17,1},{25,9},{2,18},{10... | collective-permute-start | bytes 442376 | tf_op jit(solution)/shard_map/ppermute | solution.py:749
  16.2 7.5 %collective-permute-start.4 = (bf16[576,128]{1,0:T(8,128)(2,1)S(1)}, bf16[576,128]{1,0:T(8,128)(2,1)S(1)}, u32[]{:S(2)}, u32[]{:S(2)}) collective-permute-start(bf16[576,128]{1,0:T(8,128)(2,1)S(1)} %get-tuple-element.60), channel_id=1, source_target_pairs={{0,24},{8,16},{16,8},{24,0},{1,25},{9,17},{17,9},{25,1},{2,26},{10... | collective-permute-start | bytes 442376 | tf_op jit(solution)/shard_map/ppermute | solution.py:749
